TPU v7x, 128 devices: a whole 4x4x4 slice. The times are simulated.
128 devices in a mesh: pod: 1, dp: 16 (over z, y), tp: 8 (over x, core).
Axes of the slice: x: 4, y: 4, z: 4, core: 2. Of those that a mesh axis runs over, the one named last changes fastest.
Arguments:
- x_in: bfloat16 [128, 512, 1536], P(('pod', 'dp'))
- seg_ids: int32 [128, 512], P(('pod', 'dp'))
- gain_one: bfloat16 [1536], replicated
- gain_two: bfloat16 [1536], replicated
- w_qkv: bfloat16 [1536, 4608], P(None, 'tp')
- w_out: bfloat16 [16, 96, 1536], P('tp')
- w_up: bfloat16 [1536, 6144], P(None, 'tp')
- w_down: bfloat16 [6144, 1536], P('tp')
- grad_y: bfloat16 [128, 512, 1536], P(('pod', 'dp'))
Outputs:
- output 1: bfloat16 [128, 512, 1536], P(('pod', 'dp'))
- output 2: bfloat16 [128, 512, 1536], P(('pod', 'dp'))
- output 3: bfloat16 [1536], P('pod')
- output 4: bfloat16 [1536], P('pod')
- output 5: bfloat16 [1536, 4608], P('pod', 'tp')
- output 6: bfloat16 [16, 96, 1536], P(('pod', 'tp'))
- output 7: bfloat16 [1536, 6144], P('pod', 'tp')
- output 8: bfloat16 [6144, 1536], P(('pod', 'tp'))
All inputs are finite; a program needn't handle non-finite values.
Results may differ from a plain program's by a relative error of at most 0.02.
Values are sent between devices in bfloat16 or wider.
A program may use at most 1 GiB of HBM per device.

v0:
```python
import jax
import jax.numpy as jnp
from jax import lax
from jax.sharding import PartitionSpec as P

EPS_NORM = 1e-5
NEG_LARGE = -1e30


def gelu_tanh(values):
    return jax.nn.gelu(values, approximate=True)


def norm_forward(x_rows, gain_vec):
    x_f32 = x_rows.astype(jnp.float32)
    centered = x_f32 - jnp.mean(x_f32, axis=-1, keepdims=True)
    inv_std = lax.rsqrt(jnp.mean(centered * centered, axis=-1, keepdims=True) + EPS_NORM)
    x_hat = centered * inv_std
    return (x_hat * gain_vec.astype(jnp.float32)).astype(jnp.bfloat16), x_hat, inv_std


def norm_backward(grad_out, x_hat, inv_std, gain_vec):
    grad_f32 = grad_out.astype(jnp.float32)
    grad_gain = jnp.sum(grad_f32 * x_hat, axis=0)
    grad_hat = grad_f32 * gain_vec.astype(jnp.float32)
    mean_one = jnp.mean(grad_hat, axis=-1, keepdims=True)
    mean_two = jnp.mean(grad_hat * x_hat, axis=-1, keepdims=True)
    return inv_std * (grad_hat - mean_one - x_hat * mean_two), grad_gain


def matmul_nt(lhs, rhs):
    return lax.dot_general(lhs, rhs, (((1,), (1,)), ((), ())), preferred_element_type=jnp.float32)


def matmul_tn(lhs, rhs):
    return lax.dot_general(lhs, rhs, (((0,), (0,)), ((), ())), preferred_element_type=jnp.float32)


def attention_forward(q_blk, k_blk, v_blk, allowed, score_scale):
    scores = jnp.einsum("bqnd,bknd->bnqk", q_blk, k_blk, preferred_element_type=jnp.float32) * score_scale
    attn_probs = jax.nn.softmax(jnp.where(allowed, scores, NEG_LARGE), axis=-1)
    attn_out = jnp.einsum("bnqk,bknd->bqnd", attn_probs.astype(jnp.bfloat16), v_blk, preferred_element_type=jnp.float32)
    return attn_out.astype(jnp.bfloat16), attn_probs


def attention_backward(grad_out, q_blk, k_blk, v_blk, attn_probs, score_scale):
    grad_v = jnp.einsum("bnqk,bqnd->bknd", attn_probs.astype(jnp.bfloat16), grad_out, preferred_element_type=jnp.float32)
    grad_probs = jnp.einsum("bqnd,bknd->bnqk", grad_out, v_blk, preferred_element_type=jnp.float32)
    grad_scores = attn_probs * (grad_probs - jnp.sum(grad_probs * attn_probs, axis=-1, keepdims=True))
    grad_low = (grad_scores * score_scale).astype(jnp.bfloat16)
    grad_q = jnp.einsum("bnqk,bknd->bqnd", grad_low, k_blk, preferred_element_type=jnp.float32)
    grad_k = jnp.einsum("bnqk,bqnd->bknd", grad_low, q_blk, preferred_element_type=jnp.float32)
    return grad_q, grad_k, grad_v


def solution(mesh):
    batch_spec = P(("pod", "dp"), None, None)
    seg_spec = P(("pod", "dp"), None)

    def local_step(x_in, seg_ids, gain_one, gain_two, w_qkv, w_out, w_up, w_down, grad_y):
        batch_loc, seq_len, hidden = x_in.shape
        heads_loc = w_out.shape[0]
        head_dim = w_out.shape[1]
        score_scale = head_dim ** -0.5
        tokens = batch_loc * seq_len
        positions = jnp.arange(seq_len)
        allowed = (positions[:, None] >= positions[None, :])[None, None] & (seg_ids[:, None, :, None] == seg_ids[:, None, None, :])
        x_rows = x_in.reshape(tokens, hidden)
        normed_a, hat_a, inv_a = norm_forward(x_rows, gain_one)
        qkv_rows = jnp.dot(normed_a, w_qkv, preferred_element_type=jnp.float32).astype(jnp.bfloat16)
        qkv_rows = qkv_rows.reshape(batch_loc, seq_len, heads_loc, 3, head_dim)
        q_blk = qkv_rows[:, :, :, 0]
        k_blk = qkv_rows[:, :, :, 1]
        v_blk = qkv_rows[:, :, :, 2]
        attn_out, attn_probs = attention_forward(q_blk, k_blk, v_blk, allowed, score_scale)
        attn_rows = attn_out.reshape(tokens, heads_loc, head_dim)
        part_one = lax.dot_general(attn_rows, w_out, (((1, 2), (0, 1)), ((), ())), preferred_element_type=jnp.float32)
        sum_one = lax.psum(part_one.astype(jnp.bfloat16), "tp")
        x_one = (x_rows.astype(jnp.float32) + sum_one.astype(jnp.float32)).astype(jnp.bfloat16)
        normed_b, hat_b, inv_b = norm_forward(x_one, gain_two)
        pre_act = jnp.dot(normed_b, w_up, preferred_element_type=jnp.float32)
        act_val, gelu_pull = jax.vjp(gelu_tanh, pre_act)
        hidden_act = act_val.astype(jnp.bfloat16)
        part_two = jnp.dot(hidden_act, w_down, preferred_element_type=jnp.float32)
        sum_two = lax.psum(part_two.astype(jnp.bfloat16), "tp")
        y_rows = (x_one.astype(jnp.float32) + sum_two.astype(jnp.float32)).astype(jnp.bfloat16)

        grad_rows = grad_y.reshape(tokens, hidden)
        grad_down = matmul_tn(hidden_act, grad_rows)
        grad_hidden = matmul_nt(grad_rows, w_down).astype(jnp.bfloat16)
        grad_pre = gelu_pull(grad_hidden.astype(jnp.float32))[0].astype(jnp.bfloat16)
        grad_up = matmul_tn(normed_b, grad_pre)
        part_b = matmul_nt(grad_pre, w_up).astype(jnp.bfloat16)
        grad_norm_b = lax.psum(part_b, "tp")
        back_b, gain_grad_two = norm_backward(grad_norm_b, hat_b, inv_b, gain_two)
        grad_x_one = (grad_rows.astype(jnp.float32) + back_b).astype(jnp.bfloat16)
        grad_out_w = lax.dot_general(attn_rows, grad_x_one, (((0,), (0,)), ((), ())), preferred_element_type=jnp.float32)
        grad_attn = lax.dot_general(grad_x_one, w_out, (((1,), (2,)), ((), ())), preferred_element_type=jnp.float32).astype(jnp.bfloat16)
        grad_q, grad_k, grad_v = attention_backward(grad_attn.reshape(batch_loc, seq_len, heads_loc, head_dim), q_blk, k_blk, v_blk, attn_probs, score_scale)
        grad_qkv = jnp.stack([grad_q, grad_k, grad_v], axis=3).astype(jnp.bfloat16).reshape(tokens, 3 * heads_loc * head_dim)
        grad_wqkv = matmul_tn(normed_a, grad_qkv)
        part_a = matmul_nt(grad_qkv, w_qkv).astype(jnp.bfloat16)
        grad_norm_a = lax.psum(part_a, "tp")
        back_a, gain_grad_one = norm_backward(grad_norm_a, hat_a, inv_a, gain_one)
        grad_x = (grad_x_one.astype(jnp.float32) + back_a).astype(jnp.bfloat16)

        weight_grads = lax.psum(tuple(grad_mat.astype(jnp.bfloat16) for grad_mat in (grad_wqkv, grad_out_w, grad_up, grad_down)), "dp")
        gain_grads = lax.psum((gain_grad_one, gain_grad_two), "dp")
        return (
            y_rows.reshape(x_in.shape),
            grad_x.reshape(x_in.shape),
            gain_grads[0].astype(jnp.bfloat16),
            gain_grads[1].astype(jnp.bfloat16),
            weight_grads[0],
            weight_grads[1],
            weight_grads[2],
            weight_grads[3],
        )

    return jax.shard_map(
        local_step,
        mesh=mesh,
        in_specs=(batch_spec, seg_spec, P(None), P(None), P(None, "tp"), P("tp", None, None), P(None, "tp"), P("tp", None), batch_spec),
        out_specs=(batch_spec, batch_spec, P("pod"), P("pod"), P("pod", "tp"), P(("pod", "tp"), None, None), P("pod", "tp"), P(("pod", "tp"), None)),
        check_vma=False,
    )
```

profile of v0, /device:TPU:0, one launch (start us, length us, event | category | flops | bytes accessed | tf_op | source)
XLA Modules:
  0.0 988.7 jit_solution(4948559251610630346)
XLA Ops:
  14.5 8.0 fusion.29
  23.8 8.6 fusion.35
  32.4 7.7 convolution_convert_fusion.4
  48.5 13.9 %fusion.109 = (f32[8,2,512]{2,1,0:T(2,128)S(1)}, f32[8,2,512,512]{2,3,1,0:T(8,128)}) fusion(pred[8,512,512]{1,2,0:T(8,128)(4,1)} %compare_and_fusion, bf16[8,512,2,1,96]{1,0,4,3,2:T(8,128)(2,1)} %get-tuple-element.25, bf16[8,512,2,1,96]{1,0,4,3,2:T(8,128)(2,1)} %get-tuple-element.24), kind=kOutput, calls=%fused_computation.131 | convolution fusion | flops 822084096 | bytes 22052864 | tf_op jit(solution)/shard_map/sub | solution.py:41
  62.4 8.1 fusion.93
  71.9 6.6 bitcast_convert_fusion
  78.6 146.2 %all-reduce.8.cloned.1.call-done = bf16[4096,1536]{1,0:T(8,128)(2,1)} async-done(((bf16[4096,1536]{1,0:T(8,128)(2,1)}), bf16[4096,1536]{1,0:T(8,128)(2,1)}) %all-reduce.8.cloned.1.call-update) | async-done | bytes 12582928 | tf_op jit(solution)/shard_map/psum | solution.py:78
  224.8 14.3 %convert_reduce_fusion = (f32[4096]{0:T(1024)S(1)}, bf16[4096,1536]{1,0:T(8,128)(2,1)}) fusion(bf16[4096,1536]{1,0:T(8,128)(2,1)} %all-reduce.8.cloned.1.call-done, bf16[8,512,1536]{2,1,0:T(8,128)(2,1)} %param.9), kind=kLoop, calls=%fused_computation.4 | loop fusion | flops 37744640 | bytes 37765120 | tf_op jit(solution)/shard_map/reduce_sum | solution.py:16
  239.2 8.0 fusion.17
  247.2 8.0 fusion.12
  255.2 12.4 %fusion.110 = f32[4096,768]{1,0:T(8,128)} fusion(bf16[4096,1536]{1,0:T(8,128)(2,1)S(1)} %fusion.12, bf16[1536,768]{1,0:T(8,128)(2,1)S(1)} %copy-done), kind=kOutput, calls=%fused_computation.132 | convolution fusion | flops 9663676416 | bytes 27525120 | tf_op jit(solution)/shard_map/dot_general | solution.py:81
  267.5 24.5 %fusion.43 = bf16[4096,768]{1,0:T(8,128)(2,1)} fusion(f32[4096,768]{1,0:T(8,128)} %fusion.110, bf16[4096,1536]{1,0:T(8,128)(2,1)} %bitcast.127, bf16[768,1536]{1,0:T(8,128)(2,1)S(1)} %copy-done.26), kind=kOutput, calls=%fused_computation.64 | convolution fusion | flops 9732882432 | bytes 33816576 | tf_op jit(solution)/shard_map/dot_general | solution.py:32
  292.0 15.3 %convolution_convert_fusion = bf16[4096,1536]{1,0:T(8,128)(2,1)} fusion(bf16[4096,768]{1,0:T(8,128)(2,1)} %fusion.43, bf16[1536,768]{1,0:T(8,128)(2,1)S(1)} %copy-done), kind=kOutput, calls=%fused_computation.58 | convolution fusion | flops 9669967872 | bytes 21233664 | tf_op jit(solution)/shard_map/dot_general | solution.py:32
  309.0 17.1 %convolution_convert_fusion.1 = bf16[4096,1536]{1,0:T(8,128)(2,1)} fusion(bf16[768,1536]{1,0:T(8,128)(2,1)S(1)} %copy-done.27, f32[4096,768]{1,0:T(8,128)} %fusion.110), kind=kOutput, calls=%fused_computation.59 | convolution fusion | flops 9698279424 | bytes 27525120 | tf_op jit(solution)/shard_map/dot_general | solution.py:84
  326.1 124.9 %all-reduce.10.cloned.1.call-done = bf16[4096,1536]{1,0:T(8,128)(2,1)} async-done(((bf16[4096,1536]{1,0:T(8,128)(2,1)}), bf16[4096,1536]{1,0:T(8,128)(2,1)}) %all-reduce.10.cloned.1.call-update) | async-done | bytes 12582928 | tf_op jit(solution)/shard_map/psum | solution.py:94
  451.0 14.9 %fusion.19 = (f32[1536]{0:T(1024)}, f32[4096]{0:T(1024)S(1)}, f32[4096]{0:T(1024)S(1)}) fusion(bf16[4096,1536]{1,0:T(8,128)(2,1)} %get-tuple-element.23, bf16[4096,1536]{1,0:T(8,128)(2,1)} %all-reduce.10.cloned.1.call-done, f32[4096]{0:T(1024)S(1)} %add_rsqrt_fusion, f32[4096]{0:T(1024)S(1)} %broadcast_multiply_fusion.4, f32[1536]{0:T(1024)S(1)} %convert_element_type.153), kind=kLoop, calls=%fused_computation.26 | loop fusion | flops 62904832 | bytes 25243648 | tf_op jit(solution)/shard_map/reduce_sum | solution.py:24
  465.9 14.1 %fusion.16 = bf16[4096,1536]{1,0:T(8,128)(2,1)S(1)} fusion(bf16[4096,1536]{1,0:T(8,128)(2,1)} %get-tuple-element.23, bf16[4096,1536]{1,0:T(8,128)(2,1)S(1)} %copy-done.4, f32[4096]{0:T(1024)S(1)} %get-tuple-element.33, f32[4096]{0:T(1024)S(1)} %get-tuple-element.34, f32[1536]{0:T(1024)S(1)} %convert_element_type.153, f32[4096]{0:T(1024)S(1)} %add_rsqrt_fusion, ...), kind=kLoop, calls=%fused_computation.23 | loop fusion | flops 75497472 | bytes 50403328 | tf_op jit(solution)/shard_map/convert_element_type | solution.py:96
  484.6 9.8 fusion.82
  494.4 8.1 fusion.91
  502.5 24.5 %fusion.76 = bf16[8,512,2,1,96]{1,4,2,0,3:T(8,128)(2,1)} fusion(f32[8,2,512,512]{2,3,1,0:T(8,128)} %fusion.91, bf16[8,512,2,1,96]{1,0,4,3,2:T(8,128)(2,1)} %get-tuple-element.24, f32[8,2,512,512]{2,3,1,0:T(8,128)} %get-tuple-element.32, f32[8,2,512]{2,1,0:T(2,128)S(1)} %copy-done.31), kind=kOutput, calls=%fused_computation.98 | convolution fusion | flops 834675200 | bytes 36732928 | tf_op jit(solution)/shard_map/bnqk,bknd->bqnd/dot_general | solution.py:51
  527.1 23.9 %fusion.79 = bf16[8,512,2,1,96]{1,4,2,0,3:T(8,128)(2,1)} fusion(f32[8,2,512,512]{2,3,1,0:T(8,128)} %fusion.91, bf16[8,512,2,1,96]{1,0,4,3,2:T(8,128)(2,1)S(1)} %copy-done.11, f32[8,2,512,512]{2,3,1,0:T(8,128)} %get-tuple-element.32, f32[8,2,512]{2,1,0:T(2,128)S(1)} %copy-done.31), kind=kOutput, calls=%fused_computation.99 | convolution fusion | flops 834675200 | bytes 36732928 | tf_op jit(solution)/shard_map/bnqk,bqnd->bknd/dot_general | solution.py:52
  562.1 12.8 %convolution_convert_fusion.2 = bf16[4096,1536]{1,0:T(8,128)(2,1)} fusion(bf16[4096,576]{0,1:T(8,128)(2,1)S(1)} %bitcast.133, bf16[1536,576]{0,1:T(8,128)(2,1)S(1)} %copy-done.29), kind=kOutput, calls=%fused_computation.60 | convolution fusion | flops 7254048768 | bytes 19070976 | tf_op jit(solution)/shard_map/dot_general | solution.py:32
  575.7 12.5 %fusion.31 = bf16[8,512,1536]{2,1,0:T(8,128)(2,1)} fusion(bf16[8,512,1536]{2,1,0:T(8,128)(2,1)} %param.9, f32[1536]{0:T(1024)S(1)} %copy-done.19, f32[8,512]{1,0:T(8,128)S(1)} %copy-done.23, f32[8,512]{1,0:T(8,128)S(1)} %copy-done.21), kind=kLoop, calls=%fused_computation.43 | loop fusion | flops 31457280 | bytes 25204736 | tf_op jit(solution)/shard_map/convert_element_type | solution.py:19
  588.2 16.0 %convolution_convert_fusion.5 = bf16[1536,768]{1,0:T(8,128)(2,1)} fusion(bf16[4096,1536]{1,0:T(8,128)(2,1)} %copy-done.5, bf16[4096,768]{1,0:T(8,128)(2,1)} %fusion.43), kind=kOutput, calls=%fused_computation.94 | convolution fusion | flops 9664856064 | bytes 21233664 | tf_op jit(solution)/shard_map/dot_general | solution.py:36
  604.2 17.9 %convolution_convert_fusion.6 = bf16[768,1536]{1,0:T(8,128)(2,1)} fusion(bf16[4096,1536]{1,0:T(8,128)(2,1)} %bitcast.128, f32[4096,768]{1,0:T(8,128)} %fusion.110), kind=kOutput, calls=%fused_computation.95 | convolution fusion | flops 9693167616 | bytes 27525120 | tf_op jit(solution)/shard_map/dot_general | solution.py:36
  627.0 8.8 convolution_convert_fusion.7
  635.8 200.9 %all-reduce.14.cloned.1.call-done = (bf16[4096,1536]{1,0:T(8,128)(2,1)}, bf16[4096,1536]{1,0:T(8,128)(2,1)}) async-done(((bf16[4096,1536]{1,0:T(8,128)(2,1)}, bf16[4096,1536]{1,0:T(8,128)(2,1)}), (bf16[4096,1536]{1,0:T(8,128)(2,1)}, bf16[4096,1536]{1,0:T(8,128)(2,1)})) %all-reduce.14.cloned.1.call-update) | async-done | bytes 25165840 | tf_op jit(solution)/shard_map/psum | solution.py:85
  836.6 13.5 %fusion.25 = (f32[1536]{0:T(1024)S(1)}, f32[4096]{0:T(1024)S(1)}, f32[4096]{0:T(1024)S(1)}) fusion(bf16[4096,1536]{1,0:T(8,128)(2,1)} %get-tuple-element.21, bf16[8,512,1536]{2,1,0:T(8,128)(2,1)} %param.9, f32[4096]{0:T(1024)S(1)} %bitcast.144, f32[4096]{0:T(1024)S(1)} %bitcast.141, f32[1536]{0:T(1024)S(1)} %copy-done.19), kind=kLoop, calls=%fused_computation.32 | loop fusion | flops 62904832 | bytes 25243648 | tf_op jit(solution)/shard_map/reduce_sum | solution.py:24
  850.2 75.2 %all-reduce = (bf16[1536]{0:T(1024)(128)(2,1)}, bf16[1536]{0:T(1024)(128)(2,1)}) all-reduce(f32[1536]{0:T(1024)S(1)} %get-tuple-element.10, f32[1536]{0:T(1024)S(1)} %copy-done.24), channel_id=1, replica_groups=mesh['pod'=1,'dp'=16,'tp'=8] {'dp'}, use_global_device_ids=true, to_apply=%region_16.17 | all-reduce | flops 3072 | bytes 18432 | tf_op jit(solution)/shard_map/psum | solution.py:108
  925.4 14.7 %fusion.26 = bf16[4096,1536]{1,0:T(8,128)(2,1)} fusion(bf16[4096,1536]{1,0:T(8,128)(2,1)} %get-tuple-element.23, bf16[4096,1536]{1,0:T(8,128)(2,1)} %get-tuple-element.20), kind=kLoop, calls=%fused_computation.33 | loop fusion | flops 25165824 | bytes 37748736 | tf_op jit(solution)/shard_map/convert_element_type | solution.py:86
  942.0 18.3 %fusion.23 = bf16[4096,1536]{1,0:T(8,128)(2,1)} fusion(bf16[4096,1536]{1,0:T(8,128)(2,1)S(1)} %copy-done.3, bf16[8,512,1536]{2,1,0:T(8,128)(2,1)} %param.9, bf16[4096,1536]{1,0:T(8,128)(2,1)} %copy-done.2, f32[4096]{0:T(1024)S(1)} %broadcast_multiply_fusion, f32[4096]{0:T(1024)S(1)} %broadcast_multiply_fusion.1, f32[1536]{0:T(1024)S(1)} %copy-done.19, ...), kind=kLoop, calls=%fused_computation.30 | loop fusion | flops 75497472 | bytes 50403328 | tf_op jit(solution)/shard_map/convert_element_type | solution.py:105
  960.3 10.5 %all-reduce.12.cloned.1.call-done = (bf16[1536,576]{0,1:T(8,128)(2,1)}, bf16[2,96,1536]{2,1,0:T(8,128)(2,1)}, bf16[1536,768]{1,0:T(8,128)(2,1)}, bf16[768,1536]{1,0:T(8,128)(2,1)}) async-done(((bf16[1536,576]{0,1:T(8,128)(2,1)}, bf16[2,96,1536]{2,1,0:T(8,128)(2,1)}, bf16[1536,768]{1,0:T(8,128)(2,1)}, bf16[768,1536]{1,0:T(8,128)(2,1)}), (bf16[1536,576]{0,1:T(8,128)(2,1)}, bf16[2,96,1536]{2,1,0:T(8,128)(2,1)}, ...) | async-done | bytes 7077904 | tf_op jit(solution)/shard_map/psum | solution.py:107
  (110 shorter events, 54.2 us)
Async XLA Ops:
  7.2 248.0 %copy-start = (bf16[1536,768]{1,0:T(8,128)(2,1)S(1)}, bf16[1536,768]{1,0:T(8,128)(2,1)}, u32[]{:S(2)}) copy-start(bf16[1536,768]{1,0:T(8,128)(2,1)} %param.15) | copy-start | bytes 7077892
  7.2 217.6 %all-reduce.8.cloned.1.call-start = ((), (), s32[]{:S(2)}) async-start(), calls=%async_computation | async-start | bytes 25165824 | tf_op jit(solution)/shard_map/psum | solution.py:78
  8.1 15.0 %copy-start.18 = (f32[1536]{0:T(1024)}, f32[1536]{0:T(1024)S(1)}, u32[]{:S(2)}) copy-start(f32[1536]{0:T(1024)S(1)} %convert_element_type.143) | copy-start | bytes 18436
  14.4 17.9 %copy-start.20 = (f32[8,512]{1,0:T(8,128)}, f32[8,512]{1,0:T(8,128)S(1)}, u32[]{:S(2)}) copy-start(f32[8,512]{1,0:T(8,128)S(1)} %get-tuple-element.30) | copy-start | bytes 49156
  14.5 17.9 %copy-start.14 = (f32[1,4,8,128]{3,1,2,0:T(4,128)}, f32[1,4,8,128]{3,1,2,0:T(4,128)S(1)}, u32[]{:S(2)}) copy-start(f32[1,4,8,128]{3,1,2,0:T(4,128)S(1)} %copy.46) | copy-start | bytes 49156
  23.7 8.6 copy-start.28
  40.1 5.5 copy-start.22
  62.3 8.1 copy-start.30
  62.4 9.5 copy-start.12
  71.9 6.7 copy-start.25
  78.5 372.5 %all-reduce.10.cloned.1.call-start = ((), (), s32[]{:S(2)}) async-start(), calls=%async_computation.1 | async-start | bytes 25165824 | tf_op jit(solution)/shard_map/psum | solution.py:94
  255.1 12.4 %copy-start.5 = (bf16[4096,1536]{1,0:T(8,128)(2,1)}, bf16[4096,1536]{1,0:T(8,128)(2,1)S(1)}, u32[]{:S(2)}) copy-start(bf16[4096,1536]{1,0:T(8,128)(2,1)S(1)} %fusion.12) | copy-start | bytes 37748740
  255.1 12.4 %copy-start.26 = (bf16[768,1536]{1,0:T(8,128)(2,1)S(1)}, bf16[768,1536]{1,0:T(8,128)(2,1)}, u32[]{:S(2)}) copy-start(bf16[768,1536]{1,0:T(8,128)(2,1)} %param.16) | copy-start | bytes 7077892
  307.3 529.3 %all-reduce.14.cloned.1.call-start = ((), (), s32[]{:S(2)}) async-start(), calls=%async_computation.3 | async-start | bytes 50331648 | tf_op jit(solution)/shard_map/psum | solution.py:85
  451.0 14.9 %copy-start.4 = (bf16[4096,1536]{1,0:T(8,128)(2,1)S(1)}, bf16[4096,1536]{1,0:T(8,128)(2,1)}, u32[]{:S(2)}) copy-start(bf16[4096,1536]{1,0:T(8,128)(2,1)} %all-reduce.10.cloned.1.call-done) | copy-start | bytes 37748740
  465.9 14.2 %copy-start.13 = (bf16[2,96,1536]{2,1,0:T(8,128)(2,1)S(1)}, bf16[2,96,1536]{2,1,0:T(8,128)(2,1)}, u32[]{:S(2)}) copy-start(bf16[2,96,1536]{2,1,0:T(8,128)(2,1)} %param.14) | copy-start | bytes 1769476
  484.6 9.8 copy-start.7
  502.5 24.5 %copy-start.11 = (bf16[8,512,2,1,96]{1,0,4,3,2:T(8,128)(2,1)S(1)}, bf16[8,512,2,1,96]{1,0,4,3,2:T(8,128)(2,1)}, u32[]{:S(2)}) copy-start(bf16[8,512,2,1,96]{1,0,4,3,2:T(8,128)(2,1)} %get-tuple-element.25) | copy-start | bytes 4718596
  551.0 11.1 %copy-start.29 = (bf16[1536,576]{0,1:T(8,128)(2,1)S(1)}, bf16[1536,576]{0,1:T(8,128)(2,1)}, u32[]{:S(2)}) copy-start(bf16[1536,576]{0,1:T(8,128)(2,1)} %param.13) | copy-start | bytes 5308420
  575.0 395.9 %all-reduce.12.cloned.1.call-start = ((), (), s32[]{:S(2)}) async-start(), calls=%async_computation.2 | async-start | bytes 14155776 | tf_op jit(solution)/shard_map/psum | solution.py:107
  588.2 34.0 %slice-start = ((s8[12582912]{0:T(1024)(128)(4,1)}), s8[4194304]{0:T(1024)(128)(4,1)S(1)}, s32[]{:S(2)}) async-start(s8[12582912]{0:T(1024)(128)(4,1)} %bitcast.122), calls=%async_computation.4 | async-start | bytes 8388608
  588.2 37.5 %slice-start.3 = ((s8[4718592]{0:T(1024)(128)(4,1)}), s8[4194304]{0:T(1024)(128)(4,1)S(1)}, s32[]{:S(2)}) async-start(s8[4718592]{0:T(1024)(128)(4,1)} %bitcast.134), calls=%async_computation.7 | async-start | bytes 8388608
  604.2 18.0 %slice-start.1 = ((s8[12582912]{0:T(1024)(128)(4,1)}), s8[4194304]{0:T(1024)(128)(4,1)S(1)}, s32[]{:S(2)}) async-start(s8[12582912]{0:T(1024)(128)(4,1)} %bitcast.122), calls=%async_computation.5 | async-start | bytes 8388608
  604.2 18.0 %slice-start.2 = ((s8[12582912]{0:T(1024)(128)(4,1)}), s8[4194304]{0:T(1024)(128)(4,1)S(1)}, s32[]{:S(2)}) async-start(s8[12582912]{0:T(1024)(128)(4,1)} %bitcast.122), calls=%async_computation.6 | async-start | bytes 8388608
  604.2 18.0 %copy-start.9 = (bf16[8,2,12,8,512]{4,3,0,2,1:T(8,128)(2,1)S(1)}, bf16[8,2,12,8,512]{4,3,0,2,1:T(8,128)(2,1)}, u32[]{:S(2)}) copy-start(bf16[8,2,12,8,512]{4,3,0,2,1:T(8,128)(2,1)} %copy-done.8) | copy-start | bytes 4718596
  604.2 21.4 %slice-start.4 = ((s8[4718592]{0:T(1024)(128)(4,1)}), s8[524288]{0:T(1024)(128)(4,1)S(1)}, s32[]{:S(2)}) async-start(s8[4718592]{0:T(1024)(128)(4,1)} %bitcast.134), calls=%async_computation.8 | async-start | bytes 1048576
  622.2 4.8 copy-start.6
  627.0 209.7 %copy-start.15 = (f32[1,4,8,128]{3,1,2,0:T(4,128)S(1)}, f32[1,4,8,128]{3,1,2,0:T(4,128)}, u32[]{:S(2)}) copy-start(f32[1,4,8,128]{3,1,2,0:T(4,128)} %copy-done.14) | copy-start | bytes 49156
  627.0 209.7 %copy-start.17 = (f32[1,4,8,128]{3,1,2,0:T(4,128)S(1)}, f32[1,4,8,128]{3,1,2,0:T(4,128)}, u32[]{:S(2)}) copy-start(f32[1,4,8,128]{3,1,2,0:T(4,128)} %copy-done.16) | copy-start | bytes 49156
  836.6 13.5 %copy-start.24 = (f32[1536]{0:T(1024)S(1)}, f32[1536]{0:T(1024)}, u32[]{:S(2)}) copy-start(f32[1536]{0:T(1024)} %get-tuple-element.8) | copy-start | bytes 18436
  925.4 16.6 %copy-start.3 = (bf16[4096,1536]{1,0:T(8,128)(2,1)S(1)}, bf16[4096,1536]{1,0:T(8,128)(2,1)}, u32[]{:S(2)}) copy-start(bf16[4096,1536]{1,0:T(8,128)(2,1)} %get-tuple-element.21) | copy-start | bytes 37748740
  942.0 40.0 %copy-start.1 = (bf16[1536,768]{1,0:T(8,128)(2,1)S(1)}, bf16[1536,768]{1,0:T(8,128)(2,1)}, u32[]{:S(2)}) copy-start(bf16[1536,768]{1,0:T(8,128)(2,1)} %param.15) | copy-start | bytes 7077892
  (9 other events, 16.8 us)
Sparse Core Ops, SparseCore 0:
  78.7 146.1 all-reduce.7
  307.4 143.5 all-reduce.9
  575.1 261.5 all-reduce.13
  840.9 129.8 all-reduce.11
where the time goes:
time: 994 us; the launch traced here: 989 us
  waiting for transfers between devices  483 us (49%)
  matrix products  235 us (24%)
  other arithmetic  148 us (15%)
  blocking collectives  75.2 us (8%)
  local copies, waits for them, and re-layouts  32.8 us (3%)
  between operations  14.3 us (1%)
    psum x1, waiting for transfers between devices, local_step(): sum_two = lax.psum(part_two.astype(jnp.bfloat16), 'tp')  201 us
    psum x1, waiting for transfers between devices, local_step(): sum_one = lax.psum(part_one.astype(jnp.bfloat16), 'tp')  146 us
    psum x1, waiting for transfers between devices, local_step(): grad_norm_b = lax.psum(part_b, 'tp')  125 us
    psum x1, blocking collectives, local_step(): gain_grads = lax.psum((gain_grad_one, gain_grad_two), 'dp')  75.2 us
    dot_general x3, matrix products, matmul_nt(): lax.dot_general(lhs, rhs, (((1,), (1,)), ((), ())), preferred_element_typ...  52.6 us
    dot_general x3, matrix products, matmul_tn(): lax.dot_general(lhs, rhs, (((0,), (0,)), ((), ())), preferred_element_typ...  42.8 us
    convert_element_type x3, other arithmetic, norm_forward(): (x_hat * gain_vec.astype(jnp.float32)).astype(jnp.bfloat16)  29 us
    reduce_sum x2, other arithmetic, norm_backward(): grad_gain = jnp.sum(grad_f32 * x_hat, axis=0)  28.4 us
  transfers between devices with their start and end apart: 4, of which 4 were waited for; matrix products, arithmetic and copies ran while one was open for 12% of the time, Pallas kernels for 0%

commit v1 on v0

v1 whole, which is shorter than its diff:
```python
import jax
import jax.numpy as jnp
from jax import lax
from jax.experimental import pallas as pl
from jax.experimental.pallas import tpu as pltpu
from jax.sharding import PartitionSpec as P

EPS_NORM = 1e-5
NEG_LARGE = -1e30
F32 = jnp.float32
BF16 = jnp.bfloat16
RING = 4


def gelu_tanh(values):
    return jax.nn.gelu(values, approximate=True)


def norm_forward(x_rows, gain_vec):
    x_f32 = x_rows.astype(F32)
    centered = x_f32 - jnp.mean(x_f32, axis=-1, keepdims=True)
    inv_std = lax.rsqrt(jnp.mean(centered * centered, axis=-1, keepdims=True) + EPS_NORM)
    x_hat = centered * inv_std
    return (x_hat * gain_vec.astype(F32)).astype(BF16), x_hat, inv_std


def norm_backward(grad_out, x_hat, inv_std, gain_vec):
    grad_f32 = grad_out.astype(F32)
    grad_gain = jnp.sum(grad_f32 * x_hat, axis=0)
    grad_hat = grad_f32 * gain_vec.astype(F32)
    mean_one = jnp.mean(grad_hat, axis=-1, keepdims=True)
    mean_two = jnp.mean(grad_hat * x_hat, axis=-1, keepdims=True)
    return inv_std * (grad_hat - mean_one - x_hat * mean_two), grad_gain


def dot_nt(lhs, rhs):
    return lax.dot_general(lhs, rhs, (((lhs.ndim - 1,), (rhs.ndim - 1,)), ((), ())), preferred_element_type=F32)


def dot_tn(lhs, rhs):
    return lax.dot_general(lhs, rhs, (((0,), (0,)), ((), ())), preferred_element_type=F32)


def dot_nn(lhs, rhs):
    return lax.dot_general(lhs, rhs, (((lhs.ndim - 1,), (0,)), ((), ())), preferred_element_type=F32)


def core_swap(array):
    return lax.ppermute(array, "tp", [(i, i ^ 1) for i in range(8)])


THIRD = 512
PIECE = 48
WIDTH = 1536
HALF = WIDTH // 2
MESH_ID = pl.DeviceIdType.MESH


class Place:
    def __init__(self):
        plane = lax.axis_index("dp")
        column = lax.axis_index("tp")
        self.pos = {"z": lax.div(plane, RING), "y": lax.rem(plane, RING), "x": lax.div(column, 2)}
        self.core = lax.rem(column, 2)

    def ahead(self, axis, step):
        return lax.rem(self.pos[axis] + step, RING)

    def peer(self, axis, step):
        if axis == "x":
            return {"tp": self.ahead("x", step) * 2 + self.core}
        if axis == "y":
            return {"dp": self.pos["z"] * RING + self.ahead("y", step)}
        return {"dp": self.ahead("z", step) * RING + self.pos["y"]}

    def block(self, axis, step):
        return step if axis == "x" else self.ahead(axis, step)

    def enter(self):
        barrier = pltpu.get_barrier_semaphore()
        for axis in "xyz":
            for step in range(1, RING):
                pl.semaphore_signal(barrier, inc=1, device_id=self.peer(axis, step), device_id_type=MESH_ID)
        pl.semaphore_wait(barrier, 9)


class Sender:
    def __init__(self, place, send_sems, recv_sems):
        self.place, self.send_sems, self.recv_sems = place, send_sems, recv_sems
        self.used = 0
        self.copies = []

    def ring(self, axis, source, target):
        started = []
        for step in range(1, RING):
            copy = pltpu.make_async_remote_copy(
                src_ref=source(step), dst_ref=target(step),
                send_sem=self.send_sems.at[self.used], recv_sem=self.recv_sems.at[self.used],
                device_id=self.place.peer(axis, step), device_id_type=MESH_ID,
            )
            copy.start()
            self.used += 1
            started.append(copy)
        self.copies += started
        return started

    def drain(self):
        for copy in self.copies:
            copy.wait_send()


def wait_all(copies):
    for copy in copies:
        copy.wait_recv()


class WeightGather:
    COPIES = 21

    def __init__(self, place, sender, own, out):
        self.place, self.sender, self.own, self.out = place, sender, own, out

    def spot(self, cols):
        z, y = self.place.pos["z"], self.place.pos["y"]
        return lambda step: self.out.at[pl.ds(1, 3), z, y, :, cols]

    def start(self):
        z, y = self.place.pos["z"], self.place.pos["y"]
        self.near = []
        for part in range(2):
            cols = pl.ds(part * THIRD, THIRD)
            self.near.append(self.sender.ring(
                "x", lambda step: self.own.at[z, y, :, cols], lambda step: self.out.at[RING - step, z, y, :, cols]))
        cols = pl.ds(2 * THIRD, THIRD)
        self.whole = self.sender.ring(
            "x", lambda step: self.own.at[:, :, :, cols], lambda step: self.out.at[RING - step, :, :, :, cols])

    def second(self):
        self.mid = []
        for part, axis in enumerate("yz"):
            wait_all(self.near[part])
            spot = self.spot(pl.ds(part * THIRD, THIRD))
            self.mid.append(self.sender.ring(axis, spot, spot))

    def third(self):
        z, y = self.place.pos["z"], self.place.pos["y"]
        wait_all(self.mid[0])
        line = lambda step: self.out.at[pl.ds(1, 3), z, :, :, pl.ds(0, THIRD)]
        self.far = self.sender.ring("z", line, line)
        wait_all(self.mid[1])
        row = lambda step: self.out.at[pl.ds(1, 3), :, y, :, pl.ds(THIRD, THIRD)]
        self.far += self.sender.ring("y", row, row)

    def finish(self):
        wait_all(self.far)
        wait_all(self.whole)


def gather_kernel(count, *refs):
    owns, outs = refs[:count], refs[count : 2 * count]
    stage, send_sems, recv_sems, local_sems = refs[2 * count :]
    place = Place()
    sender = Sender(place, send_sems, recv_sems)
    gathers = [WeightGather(place, sender, own, out) for own, out in zip(owns, outs)]
    loads = [pltpu.make_async_copy(own, stage.at[i], local_sems.at[i]) for i, own in enumerate(owns)]
    for load in loads:
        load.start()
    place.enter()
    for gather in gathers:
        gather.start()
    stores = []
    for i in range(count):
        loads[i].wait()
        store = pltpu.make_async_copy(stage.at[i], outs[i].at[0], local_sems.at[count + i])
        store.start()
        stores.append(store)
    for gather in gathers:
        gather.second()
    for gather in gathers:
        gather.third()
    for gather in gathers:
        gather.finish()
    for store in stores:
        store.wait()
    sender.drain()


def gather_weights(owns, collective_id):
    count = len(owns)
    copies = WeightGather.COPIES * count
    return pl.pallas_call(
        lambda *refs: gather_kernel(count, *refs),
        out_shape=[jax.ShapeDtypeStruct((RING,) + own.shape, own.dtype) for own in owns],
        in_specs=[pl.BlockSpec(memory_space=pl.ANY)] * count,
        out_specs=[pl.BlockSpec(memory_space=pl.ANY)] * count,
        scratch_shapes=[
            pltpu.VMEM((count,) + owns[0].shape, owns[0].dtype),
            pltpu.SemaphoreType.DMA((copies,)),
            pltpu.SemaphoreType.DMA((copies,)),
            pltpu.SemaphoreType.DMA((2 * count,)),
        ],
        compiler_params=pltpu.CompilerParams(collective_id=collective_id, has_side_effects=True),
        name=f"gather_weights_{collective_id}",
    )(*owns)


ORDERS = (("z", "y", "x", 1), ("y", "x", "z", 0), ("x", "z", "y", 0))


class GradScatter:
    COPIES = 27

    def __init__(self, place, sender, grads, mine, first, second, third, final, local_sems):
        self.place, self.sender, self.grads = place, sender, grads
        self.mine, self.bufs, self.final, self.local_sems = mine, (first, second, third), final, local_sems

    def cut(self, part, step):
        axis = ORDERS[part][0]
        index = self.place.block(axis, step)
        cols = pl.ds(part * THIRD, THIRD)
        if axis == "x":
            return self.grads.at[index, :, :, :, cols]
        if axis == "z":
            return self.grads.at[:, index, :, :, cols]
        return self.grads.at[:, :, index, :, cols]

    def start(self):
        self.loads, self.one, self.two, self.three = [], [], [None] * 3, [None] * 3
        for part in range(3):
            self.one.append(self.sender.ring(
                ORDERS[part][0], lambda step: self.cut(part, step), lambda step: self.bufs[0].at[part, step - 1]))
        for part in range(3):
            load = pltpu.make_async_copy(self.cut(part, 0), self.mine.at[part], self.local_sems.at[part])
            load.start()
            self.loads.append(load)

    def second(self, part):
        self.loads[part].wait()
        wait_all(self.one[part])

        @pl.loop(0, RING)
        def _(a):
            for b in range(RING):
                total = self.mine[part, a, b].astype(F32)
                for k in range(3):
                    total = total + self.bufs[0][part, k, a, b].astype(F32)
                self.mine[part, a, b] = total.astype(BF16)

        axis, spot = ORDERS[part][1], ORDERS[part][3]

        def source(step):
            index = self.place.block(axis, step)
            return self.mine.at[part, :, index] if spot else self.mine.at[part, index]

        self.two[part] = self.sender.ring(axis, source, lambda step: self.bufs[1].at[part, step - 1])

    def third(self, part):
        wait_all(self.two[part])
        axis, spot = ORDERS[part][1], ORDERS[part][3]
        own = self.place.block(axis, 0)
        for other in range(RING):
            at = (part, other, own) if spot else (part, own, other)
            total = self.mine[at].astype(F32)
            for k in range(3):
                total = total + self.bufs[1][part, k, other].astype(F32)
            self.bufs[1][part, 3, other] = total.astype(BF16)
        axis = ORDERS[part][2]
        self.three[part] = self.sender.ring(
            axis, lambda step: self.bufs[1].at[part, 3, self.place.block(axis, step)], lambda step: self.bufs[2].at[part, step - 1])

    def finish(self, part):
        wait_all(self.three[part])
        own = self.place.block(ORDERS[part][2], 0)
        total = self.bufs[1][part, 3, own].astype(F32)
        for k in range(3):
            total = total + self.bufs[2][part, k].astype(F32)
        self.final[:, part * THIRD : (part + 1) * THIRD] = total.astype(BF16)


class PlaneGather:
    COPIES = 12

    def __init__(self, place, sender, final, out, local_sem):
        self.place, self.sender, self.final, self.out, self.local_sem = place, sender, final, out, local_sem

    def start(self):
        z, y = self.place.pos["z"], self.place.pos["y"]
        self.store = pltpu.make_async_copy(self.final, self.out.at[z, y], self.local_sem)
        self.store.start()
        self.near = []
        for part, axis in enumerate("yz"):
            cols = pl.ds(part * HALF, HALF)
            self.near.append(self.sender.ring(
                axis, lambda step: self.final.at[:, cols], lambda step: self.out.at[z, y, :, cols]))

    def second(self):
        z, y = self.place.pos["z"], self.place.pos["y"]
        self.store.wait()
        wait_all(self.near[0])
        line = lambda step: self.out.at[z, :, :, pl.ds(0, HALF)]
        self.far = self.sender.ring("z", line, line)
        wait_all(self.near[1])
        row = lambda step: self.out.at[:, y, :, pl.ds(HALF, HALF)]
        self.far += self.sender.ring("y", row, row)

    def finish(self):
        wait_all(self.far)


def gain_step(place, sender, gains, bufs, index, axis):
    copies = sender.ring(axis, lambda step: gains.at[index], lambda step: bufs.at[index, step - 1])

    def finish():
        wait_all(copies)
        gains[index + 1] = (gains[index] + bufs[index, 1]) + (bufs[index, 0] + bufs[index, 2])

    return finish


def scatter_kernel(count, with_gains, *refs):
    grads, refs = refs[:count], refs[count:]
    if with_gains:
        gain_in, refs = refs[0], refs[1:]
    outs, refs = refs[:count], refs[count:]
    if with_gains:
        gain_out, refs = refs[0], refs[1:]
    mine, first, second, third, final, send_sems, recv_sems, local_sems = refs[:8]
    place = Place()
    sender = Sender(place, send_sems, recv_sems)
    place.enter()
    works = []
    for i in range(count):
        works.append(GradScatter(place, sender, grads[i], mine.at[i], first.at[i], second.at[i], third.at[i], final.at[i], local_sems.at[i]))
    planes = [PlaneGather(place, sender, final.at[i], outs[i], local_sems.at[i, 3]) for i in range(count)]
    if with_gains:
        gains, gain_bufs = refs[8:]
        gains[0] = gain_in[...]
        gain_finish = gain_step(place, sender, gains, gain_bufs, 0, "z")
    for work in works:
        work.start()
    for work in works:
        for part in range(3):
            work.second(part)
    if with_gains:
        gain_finish()
        gain_finish = gain_step(place, sender, gains, gain_bufs, 1, "y")
    for work in works:
        for part in range(3):
            work.third(part)
    if with_gains:
        gain_finish()
        gain_finish = gain_step(place, sender, gains, gain_bufs, 2, "x")
    for work, plane in zip(works, planes):
        for part in range(3):
            work.finish(part)
        plane.start()
    if with_gains:
        gain_finish()
        gain_out[...] = gains[3]
    for plane in planes:
        plane.second()
    for plane in planes:
        plane.finish()
    sender.drain()


def scatter_grads(grads, gains, collective_id):
    count = len(grads)
    with_gains = gains is not None
    copies = (GradScatter.COPIES + PlaneGather.COPIES) * count + 9 * with_gains
    block = (RING, RING, PIECE, THIRD)
    any_spec = pl.BlockSpec(memory_space=pl.ANY)
    vmem_spec = pl.BlockSpec(memory_space=pltpu.VMEM)
    scratch = [
        pltpu.VMEM((count, 3) + block, BF16),
        pltpu.VMEM((count, 3, 3) + block, BF16),
        pltpu.VMEM((count, 3, 4) + block[1:], BF16),
        pltpu.VMEM((count, 3, 3) + block[2:], BF16),
        pltpu.VMEM((count, PIECE, WIDTH), BF16),
        pltpu.SemaphoreType.DMA((copies,)),
        pltpu.SemaphoreType.DMA((copies,)),
        pltpu.SemaphoreType.DMA((count, 4)),
    ]
    out_shape = [jax.ShapeDtypeStruct(grad.shape[1:], BF16) for grad in grads]
    operands = list(grads)
    if with_gains:
        scratch += [pltpu.VMEM((4,) + gains.shape, F32), pltpu.VMEM((3, 3) + gains.shape, F32)]
        out_shape.append(jax.ShapeDtypeStruct(gains.shape, F32))
        operands.append(gains)
    return pl.pallas_call(
        lambda *refs: scatter_kernel(count, with_gains, *refs),
        out_shape=out_shape,
        in_specs=[any_spec] * count + [vmem_spec] * with_gains,
        out_specs=[any_spec] * count + [vmem_spec] * with_gains,
        scratch_shapes=scratch,
        compiler_params=pltpu.CompilerParams(collective_id=collective_id, has_side_effects=True, vmem_limit_bytes=56 << 20),
        name=f"scatter_grads_{collective_id}",
    )(*operands)


def attention_forward(q_t, k_t, v_t, allowed, score_scale):
    scores = jnp.einsum("ndbq,ndbk->bnqk", q_t, k_t, preferred_element_type=F32) * score_scale
    attn_probs = jax.nn.softmax(jnp.where(allowed, scores, NEG_LARGE), axis=-1)
    attn_out = jnp.einsum("bnqk,ndbk->ndbq", attn_probs.astype(BF16), v_t, preferred_element_type=F32)
    return attn_out.astype(BF16), attn_probs


def attention_backward(grad_out, q_t, k_t, v_t, attn_probs, score_scale):
    grad_v = jnp.einsum("bnqk,ndbq->ndbk", attn_probs.astype(BF16), grad_out, preferred_element_type=F32)
    grad_probs = jnp.einsum("ndbq,ndbk->bnqk", grad_out, v_t, preferred_element_type=F32)
    grad_scores = attn_probs * (grad_probs - jnp.sum(grad_probs * attn_probs, axis=-1, keepdims=True))
    grad_low = (grad_scores * score_scale).astype(BF16)
    grad_q = jnp.einsum("bnqk,ndbk->ndbq", grad_low, k_t, preferred_element_type=F32)
    grad_k = jnp.einsum("bnqk,ndbq->ndbk", grad_low, q_t, preferred_element_type=F32)
    return grad_q, grad_k, grad_v


def solution(mesh):
    batch_spec = P(("pod", "dp"), None, None)
    seg_spec = P(("pod", "dp"), None)

    def local_step(x_in, seg_ids, gain_one, gain_two, w_qkv, w_out, w_up, w_down, grad_y):
        batch_loc, seq_len, hidden = x_in.shape
        heads_loc, head_dim = w_out.shape[:2]
        score_scale = head_dim ** -0.5
        rows_loc = batch_loc // RING
        tokens = rows_loc * seq_len
        shard_rows = w_up.shape[1]
        qkv_cols = w_qkv.shape[1]
        x_pos = lax.axis_index("tp") // 2

        def own_rows(array):
            return lax.dynamic_slice_in_dim(array, x_pos * rows_loc, rows_loc, axis=0)

        def grid_of(own):
            return own.reshape(RING, RING, PIECE, hidden)

        own_att = grid_of(jnp.concatenate([w_qkv.T, w_out.reshape(heads_loc * head_dim, hidden)], axis=0))
        own_up = grid_of(w_up.T)
        own_down = grid_of(w_down)
        (w_att,) = gather_weights([own_att], 1)
        up_t, down = gather_weights([own_up, own_down], 2)
        w_att = w_att.reshape(RING, shard_rows, hidden)
        up_t = up_t.reshape(RING * shard_rows, hidden)
        down = down.reshape(RING * shard_rows, hidden)
        w_qkv_t = w_att[:, :qkv_cols]
        w_out_all = w_att[:, qkv_cols:].reshape(RING * heads_loc * head_dim, hidden)

        x_rows = own_rows(x_in).reshape(tokens, hidden)
        seg_rows = own_rows(seg_ids)
        grad_rows = own_rows(grad_y).reshape(tokens, hidden)
        positions = jnp.arange(seq_len)
        allowed = (positions[:, None] >= positions[None, :])[None, None] & (seg_rows[:, None, :, None] == seg_rows[:, None, None, :])
        normed_a, hat_a, inv_a = norm_forward(x_rows, gain_one)
        qkv_t = dot_nt(w_qkv_t, normed_a).astype(BF16)
        qkv_t = qkv_t.reshape(RING * heads_loc, 3, head_dim, rows_loc, seq_len)
        q_t, k_t, v_t = qkv_t[:, 0], qkv_t[:, 1], qkv_t[:, 2]
        attn_t, attn_probs = attention_forward(q_t, k_t, v_t, allowed, score_scale)
        attn_flat = attn_t.reshape(RING * heads_loc * head_dim, tokens)

        def pair_sum(part):
            return part.astype(F32) + core_swap(part).astype(F32)

        part_one = dot_tn(attn_flat, w_out_all).astype(BF16)
        sum_one = pair_sum(part_one).astype(BF16)
        x_one = (x_rows.astype(F32) + sum_one.astype(F32)).astype(BF16)
        normed_b, hat_b, inv_b = norm_forward(x_one, gain_two)
        pre_act = dot_nt(up_t, normed_b)
        act_val, gelu_pull = jax.vjp(gelu_tanh, pre_act)
        hidden_act = act_val.astype(BF16)
        part_two = dot_tn(hidden_act, down).astype(BF16)
        sum_two = pair_sum(part_two).astype(BF16)
        y_rows = (x_one.astype(F32) + sum_two.astype(F32)).astype(BF16)

        grad_hidden = dot_nt(down, grad_rows).astype(BF16)
        grad_pre = gelu_pull(grad_hidden.astype(F32))[0].astype(BF16)

        grid_shape = (RING, RING, RING, PIECE, hidden)
        grad_down_w = dot_nn(hidden_act, grad_rows).astype(BF16).reshape(grid_shape)
        grad_up_w = dot_nn(grad_pre, normed_b).astype(BF16).reshape(grid_shape)
        grad_up_own, grad_down_own = scatter_grads([grad_up_w, grad_down_w], None, 3)

        part_b = dot_tn(grad_pre, up_t).astype(BF16)
        grad_norm_b = pair_sum(part_b).astype(BF16)
        back_b, gain_grad_two = norm_backward(grad_norm_b, hat_b, inv_b, gain_two)
        grad_x_one = (grad_rows.astype(F32) + back_b).astype(BF16)
        grad_out_w = dot_nn(attn_flat, grad_x_one).astype(BF16)
        grad_attn = dot_nt(w_out_all, grad_x_one).astype(BF16)
        grad_q, grad_k, grad_v = attention_backward(grad_attn.reshape(attn_t.shape), q_t, k_t, v_t, attn_probs, score_scale)
        grad_qkv_t = jnp.stack([grad_q, grad_k, grad_v], axis=1).astype(BF16).reshape(RING * qkv_cols, tokens)
        part_a = dot_tn(grad_qkv_t, w_qkv_t.reshape(RING * qkv_cols, hidden)).astype(BF16)
        grad_norm_a = pair_sum(part_a).astype(BF16)
        back_a, gain_grad_one = norm_backward(grad_norm_a, hat_a, inv_a, gain_one)
        grad_x = (grad_x_one.astype(F32) + back_a).astype(BF16)

        grad_qkv_w = dot_nn(grad_qkv_t, normed_a).astype(BF16)
        grad_att = jnp.concatenate([grad_qkv_w.reshape(RING, qkv_cols, hidden), grad_out_w.reshape(RING, shard_rows - qkv_cols, hidden)], axis=1)
        gains = jnp.concatenate([gain_grad_one[None], gain_grad_two[None], jnp.zeros((6, hidden), F32)], axis=0)
        grad_att_own, gains = scatter_grads([grad_att.reshape(grid_shape)], gains, 4)
        grad_att_own = grad_att_own.reshape(shard_rows, hidden)

        def spread(rows):
            core = lax.axis_index("tp") % 2
            mine = lax.dynamic_slice_in_dim(rows.reshape(rows_loc, seq_len, hidden), core, 1, axis=0)
            return lax.all_gather(mine, "tp", axis=0, tiled=True)

        return (
            spread(y_rows),
            spread(grad_x),
            gains[0].astype(BF16),
            gains[1].astype(BF16),
            grad_att_own[:qkv_cols].T,
            grad_att_own[qkv_cols:].reshape(heads_loc, head_dim, hidden),
            grad_up_own.reshape(shard_rows, hidden).T,
            grad_down_own.reshape(shard_rows, hidden),
        )

    return jax.shard_map(
        local_step,
        mesh=mesh,
        in_specs=(batch_spec, seg_spec, P(None), P(None), P(None, "tp"), P("tp", None, None), P(None, "tp"), P("tp", None), batch_spec),
        out_specs=(batch_spec, batch_spec, P("pod"), P("pod"), P("pod", "tp"), P(("pod", "tp"), None, None), P("pod", "tp"), P(("pod", "tp"), None)),
        check_vma=False,
    )
```

time: 994 us -> 749 us (0.75)
  waiting for transfers between devices: 483 us -> 5.68 us
  Pallas kernels: 0 us -> 387 us
  other arithmetic: 148 us -> 59.2 us
  blocking collectives: 75.2 us -> 0 us
  local copies, waits for them, and re-layouts: 32.8 us -> 88.5 us
  matrix products: 235 us -> 188 us
    psum x4 -> x0, waiting for transfers between devices: 482 us -> none  [the longest x1 201 us: local_step(): sum_two = lax.psum(part_two.astype(jnp.bfloat16), 'tp')]
    pallas_call x0 -> x4, Pallas kernels: none -> 387 us  [the longest x2 229 us: scatter_grads(): pl.pallas_call(lambda *refs: scatter_kernel(count, with_gains, *refs), ou...]
    psum x1 -> x0, blocking collectives: 75.2 us -> none  [local_step(): gain_grads = lax.psum((gain_grad_one, gain_grad_two), 'dp')]
    dot_general x17 -> x16, matrix products: 221 us -> 158 us  [the longest x4 49.3 us: dot_nt(): lax.dot_general(lhs, rhs, (((lhs.ndim - 1,), (rhs.ndim - 1,)), ((), ())),...]
    convert_element_type x9 -> x7, other arithmetic: 79.9 us -> 24.7 us  [the longest x4 8.15 us: norm_forward(): return ((x_hat * gain_vec.astype(F32)).astype(BF16), x_hat, inv_std)]
    slice x1 -> x6, local copies, waits for them, and re-layouts: 2.32 us -> 22 us  [the longest x1 6.68 us: local_step(): q_t, k_t, v_t = (qkv_t[:, 0], qkv_t[:, 1], qkv_t[:, 2])]
    sub x0 -> x1, matrix products: none -> 19.2 us  [attention_backward(): grad_probs - jnp.sum(grad_probs * attn_probs, axis=-1, keepdims=True)]
    reduce_sum x2, other arithmetic: 28.4 us -> 10.1 us  [norm_backward(): grad_gain = jnp.sum(grad_f32 * x_hat, axis=0)]
  transfers between devices with their start and end apart: 4 -> 6, of which waited for: 4 -> 1; matrix products, arithmetic and copies ran while one was open for 12% -> 24% of each run, Pallas kernels for 0% -> 46%
where the time goes in v1:
time: 749 us; the launch traced here: 745 us
  Pallas kernels  387 us (52%)
  matrix products  188 us (25%)
  local copies, waits for them, and re-layouts  88.5 us (12%)
  other arithmetic  59.2 us (8%)
  between operations  15 us (2%)
    pallas_call x2, Pallas kernels, scatter_grads(): pl.pallas_call(lambda *refs: scatter_kernel(count, with_gains, *refs), ou...  229 us
    pallas_call x2, Pallas kernels, gather_weights(): pl.pallas_call(lambda *refs: gather_kernel(count, *refs), out_shape=[jax....  158 us
    dot_general x4, matrix products, dot_nt(): lax.dot_general(lhs, rhs, (((lhs.ndim - 1,), (rhs.ndim - 1,)), ((), ())),...  49.3 us
    dot_general x4, matrix products, dot_nn(): lax.dot_general(lhs, rhs, (((lhs.ndim - 1,), (0,)), ((), ())), preferred_...  46.4 us
    dot_general x4, matrix products, dot_tn(): lax.dot_general(lhs, rhs, (((0,), (0,)), ((), ())), preferred_element_typ...  45.5 us
    unnamed x95, local copies, waits for them, and re-layouts  28.7 us
    sub x1, matrix products, attention_backward(): grad_probs - jnp.sum(grad_probs * attn_probs, axis=-1, keepdims=True)  19.2 us
  transfers between devices with their start and end apart: 6, of which 1 were waited for; matrix products, arithmetic and copies ran while one was open for 24% of the time, Pallas kernels for 46%

profile of v1, /device:TPU:0, one launch (start us, length us, event | category | flops | bytes accessed | tf_op | source)
XLA Modules:
  0.0 744.6 jit_solution(2282994988764239014)
XLA Ops:
  15.4 47.1 %gather_weights_1.1 = bf16[4,4,4,48,1536]{4,3,2,1,0:T(8,128)(2,1)} custom-call(bf16[4,4,48,1536]{3,2,1,0:T(8,128)(2,1)} %bitcast.155), custom_call_target="tpu_custom_call" | custom-call | tf_op jit(solution)/shard_map/gather_weights_1/pallas_call | solution.py:191
  69.6 9.5 %fusion.64 = bf16[4,576,1024]{2,1,0:T(8,128)(2,1)} fusion(bf16[1024,1536]{1,0:T(8,128)(2,1)S(1)} %fusion.60, bf16[4,768,1536]{2,1,0:T(8,128)(2,1)S(1)} %bitcast.147), kind=kOutput, calls=%fused_computation.97 | convolution fusion | flops 7250116608 | bytes 14942208 | tf_op jit(solution)/shard_map/dot_general | solution.py:37
  79.1 8.8 %reshape.214 = bf16[8,3,96,2,512]{4,3,2,1,0:T(2,128)(2,1)} reshape(bf16[4,576,1024]{2,1,0:T(8,128)(2,1)} %fusion.64) | data formatting | bytes 9437184 | tf_op jit(solution)/shard_map/reshape | solution.py:456
  87.9 6.7 fusion.132
  96.2 10.8 %fusion.133 = (f32[2,8,512]{2,1,0:T(8,128)S(1)}, f32[2,8,512,512]{2,3,1,0:T(8,128)}) fusion(pred[2,512,512]{1,2,0:T(8,128)(4,1)} %compare_and_fusion, bf16[8,1,96,2,512]{4,3,2,1,0:T(2,128)(2,1)S(1)} %get-tuple-element.34, bf16[8,1,96,2,512]{4,3,2,1,0:T(2,128)(2,1)S(1)} %get-tuple-element.33), kind=kOutput, calls=%fused_computation.151 | convolution fusion | flops 822084096 | bytes 20480000 | tf_op jit(solution)/shard_map/sub | solution.py:403
  107.0 6.8 fusion.130
  122.3 5.1 copy.52
  127.4 111.0 %gather_weights_2.1 = (bf16[4,4,4,48,1536]{4,3,2,1,0:T(8,128)(2,1)}, bf16[4,4,4,48,1536]{4,3,2,1,0:T(8,128)(2,1)}) custom-call(bf16[4,4,48,1536]{3,2,1,0:T(8,128)(2,1)} %bitcast.154, bf16[4,4,48,1536]{3,2,1,0:T(8,128)(2,1)} %bitcast.166), custom_call_target="tpu_custom_call" | custom-call | tf_op jit(solution)/shard_map/gather_weights_2/pallas_call | solution.py:191
  240.8 6.3 convert_reduce_fusion
  248.1 13.1 %fusion.128 = f32[3072,1024]{1,0:T(8,128)} fusion(bf16[3072,1536]{1,0:T(8,128)(2,1)S(1)} %bitcast.189, bf16[1024,1536]{1,0:T(8,128)(2,1)S(1)} %get-tuple-element.31, f32[1536]{0:T(1024)S(1)} %convert_element_type.195, f32[1024]{0:T(1024)S(1)} %add_rsqrt_fusion, f32[1024]{0:T(1024)S(1)} %broadcast_multiply_fusion.4), kind=kOutput, calls=%fused_computation.148 | convolution fusion | flops 9671540736 | bytes 25180160 | tf_op jit(solution)/shard_map/dot_general | solution.py:37
  261.2 23.0 %fusion.6 = bf16[3072,1024]{1,0:T(8,128)(2,1)} fusion(f32[3072,1024]{1,0:T(8,128)} %fusion.128, bf16[3072,1536]{1,0:T(8,128)(2,1)} %bitcast.184, bf16[1024,1536]{1,0:T(8,128)(2,1)S(1)} %bitcast.150), kind=kOutput, calls=%fused_computation.14 | convolution fusion | flops 9732882432 | bytes 31457280 | tf_op jit(solution)/shard_map/dot_general | solution.py:37
  284.2 16.2 %convolution_convert_fusion.3 = bf16[1024,1536]{1,0:T(8,128)(2,1)} fusion(bf16[3072,1024]{1,0:T(8,128)(2,1)} %fusion.6, bf16[3072,1536]{1,0:T(8,128)(2,1)} %bitcast.186), kind=kOutput, calls=%fused_computation.90 | convolution fusion | flops 9665249280 | bytes 18874368 | tf_op jit(solution)/shard_map/dot_general | solution.py:41
  300.3 16.1 %convolution_convert_fusion.4 = bf16[1024,1536]{1,0:T(8,128)(2,1)} fusion(bf16[3072,1536]{1,0:T(8,128)(2,1)} %bitcast.185, f32[3072,1024]{1,0:T(8,128)S(1)} %copy-done.37), kind=kOutput, calls=%fused_computation.91 | convolution fusion | flops 9693560832 | bytes 25165824 | tf_op jit(solution)/shard_map/dot_general | solution.py:41
  316.9 6.1 fusion.44
  323.1 6.9 fusion.41
  331.3 6.6 slice.43
  345.5 7.7 %fusion.105 = bf16[8,1,96,2,512]{4,2,3,0,1:T(8,128)(2,1)} fusion(bf16[2,8,512,512]{2,3,1,0:T(8,128)(2,1)} %copy-done.10, bf16[8,96,2,512]{3,2,1,0:T(2,128)(2,1)} %reshape.223), kind=kOutput, calls=%fused_computation.120 | convolution fusion | flops 806092800 | bytes 11534336 | tf_op jit(solution)/shard_map/bnqk,ndbq->ndbk/dot_general | solution.py:409
  353.2 19.2 %multiply_convert_fusion = bf16[2,8,512,512]{2,3,1,0:T(8,128)(2,1)} fusion(bf16[8,1,96,2,512]{4,3,2,1,0:T(2,128)(2,1)} %get-tuple-element.32, bf16[8,96,2,512]{3,2,1,0:T(2,128)(2,1)} %reshape.223, f32[2,8,512,512]{2,3,1,0:T(8,128)} %get-tuple-element.42, f32[2,8,512]{2,1,0:T(8,128)S(1)} %get-tuple-element.41), kind=kOutput, calls=%fused_computation.4 | convolution fusion | flops 1639981568 | bytes 28344320 | tf_op jit(solution)/shard_map/sub | solution.py:411
  372.3 6.7 fusion.95
  383.1 9.3 %copy.61 = bf16[8,3,96,2,512]{4,3,2,1,0:T(2,128)(2,1)} copy(bf16[8,3,96,2,512]{4,2,3,0,1:T(8,128)(2,1)} %pad_maximum_fusion.1) | data formatting | bytes 9437184 | tf_op jit(solution)/shard_map/stack | solution.py:490
  398.6 10.3 %convolution_convert_fusion.5 = bf16[1024,1536]{1,0:T(8,128)(2,1)S(1)} fusion(bf16[2304,1024]{1,0:T(8,128)(2,1)S(1)} %bitcast.161, bf16[2304,1536]{1,0:T(8,128)(2,1)} %bitcast.156), kind=kOutput, calls=%fused_computation.92 | convolution fusion | flops 7249330176 | bytes 14942208 | tf_op jit(solution)/shard_map/dot_general | solution.py:41
  409.0 5.6 collective-permute-done.3
  423.0 4.5 fusion.56
  427.6 15.3 %convolution_convert_fusion.1 = bf16[3072,1536]{1,0:T(8,128)(2,1)} fusion(bf16[3072,1024]{1,0:T(8,128)(2,1)} %fusion.6, bf16[1024,1536]{1,0:T(8,128)(2,1)S(1)} %get-tuple-element.31, f32[1536]{0:T(1024)S(1)} %convert_element_type.195, f32[1024]{0:T(1024)S(1)} %add_rsqrt_fusion, f32[1024]{0:T(1024)S(1)} %broadcast_multiply_fusion.4), kind=kOutput, calls=%fused_computation.24 | convolution fusion | flops 9676259328 | bytes 18888704 | tf_op jit(solution)/shard_map/dot_general | solution.py:45
  442.9 16.5 %convolution_convert_fusion = bf16[3072,1536]{1,0:T(8,128)(2,1)} fusion(bf16[1024,1536]{1,0:T(8,128)(2,1)S(1)} %bitcast.151, f32[3072,1024]{1,0:T(8,128)} %fusion.128), kind=kOutput, calls=%fused_computation.23 | convolution fusion | flops 9696706560 | bytes 25165824 | tf_op jit(solution)/shard_map/dot_general | solution.py:45
  459.3 150.9 %scatter_grads_3.1 = (bf16[4,4,48,1536]{3,2,1,0:T(8,128)(2,1)}, bf16[4,4,48,1536]{3,2,1,0:T(8,128)(2,1)}) custom-call(bf16[4,4,4,48,1536]{4,3,2,1,0:T(8,128)(2,1)} %bitcast.152, bf16[4,4,4,48,1536]{4,3,2,1,0:T(8,128)(2,1)} %bitcast.153), custom_call_target="tpu_custom_call" | custom-call | tf_op jit(solution)/shard_map/scatter_grads_3/pallas_call | solution.py:390
  610.2 4.3 copy.62
  614.5 4.4 convolution_convert_fusion.7
  618.9 10.2 %convolution_convert_fusion.2 = bf16[2304,1536]{1,0:T(8,128)(2,1)S(1)} fusion(bf16[2304,1024]{1,0:T(8,128)(2,1)} %bitcast.162, bf16[1024,1536]{1,0:T(8,128)(2,1)S(1)} %bitcast.163), kind=kOutput, calls=%fused_computation.25 | convolution fusion | flops 7251296256 | bytes 14942208 | tf_op jit(solution)/shard_map/dot_general | solution.py:45
  633.7 78.2 %scatter_grads_4.1 = (bf16[4,4,48,1536]{3,2,1,0:T(8,128)(2,1)}, f32[8,1536]{1,0:T(8,128)}) custom-call(bf16[4,4,4,48,1536]{4,3,2,1,0:T(8,128)(2,1)} %bitcast.148, f32[8,1536]{1,0:T(8,128)} %maximum_maximum_fusion.refs_1_), custom_call_target="tpu_custom_call" | custom-call | tf_op jit(solution)/shard_map/scatter_grads_4/pallas_call | solution.py:390
  718.1 11.0 %copy.166 = bf16[8,512,1536]{2,1,0:T(8,128)(2,1)} copy(bf16[8,512,1536]{2,1,0:T(8,128)(2,1)} %all-gather.3.cloned.1.call-done) | data formatting | bytes 25165824
  731.1 5.0 copy.167
  (148 shorter events, 70.7 us)
Async XLA Ops:
  7.2 6.7 copy-start.24
  7.2 710.8 %all-gather.3.cloned.1.call-start = ((), (), s32[]{:S(2)}) async-start(), calls=%async_computation | async-start | bytes 14155776 | tf_op jit(solution)/shard_map/all_gather | solution.py:505
  10.3 55.6 %copy-start.27 = (f32[1,4,2,128]{3,1,2,0:T(4,128)}, f32[1,4,2,128]{3,1,2,0:T(4,128)S(1)}, u32[]{:S(2)}) copy-start(f32[1,4,2,128]{3,1,2,0:T(4,128)S(1)} %copy.77) | copy-start | bytes 12292
  13.8 52.1 %copy-start.29 = (f32[1,4,2,128]{3,1,2,0:T(4,128)}, f32[1,4,2,128]{3,1,2,0:T(4,128)S(1)}, u32[]{:S(2)}) copy-start(f32[1,4,2,128]{3,1,2,0:T(4,128)S(1)} %copy.78) | copy-start | bytes 12292
  13.8 52.1 %copy-start.25 = (f32[1536]{0:T(1024)}, f32[1536]{0:T(1024)S(1)}, u32[]{:S(2)}) copy-start(f32[1536]{0:T(1024)S(1)} %convert_element_type.182) | copy-start | bytes 18436
  62.5 7.0 copy-start.2
  94.6 12.4 %copy-start.18 = (bf16[8,1,96,2,512]{4,3,2,1,0:T(2,128)(2,1)}, bf16[8,1,96,2,512]{4,3,2,1,0:T(2,128)(2,1)S(1)}, u32[]{:S(2)}) copy-start(bf16[8,1,96,2,512]{4,3,2,1,0:T(2,128)(2,1)S(1)} %get-tuple-element.33) | copy-start | bytes 4718596
  94.6 12.4 %copy-start.20 = (bf16[8,1,96,2,512]{4,3,2,1,0:T(2,128)(2,1)}, bf16[8,1,96,2,512]{4,3,2,1,0:T(2,128)(2,1)S(1)}, u32[]{:S(2)}) copy-start(bf16[8,1,96,2,512]{4,3,2,1,0:T(2,128)(2,1)S(1)} %get-tuple-element.34) | copy-start | bytes 4718596
  107.0 6.8 copy-start.21
  122.2 118.5 %copy-start.13 = (bf16[1024,1536]{1,0:T(8,128)(2,1)}, bf16[1024,1536]{1,0:T(8,128)(2,1)S(1)}, u32[]{:S(2)}) copy-start(bf16[1024,1536]{1,0:T(8,128)(2,1)S(1)} %convolution_convert_fusion.6) | copy-start | bytes 9437188
  122.2 118.5 %collective-permute-start = (bf16[1024,1536]{1,0:T(8,128)(2,1)S(1)}, bf16[1024,1536]{1,0:T(8,128)(2,1)}, u32[]{:S(2)}, u32[]{:S(2)}) collective-permute-start(bf16[1024,1536]{1,0:T(8,128)(2,1)S(1)} %convolution_convert_fusion.6), channel_id=1, source_target_pairs={{0,1},{1,0},{2,3},{3,2},{4,5},{5,4},{6,7},{7,6},{8,9},{9,8},{10,11... | collective-permute-start | bytes 9437192 | tf_op jit(solution)/shard_map/ppermute | solution.py:49
  238.4 9.6 %slice-start.3 = ((s8[9437184]{0:T(1024)(128)(4,1)}), s8[4194304]{0:T(1024)(128)(4,1)S(1)}, s32[]{:S(2)}) async-start(s8[9437184]{0:T(1024)(128)(4,1)} %bitcast.187), calls=%async_computation.5 | async-start | bytes 8388608
  240.7 20.5 %copy-start.4 = (bf16[2,512,1536]{2,1,0:T(8,128)(2,1)}, bf16[2,512,1536]{2,1,0:T(8,128)(2,1)S(1)}, u32[]{:S(2)}) copy-start(bf16[2,512,1536]{2,1,0:T(8,128)(2,1)S(1)} %constant_dynamic-slice_fusion.1) | copy-start | bytes 9437188
  240.7 7.3 slice-start.4
  240.7 7.3 slice-start.5
  284.2 16.2 %copy-start.37 = (f32[3072,1024]{1,0:T(8,128)S(1)}, f32[3072,1024]{1,0:T(8,128)}, u32[]{:S(2)}) copy-start(f32[3072,1024]{1,0:T(8,128)} %fusion.128) | copy-start | bytes 37748740
  300.3 16.6 %collective-permute-start.2 = (bf16[1024,1536]{1,0:T(8,128)(2,1)}, bf16[1024,1536]{1,0:T(8,128)(2,1)}, u32[]{:S(2)}, u32[]{:S(2)}) collective-permute-start(bf16[1024,1536]{1,0:T(8,128)(2,1)} %convolution_convert_fusion.3), channel_id=1, source_target_pairs={{0,1},{1,0},{2,3},{3,2},{4,5},{5,4},{6,7},{7,6},{8,9},{9,8},{10,11... | collective-permute-start | bytes 9437192 | tf_op jit(solution)/shard_map/ppermute | solution.py:49
  316.4 6.7 collective-permute-start.1
  331.3 386.8 %all-gather.5.cloned.1.call-start = ((), (), s32[]{:S(2)}) async-start(), calls=%async_computation.1 | async-start | bytes 14155776 | tf_op jit(solution)/shard_map/all_gather | solution.py:505
  372.3 6.7 copy-start.19
  372.3 6.7 copy-start.36
  392.4 22.2 %slice-start = ((s8[12582912]{0:T(1024)(128)(4,1)}), s8[4194304]{0:T(1024)(128)(4,1)S(1)}, s32[]{:S(2)}) async-start(s8[12582912]{0:T(1024)(128)(4,1)} %bitcast.143), calls=%async_computation.2 | async-start | bytes 8388608
  398.6 16.1 %slice-start.1 = ((s8[12582912]{0:T(1024)(128)(4,1)}), s8[4194304]{0:T(1024)(128)(4,1)S(1)}, s32[]{:S(2)}) async-start(s8[12582912]{0:T(1024)(128)(4,1)} %bitcast.143), calls=%async_computation.3 | async-start | bytes 8388608
  398.6 16.1 %slice-start.2 = ((s8[12582912]{0:T(1024)(128)(4,1)}), s8[4194304]{0:T(1024)(128)(4,1)S(1)}, s32[]{:S(2)}) async-start(s8[12582912]{0:T(1024)(128)(4,1)} %bitcast.143), calls=%async_computation.4 | async-start | bytes 8388608
  398.6 16.1 %copy-start.26 = (f32[1536]{0:T(1024)S(1)}, f32[1536]{0:T(1024)}, u32[]{:S(2)}) copy-start(f32[1536]{0:T(1024)} %copy-done.25) | copy-start | bytes 18436
  398.6 16.1 %copy-start.28 = (f32[1,4,2,128]{3,1,2,0:T(4,128)S(1)}, f32[1,4,2,128]{3,1,2,0:T(4,128)}, u32[]{:S(2)}) copy-start(f32[1,4,2,128]{3,1,2,0:T(4,128)} %copy-done.27) | copy-start | bytes 12292
  398.6 16.1 %copy-start.30 = (f32[1,4,2,128]{3,1,2,0:T(4,128)S(1)}, f32[1,4,2,128]{3,1,2,0:T(4,128)}, u32[]{:S(2)}) copy-start(f32[1,4,2,128]{3,1,2,0:T(4,128)} %copy-done.29) | copy-start | bytes 12292
  408.9 9.8 %copy-start.8 = (bf16[1024,1536]{1,0:T(8,128)(2,1)S(1)}, bf16[1024,1536]{1,0:T(8,128)(2,1)}, u32[]{:S(2)}) copy-start(bf16[1024,1536]{1,0:T(8,128)(2,1)} %get-tuple-element.35) | copy-start | bytes 9437188
  408.9 5.7 collective-permute-start.3
  427.6 15.3 %copy-start.6 = (bf16[2,512,1536]{2,1,0:T(8,128)(2,1)S(1)}, bf16[2,512,1536]{2,1,0:T(8,128)(2,1)}, u32[]{:S(2)}) copy-start(bf16[2,512,1536]{2,1,0:T(8,128)(2,1)} %copy-done.4) | copy-start | bytes 9437188
  459.3 155.2 %copy-start.9 = (bf16[1024,1536]{1,0:T(8,128)(2,1)S(1)}, bf16[1024,1536]{1,0:T(8,128)(2,1)}, u32[]{:S(2)}) copy-start(bf16[1024,1536]{1,0:T(8,128)(2,1)} %get-tuple-element.35) | copy-start | bytes 9437188
  718.1 13.0 %copy-start.3 = (bf16[8,512,1536]{2,1,0:T(8,128)(2,1)S(1)}, bf16[8,512,1536]{2,1,0:T(8,128)(2,1)}, u32[]{:S(2)}) copy-start(bf16[8,512,1536]{2,1,0:T(8,128)(2,1)} %all-gather.5.cloned.1.call-done) | copy-start | bytes 37748740
  (18 other events, 76.4 us)
Sparse Core Ops, SparseCore 0:
  331.4 64.5 all-gather.2
  423.1 116.6 all-gather.4

commit v2 on v1

--- a/solution.py
+++ b/solution.py
@@ -1,3 +1,5 @@
+import functools
+
 import jax
 import jax.numpy as jnp
 from jax import lax
@@ -114,6 +116,73 @@
         copy.wait_recv()
 
 
+SEQ = 512
+BLOCK = 256
+HEAD = 96
+SCALE = HEAD ** -0.5
+
+
+def head_slice(ref, index, kind, lo, hi, kinds=3):
+    head, row = lax.div(index, 2), lax.rem(index, 2)
+    start = pl.multiple_of((head * kinds + kind) * HEAD, 32)
+    return ref.at[pl.ds(start, HEAD), pl.ds(pl.multiple_of(row * SEQ + lo, 128), hi - lo)]
+
+
+def dot_cols(lhs, rhs):
+    return lax.dot_general(lhs, rhs, (((0,), (0,)), ((), ())), preferred_element_type=F32)
+
+
+def dot_rows(lhs, rhs):
+    return lax.dot_general(lhs, rhs, (((1,), (1,)), ((), ())), preferred_element_type=F32)
+
+
+def probs_block(k_t, q_t, seg, seg_col, row, first):
+    keys = first + BLOCK
+    scores = dot_cols(k_t, q_t) * SCALE
+    query = lax.broadcasted_iota(jnp.int32, (keys, BLOCK), 1) + first
+    key = lax.broadcasted_iota(jnp.int32, (keys, BLOCK), 0)
+    same = seg[row, :, first : first + BLOCK] == seg_col[row, :keys, :]
+    scores = jnp.where((query >= key) & same, scores, NEG_LARGE)
+    weights = jnp.exp(scores - jnp.max(scores, axis=0, keepdims=True))
+    return weights * (1.0 / jnp.sum(weights, axis=0, keepdims=True))
+
+
+def attention_forward(qkv, seg, seg_col, out, start, stop):
+    @pl.loop(start, stop)
+    def _(index):
+        row = lax.rem(index, 2)
+        for first in range(0, SEQ, BLOCK):
+            keys = first + BLOCK
+            probs = probs_block(
+                head_slice(qkv, index, 1, 0, keys)[...], head_slice(qkv, index, 0, first, keys)[...], seg, seg_col, row, first)
+            value = lax.dot_general(
+                head_slice(qkv, index, 2, 0, keys)[...], probs.astype(BF16), (((1,), (0,)), ((), ())), preferred_element_type=F32)
+            head_slice(out, index, 0, first, keys, kinds=1)[...] = value.astype(BF16)
+
+
+def attention_backward(qkv, seg, seg_col, grad, out, start, stop):
+    @pl.loop(start, stop)
+    def _(index):
+        row = lax.rem(index, 2)
+        grads = []
+        for first in range(0, SEQ, BLOCK):
+            keys = first + BLOCK
+            q_t = head_slice(qkv, index, 0, first, keys)[...]
+            k_t = head_slice(qkv, index, 1, 0, keys)[...]
+            g_t = head_slice(grad, index, 0, first, keys, kinds=1)[...]
+            probs = probs_block(k_t, q_t, seg, seg_col, row, first)
+            grad_probs = dot_cols(head_slice(qkv, index, 2, 0, keys)[...], g_t)
+            grad_scores = probs * (grad_probs - jnp.sum(grad_probs * probs, axis=0, keepdims=True))
+            low = (grad_scores * SCALE).astype(BF16)
+            grad_q = lax.dot_general(k_t, low, (((1,), (0,)), ((), ())), preferred_element_type=F32)
+            head_slice(out, index, 0, first, keys)[...] = grad_q.astype(BF16)
+            grads.append((dot_rows(q_t, low), dot_rows(g_t, probs.astype(BF16))))
+        for i in range(2):
+            whole = grads[1][i]
+            head_slice(out, index, 1 + i, 0, BLOCK)[...] = (grads[0][i] + whole[:, :BLOCK]).astype(BF16)
+            head_slice(out, index, 1 + i, BLOCK, SEQ)[...] = whole[:, BLOCK:].astype(BF16)
+
+
 class WeightGather:
     COPIES = 21
 
@@ -131,6 +200,8 @@
             cols = pl.ds(part * THIRD, THIRD)
             self.near.append(self.sender.ring(
                 "x", lambda step: self.own.at[z, y, :, cols], lambda step: self.out.at[RING - step, z, y, :, cols]))
+
+    def start_whole(self):
         cols = pl.ds(2 * THIRD, THIRD)
         self.whole = self.sender.ring(
             "x", lambda step: self.own.at[:, :, :, cols], lambda step: self.out.at[RING - step, :, :, :, cols])
@@ -156,9 +227,14 @@
         wait_all(self.whole)
 
 
-def gather_kernel(count, *refs):
-    owns, outs = refs[:count], refs[count : 2 * count]
-    stage, send_sems, recv_sems, local_sems = refs[2 * count :]
+def gather_kernel(count, attention, *refs):
+    owns, refs = refs[:count], refs[count:]
+    work = None
+    if attention:
+        work = functools.partial(attention_forward, refs[0], refs[1], refs[2], refs[count + 3])
+        refs = refs[3 : count + 3] + refs[count + 4 :]
+    outs = refs[:count]
+    stage, send_sems, recv_sems, local_sems = refs[count:]
     place = Place()
     sender = Sender(place, send_sems, recv_sems)
     gathers = [WeightGather(place, sender, own, out) for own, out in zip(owns, outs)]
@@ -168,16 +244,24 @@
     place.enter()
     for gather in gathers:
         gather.start()
+    for gather in gathers:
+        gather.start_whole()
     stores = []
     for i in range(count):
         loads[i].wait()
         store = pltpu.make_async_copy(stage.at[i], outs[i].at[0], local_sems.at[count + i])
         store.start()
         stores.append(store)
+    if work is not None:
+        work(0, 4)
     for gather in gathers:
         gather.second()
+    if work is not None:
+        work(4, 10)
     for gather in gathers:
         gather.third()
+    if work is not None:
+        work(10, 16)
     for gather in gathers:
         gather.finish()
     for store in stores:
@@ -185,23 +269,31 @@
     sender.drain()
 
 
-def gather_weights(owns, collective_id):
+def gather_weights(owns, collective_id, attention=()):
     count = len(owns)
     copies = WeightGather.COPIES * count
+    any_spec = pl.BlockSpec(memory_space=pl.ANY)
+    vmem_spec = pl.BlockSpec(memory_space=pltpu.VMEM)
+    out_shape = [jax.ShapeDtypeStruct((RING,) + own.shape, own.dtype) for own in owns]
+    out_specs = [any_spec] * count
+    if attention:
+        rows, tokens = attention[0].shape
+        out_shape.append(jax.ShapeDtypeStruct((rows // 3, tokens), BF16))
+        out_specs.append(vmem_spec)
     return pl.pallas_call(
-        lambda *refs: gather_kernel(count, *refs),
-        out_shape=[jax.ShapeDtypeStruct((RING,) + own.shape, own.dtype) for own in owns],
-        in_specs=[pl.BlockSpec(memory_space=pl.ANY)] * count,
-        out_specs=[pl.BlockSpec(memory_space=pl.ANY)] * count,
+        lambda *refs: gather_kernel(count, bool(attention), *refs),
+        out_shape=out_shape,
+        in_specs=[any_spec] * count + [vmem_spec] * len(attention),
+        out_specs=out_specs,
         scratch_shapes=[
             pltpu.VMEM((count,) + owns[0].shape, owns[0].dtype),
             pltpu.SemaphoreType.DMA((copies,)),
             pltpu.SemaphoreType.DMA((copies,)),
             pltpu.SemaphoreType.DMA((2 * count,)),
         ],
-        compiler_params=pltpu.CompilerParams(collective_id=collective_id, has_side_effects=True),
+        compiler_params=pltpu.CompilerParams(collective_id=collective_id, has_side_effects=True, vmem_limit_bytes=(40 if attention else 16) << 20),
         name=f"gather_weights_{collective_id}",
-    )(*owns)
+    )(*owns, *attention)
 
 
 ORDERS = (("z", "y", "x", 1), ("y", "x", "z", 0), ("x", "z", "y", 0))
@@ -317,10 +409,14 @@
     return finish
 
 
-def scatter_kernel(count, with_gains, *refs):
+def scatter_kernel(count, with_gains, attention, *refs):
     grads, refs = refs[:count], refs[count:]
     if with_gains:
         gain_in, refs = refs[0], refs[1:]
+    work = None
+    if attention:
+        work = functools.partial(attention_backward, *refs[:4], refs[4 + count])
+        refs = refs[4 : 4 + count] + refs[5 + count :]
     outs, refs = refs[:count], refs[count:]
     if with_gains:
         gain_out, refs = refs[0], refs[1:]
@@ -336,23 +432,27 @@
         gains, gain_bufs = refs[8:]
         gains[0] = gain_in[...]
         gain_finish = gain_step(place, sender, gains, gain_bufs, 0, "z")
-    for work in works:
-        work.start()
-    for work in works:
+    for item in works:
+        item.start()
+    if work is not None:
+        work(0, 14)
+    for i, item in enumerate(works):
         for part in range(3):
-            work.second(part)
+            item.second(part)
+        if work is not None and i == 0:
+            work(14, 16)
     if with_gains:
         gain_finish()
         gain_finish = gain_step(place, sender, gains, gain_bufs, 1, "y")
-    for work in works:
+    for item in works:
         for part in range(3):
-            work.third(part)
+            item.third(part)
     if with_gains:
         gain_finish()
         gain_finish = gain_step(place, sender, gains, gain_bufs, 2, "x")
-    for work, plane in zip(works, planes):
+    for item, plane in zip(works, planes):
         for part in range(3):
-            work.finish(part)
+            item.finish(part)
         plane.start()
     if with_gains:
         gain_finish()
@@ -364,7 +464,7 @@
     sender.drain()
 
 
-def scatter_grads(grads, gains, collective_id):
+def scatter_grads(grads, gains, collective_id, attention=()):
     count = len(grads)
     with_gains = gains is not None
     copies = (GradScatter.COPIES + PlaneGather.COPIES) * count + 9 * with_gains
@@ -383,36 +483,25 @@
     ]
     out_shape = [jax.ShapeDtypeStruct(grad.shape[1:], BF16) for grad in grads]
     operands = list(grads)
+    extra_outs = 0
     if with_gains:
         scratch += [pltpu.VMEM((4,) + gains.shape, F32), pltpu.VMEM((3, 3) + gains.shape, F32)]
         out_shape.append(jax.ShapeDtypeStruct(gains.shape, F32))
         operands.append(gains)
+        extra_outs = 1
+    if attention:
+        out_shape.append(jax.ShapeDtypeStruct(attention[0].shape, BF16))
+        operands += attention
+        extra_outs = 1
     return pl.pallas_call(
-        lambda *refs: scatter_kernel(count, with_gains, *refs),
+        lambda *refs: scatter_kernel(count, with_gains, bool(attention), *refs),
         out_shape=out_shape,
-        in_specs=[any_spec] * count + [vmem_spec] * with_gains,
-        out_specs=[any_spec] * count + [vmem_spec] * with_gains,
+        in_specs=[any_spec] * count + [vmem_spec] * (len(operands) - count),
+        out_specs=[any_spec] * count + [vmem_spec] * extra_outs,
         scratch_shapes=scratch,
-        compiler_params=pltpu.CompilerParams(collective_id=collective_id, has_side_effects=True, vmem_limit_bytes=56 << 20),
+        compiler_params=pltpu.CompilerParams(collective_id=collective_id, has_side_effects=True, vmem_limit_bytes=60 << 20),
         name=f"scatter_grads_{collective_id}",
     )(*operands)
-
-
-def attention_forward(q_t, k_t, v_t, allowed, score_scale):
-    scores = jnp.einsum("ndbq,ndbk->bnqk", q_t, k_t, preferred_element_type=F32) * score_scale
-    attn_probs = jax.nn.softmax(jnp.where(allowed, scores, NEG_LARGE), axis=-1)
-    attn_out = jnp.einsum("bnqk,ndbk->ndbq", attn_probs.astype(BF16), v_t, preferred_element_type=F32)
-    return attn_out.astype(BF16), attn_probs
-
-
-def attention_backward(grad_out, q_t, k_t, v_t, attn_probs, score_scale):
-    grad_v = jnp.einsum("bnqk,ndbq->ndbk", attn_probs.astype(BF16), grad_out, preferred_element_type=F32)
-    grad_probs = jnp.einsum("ndbq,ndbk->bnqk", grad_out, v_t, preferred_element_type=F32)
-    grad_scores = attn_probs * (grad_probs - jnp.sum(grad_probs * attn_probs, axis=-1, keepdims=True))
-    grad_low = (grad_scores * score_scale).astype(BF16)
-    grad_q = jnp.einsum("bnqk,ndbk->ndbq", grad_low, k_t, preferred_element_type=F32)
-    grad_k = jnp.einsum("bnqk,ndbq->ndbk", grad_low, q_t, preferred_element_type=F32)
-    return grad_q, grad_k, grad_v
 
 
 def solution(mesh):
@@ -422,7 +511,6 @@
     def local_step(x_in, seg_ids, gain_one, gain_two, w_qkv, w_out, w_up, w_down, grad_y):
         batch_loc, seq_len, hidden = x_in.shape
         heads_loc, head_dim = w_out.shape[:2]
-        score_scale = head_dim ** -0.5
         rows_loc = batch_loc // RING
         tokens = rows_loc * seq_len
         shard_rows = w_up.shape[1]
@@ -439,24 +527,20 @@
         own_up = grid_of(w_up.T)
         own_down = grid_of(w_down)
         (w_att,) = gather_weights([own_att], 1)
-        up_t, down = gather_weights([own_up, own_down], 2)
         w_att = w_att.reshape(RING, shard_rows, hidden)
-        up_t = up_t.reshape(RING * shard_rows, hidden)
-        down = down.reshape(RING * shard_rows, hidden)
         w_qkv_t = w_att[:, :qkv_cols]
         w_out_all = w_att[:, qkv_cols:].reshape(RING * heads_loc * head_dim, hidden)
 
         x_rows = own_rows(x_in).reshape(tokens, hidden)
         seg_rows = own_rows(seg_ids)
         grad_rows = own_rows(grad_y).reshape(tokens, hidden)
-        positions = jnp.arange(seq_len)
-        allowed = (positions[:, None] >= positions[None, :])[None, None] & (seg_rows[:, None, :, None] == seg_rows[:, None, None, :])
+        seg_row, seg_col = seg_rows[:, None, :], seg_rows[:, :, None]
         normed_a, hat_a, inv_a = norm_forward(x_rows, gain_one)
         qkv_t = dot_nt(w_qkv_t, normed_a).astype(BF16)
-        qkv_t = qkv_t.reshape(RING * heads_loc, 3, head_dim, rows_loc, seq_len)
-        q_t, k_t, v_t = qkv_t[:, 0], qkv_t[:, 1], qkv_t[:, 2]
-        attn_t, attn_probs = attention_forward(q_t, k_t, v_t, allowed, score_scale)
-        attn_flat = attn_t.reshape(RING * heads_loc * head_dim, tokens)
+        qkv_t = qkv_t.reshape(RING * qkv_cols, tokens)
+        up_t, down, attn_flat = gather_weights([own_up, own_down], 2, (qkv_t, seg_row, seg_col))
+        up_t = up_t.reshape(RING * shard_rows, hidden)
+        down = down.reshape(RING * shard_rows, hidden)
 
         def pair_sum(part):
             return part.astype(F32) + core_swap(part).astype(F32)
@@ -478,16 +562,14 @@
         grid_shape = (RING, RING, RING, PIECE, hidden)
         grad_down_w = dot_nn(hidden_act, grad_rows).astype(BF16).reshape(grid_shape)
         grad_up_w = dot_nn(grad_pre, normed_b).astype(BF16).reshape(grid_shape)
-        grad_up_own, grad_down_own = scatter_grads([grad_up_w, grad_down_w], None, 3)
-
         part_b = dot_tn(grad_pre, up_t).astype(BF16)
         grad_norm_b = pair_sum(part_b).astype(BF16)
         back_b, gain_grad_two = norm_backward(grad_norm_b, hat_b, inv_b, gain_two)
         grad_x_one = (grad_rows.astype(F32) + back_b).astype(BF16)
         grad_out_w = dot_nn(attn_flat, grad_x_one).astype(BF16)
         grad_attn = dot_nt(w_out_all, grad_x_one).astype(BF16)
-        grad_q, grad_k, grad_v = attention_backward(grad_attn.reshape(attn_t.shape), q_t, k_t, v_t, attn_probs, score_scale)
-        grad_qkv_t = jnp.stack([grad_q, grad_k, grad_v], axis=1).astype(BF16).reshape(RING * qkv_cols, tokens)
+        grad_up_own, grad_down_own, grad_qkv_t = scatter_grads(
+            [grad_up_w, grad_down_w], None, 3, (qkv_t, seg_row, seg_col, grad_attn))
         part_a = dot_tn(grad_qkv_t, w_qkv_t.reshape(RING * qkv_cols, hidden)).astype(BF16)
         grad_norm_a = pair_sum(part_a).astype(BF16)
         back_a, gain_grad_one = norm_backward(grad_norm_a, hat_a, inv_a, gain_one)

time: 749 us -> 656 us (0.88)
  local copies, waits for them, and re-layouts: 88.5 us -> 45.8 us
  matrix products: 188 us -> 154 us
  other arithmetic: 59.2 us -> 43.5 us
    sub x2 -> x0, matrix products: 29.9 us -> none  [the longest x1 19.2 us: attention_backward(): grad_probs - jnp.sum(grad_probs * attn_probs, axis=-1, keepdims=True)]
    dot_general x4 -> x0, matrix products: 17.2 us -> none  [the longest x1 7.66 us: attention_backward(): jnp.einsum('bnqk,ndbq->ndbk', attn_probs.astype(BF16), grad_out, preferre...]
    reshape x2 -> x0, local copies, waits for them, and re-layouts: 12.7 us -> none  [the longest x1 8.82 us: local_step(): qkv_t = qkv_t.reshape(RING * heads_loc, 3, head_dim, rows_loc, seq_len)]
    dot_general x4, matrix products: 45.5 us -> 56.6 us  [dot_tn(): lax.dot_general(lhs, rhs, (((0,), (0,)), ((), ())), preferred_element_typ...]
    another operation x1 -> x0, local copies, waits for them, and re-layouts: 9.33 us -> none  [local_step(): jnp.stack([grad_q, grad_k, grad_v], axis=1).astype(BF16)]
    unnamed x95 -> x63, local copies, waits for them, and re-layouts: 28.7 us -> 20.2 us
  transfers between devices with their start and end apart: 6 -> 6, of which waited for: 1 -> 2; matrix products, arithmetic and copies ran while one was open for 24% -> 18% of each run, Pallas kernels for 46% -> 39%
where the time goes in v2:
time: 656 us; the launch traced here: 652 us
  Pallas kernels  384 us (59%)
  matrix products  154 us (23%)
  local copies, waits for them, and re-layouts  45.8 us (7%)
  other arithmetic  43.5 us (7%)
  between operations  14.8 us (2%)
  waiting for transfers between devices  9.2 us (1%)
    pallas_call x2, Pallas kernels, scatter_grads(): pl.pallas_call(lambda *refs: scatter_kernel(count, with_gains, bool(atten...  257 us
    pallas_call x2, Pallas kernels, gather_weights(): pl.pallas_call(lambda *refs: gather_kernel(count, bool(attention), *refs)...  127 us
    dot_general x4, matrix products, dot_tn(): lax.dot_general(lhs, rhs, (((0,), (0,)), ((), ())), preferred_element_typ...  56.6 us
    dot_general x4, matrix products, dot_nt(): lax.dot_general(lhs, rhs, (((lhs.ndim - 1,), (rhs.ndim - 1,)), ((), ())),...  50.2 us
    dot_general x4, matrix products, dot_nn(): lax.dot_general(lhs, rhs, (((lhs.ndim - 1,), (0,)), ((), ())), preferred_...  47.2 us
    unnamed x63, local copies, waits for them, and re-layouts  20.2 us
  transfers between devices with their start and end apart: 6, of which 2 were waited for; matrix products, arithmetic and copies ran while one was open for 18% of the time, Pallas kernels for 39%

profile of v2, /device:TPU:0, one launch (start us, length us, event | category | flops | bytes accessed | tf_op | source)
XLA Modules:
  0.0 652.5 jit_solution(10193170427175452962)
XLA Ops:
  10.3 2.9 fusion.36
  13.5 3.0 copy.23
  18.2 47.2 %gather_weights_1.1 = bf16[4,4,4,48,1536]{4,3,2,1,0:T(8,128)(2,1)S(1)} custom-call(bf16[4,4,48,1536]{3,2,1,0:T(8,128)(2,1)S(1)} %bitcast.85), custom_call_target="tpu_custom_call" | custom-call | tf_op jit(solution)/shard_map/gather_weights_1/pallas_call | solution.py:283
  67.1 5.2 fusion.40
  72.4 7.8 %fusion.44 = bf16[4,576,1024]{2,1,0:T(8,128)(2,1)S(1)} fusion(bf16[1024,1536]{1,0:T(8,128)(2,1)S(1)} %fusion.40, bf16[4,768,1536]{2,1,0:T(8,128)(2,1)S(1)} %bitcast.80), kind=kOutput, calls=%fused_computation.73 | convolution fusion | flops 7250116608 | bytes 14942208 | tf_op jit(solution)/shard_map/dot_general | solution.py:39
  80.2 80.2 %gather_weights_2.1 = (bf16[4,4,4,48,1536]{4,3,2,1,0:T(8,128)(2,1)}, bf16[4,4,4,48,1536]{4,3,2,1,0:T(8,128)(2,1)}, bf16[768,1024]{1,0:T(8,128)(2,1)S(1)}) custom-call(bf16[4,4,48,1536]{3,2,1,0:T(8,128)(2,1)S(1)} %bitcast.84, bf16[4,4,48,1536]{3,2,1,0:T(8,128)(2,1)S(1)} %bitcast.86, bf16[2304,1024]{1,0:T(8,128)(2,1)S(1)} %bitcast.82, ...), custom_call_target="tpu_custom_call" | custom-call | tf_op jit(solution)/shard_map/gather_weights_2/pallas_call | solution.py:283
  160.5 2.9 convolution_convert_fusion.6
  166.0 3.5 collective-permute-done
  169.5 3.3 convert_reduce_fusion
  173.7 15.6 %fusion.50 = f32[3072,1024]{1,0:T(8,128)} fusion(bf16[3072,1536]{1,0:T(8,128)(2,1)} %bitcast.115, bf16[1024,1536]{1,0:T(8,128)(2,1)S(1)} %get-tuple-element.35, f32[1536]{0:T(1024)S(1)} %convert_element_type.158, f32[1024]{0:T(1024)S(1)} %add_rsqrt_fusion, f32[1024]{0:T(1024)S(1)} %broadcast_multiply_fusion.4), kind=kOutput, calls=%fused_computation.93 | convolution fusion | flops 9671540736 | bytes 25180160 | tf_op jit(solution)/shard_map/dot_general | solution.py:39
  189.4 23.1 %fusion.2 = bf16[3072,1024]{1,0:T(8,128)(2,1)} fusion(f32[3072,1024]{1,0:T(8,128)} %fusion.50, bf16[3072,1536]{1,0:T(8,128)(2,1)} %bitcast.113, bf16[1024,1536]{1,0:T(8,128)(2,1)S(1)} %bitcast.88), kind=kOutput, calls=%fused_computation.6 | convolution fusion | flops 9732882432 | bytes 31457280 | tf_op jit(solution)/shard_map/dot_general | solution.py:39
  212.4 26.3 %convolution_convert_fusion.3 = bf16[1024,1536]{1,0:T(8,128)(2,1)} fusion(bf16[3072,1024]{1,0:T(8,128)(2,1)} %fusion.2, bf16[3072,1536]{1,0:T(8,128)(2,1)} %bitcast.116), kind=kOutput, calls=%fused_computation.66 | convolution fusion | flops 9665249280 | bytes 18874368 | tf_op jit(solution)/shard_map/dot_general | solution.py:43
  238.9 16.0 %convolution_convert_fusion.4 = bf16[1024,1536]{1,0:T(8,128)(2,1)} fusion(bf16[3072,1536]{1,0:T(8,128)(2,1)} %bitcast.114, f32[3072,1024]{1,0:T(8,128)S(1)} %copy-done.28), kind=kOutput, calls=%fused_computation.67 | convolution fusion | flops 9693560832 | bytes 25165824 | tf_op jit(solution)/shard_map/dot_general | solution.py:43
  255.2 5.6 fusion.27
  260.9 6.9 %fusion.24 = (bf16[1024,1536]{1,0:T(8,128)(2,1)}, bf16[1024,1536]{1,0:T(8,128)(2,1)S(1)}) fusion(bf16[1024,1536]{1,0:T(8,128)(2,1)S(1)} %get-tuple-element.35, bf16[1024,1536]{1,0:T(8,128)(2,1)S(1)} %get-tuple-element.33, f32[1024]{0:T(1024)S(1)} %get-tuple-element.40, f32[1024]{0:T(1024)S(1)} %get-tuple-element.41, f32[1536]{0:T(1024)S(1)} %convert_element_type.158, ...), kind=kLoop, calls=%fused_computation.40 | loop fusion | flops 29884416 | bytes 22042624 | tf_op jit(solution)/shard_map/convert_element_type | solution.py:568
  269.2 6.3 slice.31
  275.5 15.7 %convolution_convert_fusion.2 = bf16[3072,1536]{1,0:T(8,128)(2,1)} fusion(bf16[3072,1024]{1,0:T(8,128)(2,1)} %fusion.2, bf16[1024,1536]{1,0:T(8,128)(2,1)S(1)} %get-tuple-element.35, f32[1536]{0:T(1024)S(1)} %convert_element_type.158, f32[1024]{0:T(1024)S(1)} %add_rsqrt_fusion, f32[1024]{0:T(1024)S(1)} %broadcast_multiply_fusion.4), kind=kOutput, calls=%fused_computation.17 | convolution fusion | flops 9676259328 | bytes 18888704 | tf_op jit(solution)/shard_map/dot_general | solution.py:47
  291.3 16.4 %convolution_convert_fusion.1 = bf16[3072,1536]{1,0:T(8,128)(2,1)} fusion(bf16[1024,1536]{1,0:T(8,128)(2,1)S(1)} %bitcast.89, f32[3072,1024]{1,0:T(8,128)} %fusion.50), kind=kOutput, calls=%fused_computation.16 | convolution fusion | flops 9696706560 | bytes 25165824 | tf_op jit(solution)/shard_map/dot_general | solution.py:47
  307.7 3.7 convolution_convert_fusion.8.refs_5_
  311.5 147.8 %scatter_grads_3.1 = (bf16[4,4,48,1536]{3,2,1,0:T(8,128)(2,1)}, bf16[4,4,48,1536]{3,2,1,0:T(8,128)(2,1)}, bf16[2304,1024]{1,0:T(8,128)(2,1)}) custom-call(bf16[4,4,4,48,1536]{4,3,2,1,0:T(8,128)(2,1)} %bitcast.90, bf16[4,4,4,48,1536]{4,3,2,1,0:T(8,128)(2,1)} %bitcast.91, bf16[2304,1024]{1,0:T(8,128)(2,1)} %bitcast.83, s32[2,1,512]{2,1,0:T(1,128)} %copy-done.6, ...), custom_call_target="tpu_custom_call" | custom-call | tf_op jit(solution)/shard_map/scatter_grads_3/pallas_call | solution.py:496
  459.3 11.3 %convolution_convert_fusion.5 = bf16[1024,1536]{1,0:T(8,128)(2,1)S(1)} fusion(bf16[2304,1024]{1,0:T(8,128)(2,1)} %get-tuple-element.19, bf16[2304,1536]{1,0:T(8,128)(2,1)} %bitcast.92), kind=kOutput, calls=%fused_computation.68 | convolution fusion | flops 7249330176 | bytes 14942208 | tf_op jit(solution)/shard_map/dot_general | solution.py:43
  470.8 5.6 collective-permute-done.3
  476.4 5.1 fusion.33
  481.6 4.0 fusion.31
  487.0 4.3 copy.26
  491.3 4.8 convolution_convert_fusion.7
  496.1 10.2 %convolution_convert_fusion = bf16[2304,1536]{1,0:T(8,128)(2,1)S(1)} fusion(bf16[2304,1024]{1,0:T(8,128)(2,1)} %get-tuple-element.19, bf16[1024,1536]{1,0:T(8,128)(2,1)S(1)} %copy-done.15), kind=kOutput, calls=%fused_computation.15 | convolution fusion | flops 7251296256 | bytes 14942208 | tf_op jit(solution)/shard_map/dot_general | solution.py:47
  506.3 3.9 pad_maximum_fusion
  511.0 108.9 %scatter_grads_4.1 = (bf16[4,4,48,1536]{3,2,1,0:T(8,128)(2,1)}, f32[8,1536]{1,0:T(8,128)}) custom-call(bf16[4,4,4,48,1536]{4,3,2,1,0:T(8,128)(2,1)} %bitcast.87, f32[8,1536]{1,0:T(8,128)} %maximum_maximum_fusion.refs_1_), custom_call_target="tpu_custom_call" | custom-call | tf_op jit(solution)/shard_map/scatter_grads_4/pallas_call | solution.py:496
  621.8 2.8 slice.28
  626.0 11.0 %copy.32 = bf16[8,512,1536]{2,1,0:T(8,128)(2,1)} copy(bf16[8,512,1536]{2,1,0:T(8,128)(2,1)} %all-gather.3.cloned.1.call-done) | data formatting | bytes 25165824
  639.0 5.0 copy.33
  (101 shorter events, 20.9 us)
Async XLA Ops:
  7.2 6.0 copy-start.26
  7.2 9.4 %copy-start.19 = (bf16[2,96,1536]{2,1,0:T(8,128)(2,1)S(1)}, bf16[2,96,1536]{2,1,0:T(8,128)(2,1)}, u32[]{:S(2)}) copy-start(bf16[2,96,1536]{2,1,0:T(8,128)(2,1)} %param.14) | copy-start | bytes 1769476
  7.2 618.8 %all-gather.3.cloned.1.call-start = ((), (), s32[]{:S(2)}) async-start(), calls=%async_computation | async-start | bytes 14155776 | tf_op jit(solution)/shard_map/all_gather | solution.py:587
  7.9 72.3 %copy-start.6 = (s32[2,1,512]{2,1,0:T(1,128)}, s32[2,1,512]{2,1,0:T(1,128)S(1)}, u32[]{:S(2)}) copy-start(s32[2,1,512]{2,1,0:T(1,128)S(1)} %broadcast_in_dim.10.refs_3_) | copy-start | bytes 12292
  10.3 56.8 %copy-start.22 = (f32[1,4,2,128]{3,1,2,0:T(4,128)}, f32[1,4,2,128]{3,1,2,0:T(4,128)S(1)}, u32[]{:S(2)}) copy-start(f32[1,4,2,128]{3,1,2,0:T(4,128)S(1)} %copy.27) | copy-start | bytes 12292
  13.2 53.9 %copy-start.24 = (f32[1,4,2,128]{3,1,2,0:T(4,128)}, f32[1,4,2,128]{3,1,2,0:T(4,128)S(1)}, u32[]{:S(2)}) copy-start(f32[1,4,2,128]{3,1,2,0:T(4,128)S(1)} %copy.28) | copy-start | bytes 12292
  13.3 53.9 %copy-start.20 = (f32[1536]{0:T(1024)}, f32[1536]{0:T(1024)S(1)}, u32[]{:S(2)}) copy-start(f32[1536]{0:T(1024)S(1)} %convert_element_type.148) | copy-start | bytes 18436
  13.5 66.7 %copy-start.4 = (s32[2,512,1]{2,1,0:T(8,128)}, s32[2,512,1]{2,1,0:T(8,128)S(1)}, u32[]{:S(2)}) copy-start(s32[2,512,1]{2,1,0:T(8,128)S(1)} %copy.24.refs_4_) | copy-start | bytes 12292
  65.4 14.7 %copy-start.2 = (bf16[4,4,4,48,1536]{4,3,2,1,0:T(8,128)(2,1)}, bf16[4,4,4,48,1536]{4,3,2,1,0:T(8,128)(2,1)S(1)}, u32[]{:S(2)}) copy-start(bf16[4,4,4,48,1536]{4,3,2,1,0:T(8,128)(2,1)S(1)} %gather_weights_1.1) | copy-start | bytes 28311556
  72.4 7.8 %copy-start.14 = (bf16[1024,1536]{1,0:T(8,128)(2,1)}, bf16[1024,1536]{1,0:T(8,128)(2,1)S(1)}, u32[]{:S(2)}) copy-start(bf16[1024,1536]{1,0:T(8,128)(2,1)S(1)} %fusion.40) | copy-start | bytes 9437188
  72.4 7.9 %copy-start.5 = (bf16[768,1536]{1,0:T(8,128)(2,1)S(1)}, bf16[768,1536]{1,0:T(8,128)(2,1)}, u32[]{:S(2)}) copy-start(bf16[768,1536]{1,0:T(8,128)(2,1)} %param.16) | copy-start | bytes 7077892
  80.2 83.3 %copy-start.3 = (bf16[4,576,1024]{2,1,0:T(8,128)(2,1)}, bf16[4,576,1024]{2,1,0:T(8,128)(2,1)S(1)}, u32[]{:S(2)}) copy-start(bf16[4,576,1024]{2,1,0:T(8,128)(2,1)S(1)} %fusion.44) | copy-start | bytes 14155780
  80.2 80.3 %copy-start.16 = (bf16[4,192,1536]{2,1,0:T(8,128)(2,1)S(1)}, bf16[4,192,1536]{2,1,0:T(8,128)(2,1)}, u32[]{:S(2)}) copy-start(bf16[4,192,1536]{2,1,0:T(8,128)(2,1)} %slice.32) | copy-start | bytes 7077892
  163.5 6.0 collective-permute-start
  166.0 23.4 %copy-start.10 = (bf16[2,512,1536]{2,1,0:T(8,128)(2,1)}, bf16[2,512,1536]{2,1,0:T(8,128)(2,1)S(1)}, u32[]{:S(2)}) copy-start(bf16[2,512,1536]{2,1,0:T(8,128)(2,1)S(1)} %constant_dynamic-slice_fusion.1) | copy-start | bytes 9437188
  212.4 26.4 %copy-start.28 = (f32[3072,1024]{1,0:T(8,128)S(1)}, f32[3072,1024]{1,0:T(8,128)}, u32[]{:S(2)}) copy-start(f32[3072,1024]{1,0:T(8,128)} %fusion.50) | copy-start | bytes 37748740
  238.7 16.5 %collective-permute-start.2 = (bf16[1024,1536]{1,0:T(8,128)(2,1)}, bf16[1024,1536]{1,0:T(8,128)(2,1)}, u32[]{:S(2)}, u32[]{:S(2)}) collective-permute-start(bf16[1024,1536]{1,0:T(8,128)(2,1)} %convolution_convert_fusion.3), channel_id=1, source_target_pairs={{0,1},{1,0},{2,3},{3,2},{4,5},{5,4},{6,7},{7,6},{8,9},{9,8},{10,11... | collective-permute-start | bytes 9437192 | tf_op jit(solution)/shard_map/ppermute | solution.py:51
  254.9 6.0 collective-permute-start.1
  255.2 5.7 copy-start.11
  269.1 356.9 %all-gather.5.cloned.1.call-start = ((), (), s32[]{:S(2)}) async-start(), calls=%async_computation.1 | async-start | bytes 14155776 | tf_op jit(solution)/shard_map/all_gather | solution.py:587
  275.5 15.8 %copy-start.12 = (bf16[2,512,1536]{2,1,0:T(8,128)(2,1)S(1)}, bf16[2,512,1536]{2,1,0:T(8,128)(2,1)}, u32[]{:S(2)}) copy-start(bf16[2,512,1536]{2,1,0:T(8,128)(2,1)} %copy-done.10) | copy-start | bytes 9437188
  291.3 16.5 %copy-start.13 = (bf16[1024,1536]{1,0:T(8,128)(2,1)S(1)}, bf16[1024,1536]{1,0:T(8,128)(2,1)}, u32[]{:S(2)}) copy-start(bf16[1024,1536]{1,0:T(8,128)(2,1)} %get-tuple-element.36) | copy-start | bytes 9437188
  291.3 16.5 %copy-start.17 = (bf16[4,192,1536]{2,1,0:T(8,128)(2,1)S(1)}, bf16[4,192,1536]{2,1,0:T(8,128)(2,1)}, u32[]{:S(2)}) copy-start(bf16[4,192,1536]{2,1,0:T(8,128)(2,1)} %slice.32) | copy-start | bytes 7077892
  459.3 17.1 %copy-start.21 = (f32[1536]{0:T(1024)S(1)}, f32[1536]{0:T(1024)}, u32[]{:S(2)}) copy-start(f32[1536]{0:T(1024)} %copy-done.20) | copy-start | bytes 18436
  459.3 17.1 %copy-start.23 = (f32[1,4,2,128]{3,1,2,0:T(4,128)S(1)}, f32[1,4,2,128]{3,1,2,0:T(4,128)}, u32[]{:S(2)}) copy-start(f32[1,4,2,128]{3,1,2,0:T(4,128)} %copy-done.22) | copy-start | bytes 12292
  459.3 17.1 %copy-start.25 = (f32[1,4,2,128]{3,1,2,0:T(4,128)S(1)}, f32[1,4,2,128]{3,1,2,0:T(4,128)}, u32[]{:S(2)}) copy-start(f32[1,4,2,128]{3,1,2,0:T(4,128)} %copy-done.24) | copy-start | bytes 12292
  470.7 5.7 collective-permute-start.3
  485.6 5.6 copy-start.8
  491.3 4.8 copy-start.15
  626.0 13.0 %copy-start.9 = (bf16[8,512,1536]{2,1,0:T(8,128)(2,1)S(1)}, bf16[8,512,1536]{2,1,0:T(8,128)(2,1)}, u32[]{:S(2)}) copy-start(bf16[8,512,1536]{2,1,0:T(8,128)(2,1)} %all-gather.5.cloned.1.call-done) | copy-start | bytes 37748740
  639.0 5.0 copy-start.18
  639.0 6.4 copy-start.1
  (3 other events, 7.1 us)
Sparse Core Ops, SparseCore 0:
  269.2 91.9 all-gather.2
  487.0 110.8 all-gather.4

commit v3 on v2

--- a/solution.py
+++ b/solution.py
@@ -78,12 +78,17 @@
     def block(self, axis, step):
         return step if axis == "x" else self.ahead(axis, step)
 
-    def enter(self):
+    def sibling(self):
+        return {"tp": self.pos["x"] * 2 + 1 - self.core}
+
+    def enter(self, core=False):
         barrier = pltpu.get_barrier_semaphore()
+        if core:
+            pl.semaphore_signal(barrier, inc=1, device_id=self.sibling(), device_id_type=MESH_ID)
         for axis in "xyz":
             for step in range(1, RING):
                 pl.semaphore_signal(barrier, inc=1, device_id=self.peer(axis, step), device_id_type=MESH_ID)
-        pl.semaphore_wait(barrier, 9)
+        pl.semaphore_wait(barrier, 9 + core)
 
 
 class Sender:
@@ -106,6 +111,16 @@
         self.copies += started
         return started
 
+    def swap(self, source, target):
+        copy = pltpu.make_async_remote_copy(
+            src_ref=source, dst_ref=target,
+            send_sem=self.send_sems.at[self.used], recv_sem=self.recv_sems.at[self.used],
+            device_id=self.place.sibling(), device_id_type=MESH_ID,
+        )
+        copy.start()
+        self.used += 1
+        return copy
+
     def drain(self):
         for copy in self.copies:
             copy.wait_send()
@@ -134,6 +149,10 @@
 
 def dot_rows(lhs, rhs):
     return lax.dot_general(lhs, rhs, (((1,), (1,)), ((), ())), preferred_element_type=F32)
+
+
+def dot_plain(lhs, rhs):
+    return lax.dot_general(lhs, rhs, (((1,), (0,)), ((), ())), preferred_element_type=F32)
 
 
 def probs_block(k_t, q_t, seg, seg_col, row, first):
@@ -300,16 +319,28 @@
 
 
 class GradScatter:
-    COPIES = 27
-
-    def __init__(self, place, sender, grads, mine, first, second, third, final, local_sems):
+    def __init__(self, place, sender, grads, widths, bufs, final, local_sems):
         self.place, self.sender, self.grads = place, sender, grads
-        self.mine, self.bufs, self.final, self.local_sems = mine, (first, second, third), final, local_sems
+        self.bufs, self.final, self.local_sems = bufs, final, local_sems
+        self.parts = range(len(widths))
+        self.cols = [(sum(widths[:part]), widths[part]) for part in self.parts]
+
+    @staticmethod
+    def scratch(widths):
+        shapes = []
+        for width in widths:
+            shapes += [
+                pltpu.VMEM((RING, RING, PIECE, width), BF16),
+                pltpu.VMEM((3, RING, RING, PIECE, width), BF16),
+                pltpu.VMEM((RING, RING, PIECE, width), BF16),
+                pltpu.VMEM((3, PIECE, width), BF16),
+            ]
+        return shapes
 
     def cut(self, part, step):
         axis = ORDERS[part][0]
         index = self.place.block(axis, step)
-        cols = pl.ds(part * THIRD, THIRD)
+        cols = pl.ds(*self.cols[part])
         if axis == "x":
             return self.grads.at[index, :, :, :, cols]
         if axis == "z":
@@ -317,56 +348,61 @@
         return self.grads.at[:, :, index, :, cols]
 
     def start(self):
-        self.loads, self.one, self.two, self.three = [], [], [None] * 3, [None] * 3
-        for part in range(3):
+        self.loads, self.one, self.two, self.three = [], [], {}, {}
+        for part in self.parts:
             self.one.append(self.sender.ring(
-                ORDERS[part][0], lambda step: self.cut(part, step), lambda step: self.bufs[0].at[part, step - 1]))
-        for part in range(3):
-            load = pltpu.make_async_copy(self.cut(part, 0), self.mine.at[part], self.local_sems.at[part])
+                ORDERS[part][0], lambda step: self.cut(part, step), lambda step: self.bufs[part][1].at[step - 1]))
+        for part in self.parts:
+            load = pltpu.make_async_copy(self.cut(part, 0), self.bufs[part][0], self.local_sems.at[part])
             load.start()
             self.loads.append(load)
 
-    def second(self, part):
-        self.loads[part].wait()
-        wait_all(self.one[part])
-
-        @pl.loop(0, RING)
-        def _(a):
-            for b in range(RING):
-                total = self.mine[part, a, b].astype(F32)
+    def second(self):
+        for part in self.parts:
+            self.loads[part].wait()
+            wait_all(self.one[part])
+            mine, first, second, _ = self.bufs[part]
+
+            @pl.loop(0, RING)
+            def _(a):
+                for b in range(RING):
+                    total = mine[a, b].astype(F32)
+                    for k in range(3):
+                        total = total + first[k, a, b].astype(F32)
+                    mine[a, b] = total.astype(BF16)
+
+            axis, spot = ORDERS[part][1], ORDERS[part][3]
+
+            def source(step):
+                index = self.place.block(axis, step)
+                return mine.at[:, index] if spot else mine.at[index]
+
+            self.two[part] = self.sender.ring(axis, source, lambda step: second.at[step - 1])
+
+    def third(self):
+        for part in self.parts:
+            wait_all(self.two[part])
+            mine, _, second, third = self.bufs[part]
+            axis, spot = ORDERS[part][1], ORDERS[part][3]
+            own = self.place.block(axis, 0)
+            for other in range(RING):
+                total = mine[(other, own) if spot else (own, other)].astype(F32)
                 for k in range(3):
-                    total = total + self.bufs[0][part, k, a, b].astype(F32)
-                self.mine[part, a, b] = total.astype(BF16)
-
-        axis, spot = ORDERS[part][1], ORDERS[part][3]
-
-        def source(step):
-            index = self.place.block(axis, step)
-            return self.mine.at[part, :, index] if spot else self.mine.at[part, index]
-
-        self.two[part] = self.sender.ring(axis, source, lambda step: self.bufs[1].at[part, step - 1])
-
-    def third(self, part):
-        wait_all(self.two[part])
-        axis, spot = ORDERS[part][1], ORDERS[part][3]
-        own = self.place.block(axis, 0)
-        for other in range(RING):
-            at = (part, other, own) if spot else (part, own, other)
-            total = self.mine[at].astype(F32)
+                    total = total + second[k, other].astype(F32)
+                second[3, other] = total.astype(BF16)
+            axis = ORDERS[part][2]
+            self.three[part] = self.sender.ring(
+                axis, lambda step: second.at[3, self.place.block(axis, step)], lambda step: third.at[step - 1])
+
+    def finish(self):
+        for part in self.parts:
+            wait_all(self.three[part])
+            _, _, second, third = self.bufs[part]
+            total = second[3, self.place.block(ORDERS[part][2], 0)].astype(F32)
             for k in range(3):
-                total = total + self.bufs[1][part, k, other].astype(F32)
-            self.bufs[1][part, 3, other] = total.astype(BF16)
-        axis = ORDERS[part][2]
-        self.three[part] = self.sender.ring(
-            axis, lambda step: self.bufs[1].at[part, 3, self.place.block(axis, step)], lambda step: self.bufs[2].at[part, step - 1])
-
-    def finish(self, part):
-        wait_all(self.three[part])
-        own = self.place.block(ORDERS[part][2], 0)
-        total = self.bufs[1][part, 3, own].astype(F32)
-        for k in range(3):
-            total = total + self.bufs[2][part, k].astype(F32)
-        self.final[:, part * THIRD : (part + 1) * THIRD] = total.astype(BF16)
+                total = total + third[k].astype(F32)
+            start, width = self.cols[part]
+            self.final[:, start : start + width] = total.astype(BF16)
 
 
 class PlaneGather:
@@ -409,99 +445,211 @@
     return finish
 
 
-def scatter_kernel(count, with_gains, attention, *refs):
-    grads, refs = refs[:count], refs[count:]
-    if with_gains:
-        gain_in, refs = refs[0], refs[1:]
-    work = None
-    if attention:
-        work = functools.partial(attention_backward, *refs[:4], refs[4 + count])
-        refs = refs[4 : 4 + count] + refs[5 + count :]
-    outs, refs = refs[:count], refs[count:]
-    if with_gains:
-        gain_out, refs = refs[0], refs[1:]
-    mine, first, second, third, final, send_sems, recv_sems, local_sems = refs[:8]
-    place = Place()
-    sender = Sender(place, send_sems, recv_sems)
-    place.enter()
-    works = []
-    for i in range(count):
-        works.append(GradScatter(place, sender, grads[i], mine.at[i], first.at[i], second.at[i], third.at[i], final.at[i], local_sems.at[i]))
-    planes = [PlaneGather(place, sender, final.at[i], outs[i], local_sems.at[i, 3]) for i in range(count)]
-    if with_gains:
-        gains, gain_bufs = refs[8:]
-        gains[0] = gain_in[...]
-        gain_finish = gain_step(place, sender, gains, gain_bufs, 0, "z")
-    for item in works:
-        item.start()
-    if work is not None:
-        work(0, 14)
-    for i, item in enumerate(works):
-        for part in range(3):
-            item.second(part)
-        if work is not None and i == 0:
-            work(14, 16)
-    if with_gains:
-        gain_finish()
-        gain_finish = gain_step(place, sender, gains, gain_bufs, 1, "y")
-    for item in works:
-        for part in range(3):
-            item.third(part)
-    if with_gains:
-        gain_finish()
-        gain_finish = gain_step(place, sender, gains, gain_bufs, 2, "x")
-    for item, plane in zip(works, planes):
-        for part in range(3):
-            item.finish(part)
-        plane.start()
-    if with_gains:
-        gain_finish()
-        gain_out[...] = gains[3]
-    for plane in planes:
-        plane.second()
-    for plane in planes:
-        plane.finish()
-    sender.drain()
-
-
-def scatter_grads(grads, gains, collective_id, attention=()):
-    count = len(grads)
-    with_gains = gains is not None
-    copies = (GradScatter.COPIES + PlaneGather.COPIES) * count + 9 * with_gains
-    block = (RING, RING, PIECE, THIRD)
-    any_spec = pl.BlockSpec(memory_space=pl.ANY)
-    vmem_spec = pl.BlockSpec(memory_space=pltpu.VMEM)
+def grad_works(place, sender, grads, widths, bufs, finals, outs, local_sems):
+    parts = len(widths)
+    works, planes = [], []
+    for i, grad in enumerate(grads):
+        mine = bufs[4 * parts * i : 4 * parts * (i + 1)]
+        mine = [mine[4 * part : 4 * part + 4] for part in range(parts)]
+        works.append(GradScatter(place, sender, grad, widths, mine, finals.at[i], local_sems.at[i]))
+        planes.append(PlaneGather(place, sender, finals.at[i], outs[i], local_sems.at[i, 3]))
+    return works, planes
+
+
+def comm_scratch(count, widths, extra):
+    copies = (9 * len(widths) + PlaneGather.COPIES) * count + extra
     scratch = [
-        pltpu.VMEM((count, 3) + block, BF16),
-        pltpu.VMEM((count, 3, 3) + block, BF16),
-        pltpu.VMEM((count, 3, 4) + block[1:], BF16),
-        pltpu.VMEM((count, 3, 3) + block[2:], BF16),
         pltpu.VMEM((count, PIECE, WIDTH), BF16),
         pltpu.SemaphoreType.DMA((copies,)),
         pltpu.SemaphoreType.DMA((copies,)),
         pltpu.SemaphoreType.DMA((count, 4)),
     ]
-    out_shape = [jax.ShapeDtypeStruct(grad.shape[1:], BF16) for grad in grads]
-    operands = list(grads)
-    extra_outs = 0
-    if with_gains:
-        scratch += [pltpu.VMEM((4,) + gains.shape, F32), pltpu.VMEM((3, 3) + gains.shape, F32)]
-        out_shape.append(jax.ShapeDtypeStruct(gains.shape, F32))
-        operands.append(gains)
-        extra_outs = 1
-    if attention:
-        out_shape.append(jax.ShapeDtypeStruct(attention[0].shape, BF16))
-        operands += attention
-        extra_outs = 1
+    for _ in range(count):
+        scratch += GradScatter.scratch(widths)
+    return scratch
+
+
+ANY_SPEC = pl.BlockSpec(memory_space=pl.ANY)
+VMEM_SPEC = pl.BlockSpec(memory_space=pltpu.VMEM)
+ATT_WIDTHS = (768, 768)
+MLP_WIDTHS = (640, 512, 384)
+
+
+def last_kernel(grad, gain_in, out, gain_out, gains, gain_bufs, finals, send_sems, recv_sems, local_sems, *bufs):
+    place = Place()
+    sender = Sender(place, send_sems, recv_sems)
+    place.enter()
+    (work,), (plane,) = grad_works(place, sender, [grad], ATT_WIDTHS, bufs, finals, [out], local_sems)
+    gains[0] = gain_in[...]
+    gain_finish = gain_step(place, sender, gains, gain_bufs, 0, "z")
+    work.start()
+    gain_finish()
+    gain_finish = gain_step(place, sender, gains, gain_bufs, 1, "y")
+    work.second()
+    gain_finish()
+    gain_finish = gain_step(place, sender, gains, gain_bufs, 2, "x")
+    work.third()
+    work.finish()
+    plane.start()
+    gain_finish()
+    gain_out[...] = gains[3]
+    plane.second()
+    plane.finish()
+    sender.drain()
+
+
+def scatter_last(grad, gains):
     return pl.pallas_call(
-        lambda *refs: scatter_kernel(count, with_gains, bool(attention), *refs),
-        out_shape=out_shape,
-        in_specs=[any_spec] * count + [vmem_spec] * (len(operands) - count),
-        out_specs=[any_spec] * count + [vmem_spec] * extra_outs,
-        scratch_shapes=scratch,
-        compiler_params=pltpu.CompilerParams(collective_id=collective_id, has_side_effects=True, vmem_limit_bytes=60 << 20),
-        name=f"scatter_grads_{collective_id}",
-    )(*operands)
+        last_kernel,
+        out_shape=[jax.ShapeDtypeStruct(grad.shape[1:], BF16), jax.ShapeDtypeStruct(gains.shape, F32)],
+        in_specs=[ANY_SPEC, VMEM_SPEC],
+        out_specs=[ANY_SPEC, VMEM_SPEC],
+        scratch_shapes=[pltpu.VMEM((4,) + gains.shape, F32), pltpu.VMEM((3, 3) + gains.shape, F32)] + comm_scratch(1, ATT_WIDTHS, 9),
+        compiler_params=pltpu.CompilerParams(collective_id=4, has_side_effects=True, vmem_limit_bytes=32 << 20),
+        name="scatter_last",
+    )(grad, gains)
+
+
+QKV_ROWS = 576
+OUT_ROWS = 192
+TOKENS = 2 * SEQ
+STEP = 256
+NORM_STEP = 128
+
+
+def back_kernel(
+    grad_up, grad_down, qkv_in, seg, seg_col, attn, grad_one_in, w_att, normed_in, x_in, gain,
+    out_up, out_down, grad_att, grad_x, gain_grad,
+    qkv, grad_attn, grad_one, normed, w_qkv, w_out, part, other, stage, load_sems, stage_sems,
+    finals, send_sems, recv_sems, local_sems, *bufs,
+):
+    place = Place()
+    sender = Sender(place, send_sems, recv_sems)
+    loads = {}
+
+    def load(name, source, target, index):
+        copy = pltpu.make_async_copy(source, target, load_sems.at[index])
+        copy.start()
+        loads.setdefault(name, []).append(copy)
+
+    def ready(name):
+        for copy in loads[name]:
+            copy.wait()
+
+    load("one", grad_one_in, grad_one, 0)
+    for shard in range(RING):
+        load("out", w_att.at[shard, pl.ds(QKV_ROWS, OUT_ROWS)], w_out.at[pl.ds(shard * OUT_ROWS, OUT_ROWS)], 1 + shard)
+    load("qkv", qkv_in, qkv, 5)
+    load("normed", normed_in, normed, 6)
+    for shard in range(RING):
+        load("w", w_att.at[shard, pl.ds(0, QKV_ROWS)], w_qkv.at[pl.ds(shard * QKV_ROWS, QKV_ROWS)], 7 + shard)
+    place.enter(core=True)
+    works, planes = grad_works(place, sender, [grad_up, grad_down], MLP_WIDTHS, bufs, finals, [out_up, out_down], local_sems)
+    for work in works:
+        work.start()
+
+    stores = []
+
+    def put(rows, shard, start):
+        slot = len(stores) % 2
+        if len(stores) >= 2:
+            stores[-2].wait()
+        stage[slot] = rows.astype(BF16)
+        copy = pltpu.make_async_copy(stage.at[slot], grad_att.at[shard, pl.ds(start, OUT_ROWS)], stage_sems.at[slot])
+        copy.start()
+        stores.append(copy)
+
+    ready("one")
+    ready("out")
+    for shard in range(RING):
+        rows = pl.ds(shard * OUT_ROWS, OUT_ROWS)
+        grad_attn[rows] = dot_rows(w_out[rows], grad_one[...]).astype(BF16)
+    ready("qkv")
+    attention_backward(qkv, seg, seg_col, grad_attn, qkv, 0, 16)
+    works[0].second()
+
+    ready("w")
+    swaps = []
+    for index in range(TOKENS // STEP):
+        rows = pl.ds(index * STEP, STEP)
+        part[rows] = dot_cols(qkv[:, index * STEP : (index + 1) * STEP], w_qkv[...]).astype(BF16)
+        swaps.append(sender.swap(part.at[rows], other.at[rows]))
+    works[1].second()
+    for shard in range(RING):
+        put(dot_plain(attn[shard * OUT_ROWS : (shard + 1) * OUT_ROWS], grad_one[...]), shard, QKV_ROWS)
+    ready("normed")
+    for shard in range(RING):
+        for block in range(3):
+            start = shard * QKV_ROWS + block * OUT_ROWS
+            put(dot_plain(qkv[start : start + OUT_ROWS], normed[...]), shard, block * OUT_ROWS)
+    for store in stores[-2:]:
+        store.wait()
+    load("x", x_in, normed, 11)
+    for work in works:
+        work.third()
+    ready("x")
+    gain_grad[...] = jnp.zeros_like(gain_grad)
+    wait_all(swaps)
+    for copy in swaps:
+        copy.wait_send()
+
+    @pl.loop(0, TOKENS // NORM_STEP)
+    def _(index):
+        rows = pl.ds(pl.multiple_of(index * NORM_STEP, NORM_STEP), NORM_STEP)
+        x_f32 = normed[rows].astype(F32)
+        centered = x_f32 - jnp.mean(x_f32, axis=-1, keepdims=True)
+        inv_std = lax.rsqrt(jnp.mean(centered * centered, axis=-1, keepdims=True) + EPS_NORM)
+        x_hat = centered * inv_std
+        grad = (part[rows].astype(F32) + other[rows].astype(F32)).astype(BF16).astype(F32)
+        gain_grad[...] += jnp.sum(grad * x_hat, axis=0, keepdims=True)
+        grad_hat = grad * gain[...].astype(F32)
+        mean_one = jnp.mean(grad_hat, axis=-1, keepdims=True)
+        mean_two = jnp.mean(grad_hat * x_hat, axis=-1, keepdims=True)
+        back = inv_std * (grad_hat - mean_one - x_hat * mean_two)
+        part[rows] = (grad_one[rows].astype(F32) + back).astype(BF16)
+
+    result = pltpu.make_async_copy(part, grad_x, load_sems.at[12])
+    result.start()
+    for work, plane in zip(works, planes):
+        work.finish()
+        plane.start()
+    for plane in planes:
+        plane.second()
+    for plane in planes:
+        plane.finish()
+    result.wait()
+    sender.drain()
+
+
+def backward(grad_up, grad_down, qkv_t, seg, seg_col, attn, grad_one, w_att, normed, x_rows, gain):
+    tokens = (TOKENS, WIDTH)
+    return pl.pallas_call(
+        back_kernel,
+        out_shape=[
+            jax.ShapeDtypeStruct(grad_up.shape[1:], BF16),
+            jax.ShapeDtypeStruct(grad_down.shape[1:], BF16),
+            jax.ShapeDtypeStruct(w_att.shape, BF16),
+            jax.ShapeDtypeStruct(tokens, BF16),
+            jax.ShapeDtypeStruct((1, WIDTH), F32),
+        ],
+        in_specs=[ANY_SPEC, ANY_SPEC, ANY_SPEC, VMEM_SPEC, VMEM_SPEC, VMEM_SPEC, ANY_SPEC, ANY_SPEC, ANY_SPEC, ANY_SPEC, VMEM_SPEC],
+        out_specs=[ANY_SPEC, ANY_SPEC, ANY_SPEC, ANY_SPEC, VMEM_SPEC],
+        scratch_shapes=[
+            pltpu.VMEM(qkv_t.shape, BF16),
+            pltpu.VMEM(attn.shape, BF16),
+            pltpu.VMEM(tokens, BF16),
+            pltpu.VMEM(tokens, BF16),
+            pltpu.VMEM((RING * QKV_ROWS, WIDTH), BF16),
+            pltpu.VMEM((RING * OUT_ROWS, WIDTH), BF16),
+            pltpu.VMEM(tokens, BF16),
+            pltpu.VMEM(tokens, BF16),
+            pltpu.VMEM((2, OUT_ROWS, WIDTH), BF16),
+            pltpu.SemaphoreType.DMA((13,)),
+            pltpu.SemaphoreType.DMA((2,)),
+        ] + comm_scratch(2, MLP_WIDTHS, TOKENS // STEP),
+        compiler_params=pltpu.CompilerParams(collective_id=3, has_side_effects=True, vmem_limit_bytes=67043328),
+        name="backward",
+    )(grad_up, grad_down, qkv_t, seg, seg_col, attn, grad_one, w_att, normed, x_rows, gain)
 
 
 def solution(mesh):
@@ -535,7 +683,7 @@
         seg_rows = own_rows(seg_ids)
         grad_rows = own_rows(grad_y).reshape(tokens, hidden)
         seg_row, seg_col = seg_rows[:, None, :], seg_rows[:, :, None]
-        normed_a, hat_a, inv_a = norm_forward(x_rows, gain_one)
+        normed_a, _, _ = norm_forward(x_rows, gain_one)
         qkv_t = dot_nt(w_qkv_t, normed_a).astype(BF16)
         qkv_t = qkv_t.reshape(RING * qkv_cols, tokens)
         up_t, down, attn_flat = gather_weights([own_up, own_down], 2, (qkv_t, seg_row, seg_col))
@@ -566,19 +714,10 @@
         grad_norm_b = pair_sum(part_b).astype(BF16)
         back_b, gain_grad_two = norm_backward(grad_norm_b, hat_b, inv_b, gain_two)
         grad_x_one = (grad_rows.astype(F32) + back_b).astype(BF16)
-        grad_out_w = dot_nn(attn_flat, grad_x_one).astype(BF16)
-        grad_attn = dot_nt(w_out_all, grad_x_one).astype(BF16)
-        grad_up_own, grad_down_own, grad_qkv_t = scatter_grads(
-            [grad_up_w, grad_down_w], None, 3, (qkv_t, seg_row, seg_col, grad_attn))
-        part_a = dot_tn(grad_qkv_t, w_qkv_t.reshape(RING * qkv_cols, hidden)).astype(BF16)
-        grad_norm_a = pair_sum(part_a).astype(BF16)
-        back_a, gain_grad_one = norm_backward(grad_norm_a, hat_a, inv_a, gain_one)
-        grad_x = (grad_x_one.astype(F32) + back_a).astype(BF16)
-
-        grad_qkv_w = dot_nn(grad_qkv_t, normed_a).astype(BF16)
-        grad_att = jnp.concatenate([grad_qkv_w.reshape(RING, qkv_cols, hidden), grad_out_w.reshape(RING, shard_rows - qkv_cols, hidden)], axis=1)
-        gains = jnp.concatenate([gain_grad_one[None], gain_grad_two[None], jnp.zeros((6, hidden), F32)], axis=0)
-        grad_att_own, gains = scatter_grads([grad_att.reshape(grid_shape)], gains, 4)
+        grad_up_own, grad_down_own, grad_att, grad_x, gain_grad_one = backward(
+            grad_up_w, grad_down_w, qkv_t, seg_row, seg_col, attn_flat, grad_x_one, w_att, normed_a, x_rows, gain_one[None])
+        gains = jnp.concatenate([gain_grad_one, gain_grad_two[None], jnp.zeros((6, hidden), F32)], axis=0)
+        grad_att_own, gains = scatter_last(grad_att.reshape(grid_shape), gains)
         grad_att_own = grad_att_own.reshape(shard_rows, hidden)
 
         def spread(rows):

time: 656 us -> 586 us (0.89)
  matrix products: 154 us -> 121 us
  other arithmetic: 43.5 us -> 21.8 us
  Pallas kernels: 384 us -> 376 us
    dot_general x4 -> x3, matrix products: 56.6 us -> 33.4 us  [dot_tn(): lax.dot_general(lhs, rhs, (((0,), (0,)), ((), ())), preferred_element_typ...]
    dot_general x4 -> x2, matrix products: 47.2 us -> 32 us  [dot_nn(): lax.dot_general(lhs, rhs, (((lhs.ndim - 1,), (0,)), ((), ())), preferred_...]
    pallas_call x2, Pallas kernels: 257 us -> 248 us  [the longest x1 149 us: backward(): pl.pallas_call(back_kernel, out_shape=[jax.ShapeDtypeStruct(grad_up.shape...]
    unnamed x63 -> x55, local copies, waits for them, and re-layouts: 20.2 us -> 25.9 us
    dot_general x4 -> x3, matrix products: 50.2 us -> 55.5 us  [dot_nt(): lax.dot_general(lhs, rhs, (((lhs.ndim - 1,), (rhs.ndim - 1,)), ((), ())),...]
  transfers between devices with their start and end apart: 6 -> 5, of which waited for: 2 -> 1; matrix products, arithmetic and copies ran while one was open for 18% -> 11% of each run, Pallas kernels for 39% -> 43%
where the time goes in v3:
time: 586 us; the launch traced here: 583 us
  Pallas kernels  376 us (64%)
  matrix products  121 us (21%)
  local copies, waits for them, and re-layouts  45.1 us (8%)
  other arithmetic  21.8 us (4%)
  between operations  14.7 us (3%)
    pallas_call x1, Pallas kernels, backward(): pl.pallas_call(back_kernel, out_shape=[jax.ShapeDtypeStruct(grad_up.shape...  149 us
    pallas_call x2, Pallas kernels, gather_weights(): pl.pallas_call(lambda *refs: gather_kernel(count, bool(attention), *refs)...  127 us
    pallas_call x1, Pallas kernels, scatter_last(): pl.pallas_call(last_kernel, out_shape=[jax.ShapeDtypeStruct(grad.shape[1:...  99 us
    dot_general x3, matrix products, dot_nt(): lax.dot_general(lhs, rhs, (((lhs.ndim - 1,), (rhs.ndim - 1,)), ((), ())),...  55.5 us
    dot_general x3, matrix products, dot_tn(): lax.dot_general(lhs, rhs, (((0,), (0,)), ((), ())), preferred_element_typ...  33.4 us
    dot_general x2, matrix products, dot_nn(): lax.dot_general(lhs, rhs, (((lhs.ndim - 1,), (0,)), ((), ())), preferred_...  32 us
    unnamed x55, local copies, waits for them, and re-layouts  25.9 us
  transfers between devices with their start and end apart: 5, of which 1 were waited for; matrix products, arithmetic and copies ran while one was open for 11% of the time, Pallas kernels for 43%

profile of v3, /device:TPU:0, one launch (start us, length us, event | category | flops | bytes accessed | tf_op | source)
XLA Modules:
  0.0 582.7 jit_solution(17511643337326797518)
XLA Ops:
  9.6 3.0 copy.23
  12.7 2.5 convert_reduce_fusion.1
  15.2 1.0 fusion.30
  16.4 47.2 %gather_weights_1.1 = bf16[4,4,4,48,1536]{4,3,2,1,0:T(8,128)(2,1)S(1)} custom-call(bf16[4,4,48,1536]{3,2,1,0:T(8,128)(2,1)S(1)} %bitcast.59), custom_call_target="tpu_custom_call" | custom-call | tf_op jit(solution)/shard_map/gather_weights_1/pallas_call | solution.py:302
  63.7 1.7 slice.32
  65.3 1.0 fusion.27.normed_in
  66.4 7.8 %fusion.35 = bf16[4,576,1024]{2,1,0:T(8,128)(2,1)S(1)} fusion(bf16[1024,1536]{1,0:T(8,128)(2,1)S(1)} %fusion.27.normed_in, bf16[4,768,1536]{2,1,0:T(8,128)(2,1)S(1)} %bitcast.53), kind=kOutput, calls=%fused_computation.57 | convolution fusion | flops 7250116608 | bytes 14942208 | tf_op jit(solution)/shard_map/dot_general | solution.py:39
  74.3 80.2 %gather_weights_2.1 = (bf16[4,4,4,48,1536]{4,3,2,1,0:T(8,128)(2,1)}, bf16[4,4,4,48,1536]{4,3,2,1,0:T(8,128)(2,1)}, bf16[768,1024]{1,0:T(8,128)(2,1)S(1)}) custom-call(bf16[4,4,48,1536]{3,2,1,0:T(8,128)(2,1)S(1)} %bitcast.58, bf16[4,4,48,1536]{3,2,1,0:T(8,128)(2,1)S(1)} %bitcast.60, bf16[2304,1024]{1,0:T(8,128)(2,1)S(1)} %bitcast.55, ...), custom_call_target="tpu_custom_call" | custom-call | tf_op jit(solution)/shard_map/gather_weights_2/pallas_call | solution.py:302
  154.5 3.0 convolution_convert_fusion.4
  157.9 2.3 constant_dynamic-slice_fusion.1
  160.2 3.3 collective-permute-done
  163.5 1.6 convert_reduce_fusion
  166.2 15.8 %fusion.42 = f32[3072,1024]{1,0:T(8,128)} fusion(bf16[3072,1536]{1,0:T(8,128)(2,1)} %bitcast.81, bf16[1024,1536]{1,0:T(8,128)(2,1)S(1)} %get-tuple-element.35, f32[1536]{0:T(1024)S(1)} %convert_element_type.123, f32[1024]{0:T(1024)S(1)} %add_rsqrt_fusion, f32[1024]{0:T(1024)S(1)} %broadcast_multiply_fusion.2), kind=kOutput, calls=%fused_computation.74 | convolution fusion | flops 9671540736 | bytes 25180160 | tf_op jit(solution)/shard_map/dot_general | solution.py:39
  182.0 31.9 %fusion.2 = bf16[3072,1024]{1,0:T(8,128)(2,1)S(1)} fusion(f32[3072,1024]{1,0:T(8,128)} %fusion.42, bf16[3072,1536]{1,0:T(8,128)(2,1)} %bitcast.79, bf16[1024,1536]{1,0:T(8,128)(2,1)S(1)} %bitcast.62), kind=kOutput, calls=%fused_computation.6 | convolution fusion | flops 9732882432 | bytes 31457280 | tf_op jit(solution)/shard_map/dot_general | solution.py:39
  213.9 2.7 copy-done.23
  216.6 14.3 %convolution_convert_fusion.2 = bf16[1024,1536]{1,0:T(8,128)(2,1)} fusion(bf16[3072,1024]{1,0:T(8,128)(2,1)S(1)} %fusion.2, bf16[3072,1536]{1,0:T(8,128)(2,1)} %bitcast.82), kind=kOutput, calls=%fused_computation.53 | convolution fusion | flops 9665249280 | bytes 18874368 | tf_op jit(solution)/shard_map/dot_general | solution.py:43
  231.1 16.1 %convolution_convert_fusion.3 = bf16[1024,1536]{1,0:T(8,128)(2,1)} fusion(bf16[3072,1536]{1,0:T(8,128)(2,1)} %bitcast.80, f32[3072,1024]{1,0:T(8,128)S(1)} %copy-done.24), kind=kOutput, calls=%fused_computation.54 | convolution fusion | flops 9693560832 | bytes 25165824 | tf_op jit(solution)/shard_map/dot_general | solution.py:43
  247.7 6.2 %fusion.32 = (f32[1536]{0:T(1024)}, f32[1024]{0:T(1024)S(1)}, f32[1024]{0:T(1024)S(1)}, bf16[1024,1536]{1,0:T(8,128)(2,1)S(1)}) fusion(bf16[1024,1536]{1,0:T(8,128)(2,1)S(1)} %copy-done.10, f32[1024]{0:T(1024)S(1)} %add_rsqrt_fusion, f32[1024]{0:T(1024)S(1)} %broadcast_multiply_fusion.2, f32[1536]{0:T(1024)S(1)} %convert_element_type.123, ...), kind=kLoop, calls=%fused_computation.48 | loop fusion | flops 22016512 | bytes 12611584 | tf_op jit(solution)/shard_map/reduce_sum | solution.py:31
  253.9 6.9 %fusion.23 = (bf16[1024,1536]{1,0:T(8,128)(2,1)}, bf16[1024,1536]{1,0:T(8,128)(2,1)S(1)}) fusion(bf16[1024,1536]{1,0:T(8,128)(2,1)S(1)} %copy-done.10, bf16[1024,1536]{1,0:T(8,128)(2,1)S(1)} %get-tuple-element.33, f32[1024]{0:T(1024)S(1)} %get-tuple-element.42, f32[1024]{0:T(1024)S(1)} %get-tuple-element.43, f32[1536]{0:T(1024)S(1)} %convert_element_type.123, ...), kind=kLoop, calls=%fused_computation.39 | loop fusion | flops 29884416 | bytes 22042624 | tf_op jit(solution)/shard_map/convert_element_type | solution.py:716
  260.8 1.2 constant_dynamic-slice_fusion.2
  262.7 15.7 %convolution_convert_fusion.1 = bf16[3072,1536]{1,0:T(8,128)(2,1)} fusion(bf16[3072,1024]{1,0:T(8,128)(2,1)} %copy-done.23, bf16[1024,1536]{1,0:T(8,128)(2,1)S(1)} %copy-done.10, f32[1536]{0:T(1024)S(1)} %convert_element_type.123, f32[1024]{0:T(1024)S(1)} %add_rsqrt_fusion, f32[1024]{0:T(1024)S(1)} %broadcast_multiply_fusion.2), kind=kOutput, calls=%fused_computation.16 | convolution fusion | flops 9676259328 | bytes 18888704 | tf_op jit(solution)/shard_map/dot_general | solution.py:47
  278.4 16.3 %convolution_convert_fusion = bf16[3072,1536]{1,0:T(8,128)(2,1)} fusion(bf16[1024,1536]{1,0:T(8,128)(2,1)S(1)} %bitcast.63, f32[3072,1024]{1,0:T(8,128)} %fusion.42), kind=kOutput, calls=%fused_computation.15 | convolution fusion | flops 9696706560 | bytes 25165824 | tf_op jit(solution)/shard_map/dot_general | solution.py:47
  294.7 149.3 %backward.1 = (bf16[4,4,48,1536]{3,2,1,0:T(8,128)(2,1)}, bf16[4,4,48,1536]{3,2,1,0:T(8,128)(2,1)}, bf16[4,768,1536]{2,1,0:T(8,128)(2,1)}, bf16[1024,1536]{1,0:T(8,128)(2,1)}, f32[1,1536]{1,0:T(1,128)}) custom-call(bf16[4,4,4,48,1536]{4,3,2,1,0:T(8,128)(2,1)} %bitcast.64, bf16[4,4,4,48,1536]{4,3,2,1,0:T(8,128)(2,1)} %bitcast.65, bf16[2304,1024]{1,0:T(8,128)(2,1)} %bitcast.56, ...), custom_call_target="tpu_custom_call" | custom-call | tf_op jit(solution)/shard_map/backward/pallas_call | solution.py:626
  444.1 2.7 constant_dynamic-slice_fusion
  448.3 3.7 copy-done.2
  452.0 99.0 %scatter_last.1 = (bf16[4,4,48,1536]{3,2,1,0:T(8,128)(2,1)S(1)}, f32[8,1536]{1,0:T(8,128)S(1)}) custom-call(bf16[4,4,4,48,1536]{4,3,2,1,0:T(8,128)(2,1)S(1)} %bitcast.57, f32[8,1536]{1,0:T(8,128)S(1)} %maximum_maximum_fusion.gain_in), custom_call_target="tpu_custom_call" | custom-call | tf_op jit(solution)/shard_map/scatter_last/pallas_call | solution.py:502
  551.9 1.4 slice.28
  553.2 2.4 copy.26
  556.3 11.0 %copy.32 = bf16[8,512,1536]{2,1,0:T(8,128)(2,1)} copy(bf16[8,512,1536]{2,1,0:T(8,128)(2,1)} %all-gather.3.cloned.1.call-done) | data formatting | bytes 25165824
  567.3 2.0 copy-done.12
  569.3 5.0 copy.33
  574.3 1.4 copy.34
  (81 shorter events, 8.3 us)
Async XLA Ops:
  7.2 549.1 %all-gather.3.cloned.1.call-start = ((), (), s32[]{:S(2)}) async-start(), calls=%async_computation | async-start | bytes 14155776 | tf_op jit(solution)/shard_map/all_gather | solution.py:726
  8.7 65.5 %copy-start.6 = (s32[2,1,512]{2,1,0:T(1,128)}, s32[2,1,512]{2,1,0:T(1,128)S(1)}, u32[]{:S(2)}) copy-start(s32[2,1,512]{2,1,0:T(1,128)S(1)} %broadcast_in_dim.10.refs_3_.seg) | copy-start | bytes 12292
  9.6 64.6 %copy-start.3 = (s32[2,512,1]{2,1,0:T(8,128)}, s32[2,512,1]{2,1,0:T(8,128)S(1)}, u32[]{:S(2)}) copy-start(s32[2,512,1]{2,1,0:T(8,128)S(1)} %copy.24.refs_4_.seg_col) | copy-start | bytes 12292
  9.6 6.6 %copy-start.20 = (bf16[2,96,1536]{2,1,0:T(8,128)(2,1)S(1)}, bf16[2,96,1536]{2,1,0:T(8,128)(2,1)}, u32[]{:S(2)}) copy-start(bf16[2,96,1536]{2,1,0:T(8,128)(2,1)} %param.14) | copy-start | bytes 1769476
  12.7 3.6 copy-start.19
  15.2 50.1 %copy-start.7 = (bf16[2,512,1536]{2,1,0:T(8,128)(2,1)}, bf16[2,512,1536]{2,1,0:T(8,128)(2,1)S(1)}, u32[]{:S(2)}) copy-start(bf16[2,512,1536]{2,1,0:T(8,128)(2,1)S(1)} %get-tuple-element.37) | copy-start | bytes 9437188
  63.7 10.5 %copy-start = (bf16[4,4,4,48,1536]{4,3,2,1,0:T(8,128)(2,1)}, bf16[4,4,4,48,1536]{4,3,2,1,0:T(8,128)(2,1)S(1)}, u32[]{:S(2)}) copy-start(bf16[4,4,4,48,1536]{4,3,2,1,0:T(8,128)(2,1)S(1)} %gather_weights_1.1) | copy-start | bytes 28311556
  66.4 7.8 %copy-start.11 = (bf16[1024,1536]{1,0:T(8,128)(2,1)}, bf16[1024,1536]{1,0:T(8,128)(2,1)S(1)}, u32[]{:S(2)}) copy-start(bf16[1024,1536]{1,0:T(8,128)(2,1)S(1)} %fusion.27.normed_in) | copy-start | bytes 9437188
  66.4 7.9 %copy-start.4 = (bf16[768,1536]{1,0:T(8,128)(2,1)S(1)}, bf16[768,1536]{1,0:T(8,128)(2,1)}, u32[]{:S(2)}) copy-start(bf16[768,1536]{1,0:T(8,128)(2,1)} %param.16) | copy-start | bytes 7077892
  74.2 83.3 %copy-start.1 = (bf16[4,576,1024]{2,1,0:T(8,128)(2,1)}, bf16[4,576,1024]{2,1,0:T(8,128)(2,1)S(1)}, u32[]{:S(2)}) copy-start(bf16[4,576,1024]{2,1,0:T(8,128)(2,1)S(1)} %fusion.35) | copy-start | bytes 14155780
  74.2 80.3 %copy-start.18 = (bf16[4,192,1536]{2,1,0:T(8,128)(2,1)S(1)}, bf16[4,192,1536]{2,1,0:T(8,128)(2,1)}, u32[]{:S(2)}) copy-start(bf16[4,192,1536]{2,1,0:T(8,128)(2,1)} %slice.32) | copy-start | bytes 7077892
  154.5 3.0 copy-start.5
  154.5 3.4 copy-start.22
  157.5 6.0 %copy-start.8 = (bf16[2,512,1536]{2,1,0:T(8,128)(2,1)S(1)}, bf16[2,512,1536]{2,1,0:T(8,128)(2,1)}, u32[]{:S(2)}) copy-start(bf16[2,512,1536]{2,1,0:T(8,128)(2,1)} %copy-done.7) | copy-start | bytes 9437188
  157.5 6.0 %collective-permute-start = (bf16[1024,1536]{1,0:T(8,128)(2,1)S(1)}, bf16[1024,1536]{1,0:T(8,128)(2,1)S(1)}, u32[]{:S(2)}, u32[]{:S(2)}) collective-permute-start(bf16[1024,1536]{1,0:T(8,128)(2,1)S(1)} %convolution_convert_fusion.4), channel_id=1, source_target_pairs={{0,1},{1,0},{2,3},{3,2},{4,5},{5,4},{6,7},{7,6},{8,9},{9,8},{10,11... | collective-permute-start | bytes 9437192 | tf_op jit(solution)/shard_map/ppermute | solution.py:51
  160.2 21.8 %copy-start.13 = (bf16[2,512,1536]{2,1,0:T(8,128)(2,1)}, bf16[2,512,1536]{2,1,0:T(8,128)(2,1)S(1)}, u32[]{:S(2)}) copy-start(bf16[2,512,1536]{2,1,0:T(8,128)(2,1)S(1)} %constant_dynamic-slice_fusion.1) | copy-start | bytes 9437188
  165.1 16.9 %copy-start.9 = (bf16[1024,1536]{1,0:T(8,128)(2,1)}, bf16[1024,1536]{1,0:T(8,128)(2,1)S(1)}, u32[]{:S(2)}) copy-start(bf16[1024,1536]{1,0:T(8,128)(2,1)S(1)} %get-tuple-element.35) | copy-start | bytes 9437188
  213.9 2.7 copy-start.23
  216.6 14.5 %copy-start.24 = (f32[3072,1024]{1,0:T(8,128)S(1)}, f32[3072,1024]{1,0:T(8,128)}, u32[]{:S(2)}) copy-start(f32[3072,1024]{1,0:T(8,128)} %fusion.42) | copy-start | bytes 37748740
  230.9 16.7 %copy-start.10 = (bf16[1024,1536]{1,0:T(8,128)(2,1)S(1)}, bf16[1024,1536]{1,0:T(8,128)(2,1)}, u32[]{:S(2)}) copy-start(bf16[1024,1536]{1,0:T(8,128)(2,1)} %copy-done.9) | copy-start | bytes 9437188
  230.9 16.7 %collective-permute-start.2 = (bf16[1024,1536]{1,0:T(8,128)(2,1)}, bf16[1024,1536]{1,0:T(8,128)(2,1)}, u32[]{:S(2)}, u32[]{:S(2)}) collective-permute-start(bf16[1024,1536]{1,0:T(8,128)(2,1)} %convolution_convert_fusion.2), channel_id=1, source_target_pairs={{0,1},{1,0},{2,3},{3,2},{4,5},{5,4},{6,7},{7,6},{8,9},{9,8},{10,11... | collective-permute-start | bytes 9437192 | tf_op jit(solution)/shard_map/ppermute | solution.py:51
  247.2 6.7 %collective-permute-start.1 = (bf16[1024,1536]{1,0:T(8,128)(2,1)}, bf16[1024,1536]{1,0:T(8,128)(2,1)}, u32[]{:S(2)}, u32[]{:S(2)}) collective-permute-start(bf16[1024,1536]{1,0:T(8,128)(2,1)} %convolution_convert_fusion.3), channel_id=1, source_target_pairs={{0,1},{1,0},{2,3},{3,2},{4,5},{5,4},{6,7},{7,6},{8,9},{9,8},{10,11... | collective-permute-start | bytes 9437192 | tf_op jit(solution)/shard_map/ppermute | solution.py:51
  247.6 6.2 %copy-start.14 = (bf16[2,512,1536]{2,1,0:T(8,128)(2,1)S(1)}, bf16[2,512,1536]{2,1,0:T(8,128)(2,1)}, u32[]{:S(2)}) copy-start(bf16[2,512,1536]{2,1,0:T(8,128)(2,1)} %copy-done.13) | copy-start | bytes 9437188
  253.9 8.2 %copy-start.21 = (bf16[1536]{0:T(1024)(128)(2,1)S(1)}, bf16[1536]{0:T(1024)(128)(2,1)}, u32[]{:S(2)}) copy-start(bf16[1536]{0:T(1024)(128)(2,1)} %param.11) | copy-start | bytes 9220
  262.0 294.3 %all-gather.5.cloned.1.call-start = ((), (), s32[]{:S(2)}) async-start(), calls=%async_computation.1 | async-start | bytes 14155776 | tf_op jit(solution)/shard_map/all_gather | solution.py:726
  262.7 15.8 %copy-start.15 = (bf16[2,512,1536]{2,1,0:T(8,128)(2,1)S(1)}, bf16[2,512,1536]{2,1,0:T(8,128)(2,1)}, u32[]{:S(2)}) copy-start(bf16[2,512,1536]{2,1,0:T(8,128)(2,1)} %copy-done.13) | copy-start | bytes 9437188
  448.3 3.7 copy-start.2
  452.0 101.2 %copy-start.17 = (bf16[4,4,48,1536]{3,2,1,0:T(8,128)(2,1)S(1)}, bf16[4,4,48,1536]{3,2,1,0:T(8,128)(2,1)}, u32[]{:S(2)}) copy-start(bf16[4,4,48,1536]{3,2,1,0:T(8,128)(2,1)} %get-tuple-element.26) | copy-start | bytes 7077892
  556.3 13.0 %copy-start.12 = (bf16[8,512,1536]{2,1,0:T(8,128)(2,1)S(1)}, bf16[8,512,1536]{2,1,0:T(8,128)(2,1)}, u32[]{:S(2)}) copy-start(bf16[8,512,1536]{2,1,0:T(8,128)(2,1)} %all-gather.5.cloned.1.call-done) | copy-start | bytes 37748740
  569.3 5.0 copy-start.16
Sparse Core Ops, SparseCore 0:
  262.2 116.0 all-gather.2
  446.9 66.1 all-gather.4

commit v4 on v3

--- a/solution.py
+++ b/solution.py
@@ -18,33 +18,12 @@
     return jax.nn.gelu(values, approximate=True)
 
 
-def norm_forward(x_rows, gain_vec):
-    x_f32 = x_rows.astype(F32)
-    centered = x_f32 - jnp.mean(x_f32, axis=-1, keepdims=True)
-    inv_std = lax.rsqrt(jnp.mean(centered * centered, axis=-1, keepdims=True) + EPS_NORM)
-    x_hat = centered * inv_std
-    return (x_hat * gain_vec.astype(F32)).astype(BF16), x_hat, inv_std
-
-
-def norm_backward(grad_out, x_hat, inv_std, gain_vec):
-    grad_f32 = grad_out.astype(F32)
-    grad_gain = jnp.sum(grad_f32 * x_hat, axis=0)
-    grad_hat = grad_f32 * gain_vec.astype(F32)
-    mean_one = jnp.mean(grad_hat, axis=-1, keepdims=True)
-    mean_two = jnp.mean(grad_hat * x_hat, axis=-1, keepdims=True)
-    return inv_std * (grad_hat - mean_one - x_hat * mean_two), grad_gain
-
-
 def dot_nt(lhs, rhs):
     return lax.dot_general(lhs, rhs, (((lhs.ndim - 1,), (rhs.ndim - 1,)), ((), ())), preferred_element_type=F32)
 
 
 def dot_tn(lhs, rhs):
     return lax.dot_general(lhs, rhs, (((0,), (0,)), ((), ())), preferred_element_type=F32)
-
-
-def dot_nn(lhs, rhs):
-    return lax.dot_general(lhs, rhs, (((lhs.ndim - 1,), (0,)), ((), ())), preferred_element_type=F32)
 
 
 def core_swap(array):
@@ -131,7 +110,14 @@
         copy.wait_recv()
 
 
+ANY_SPEC = pl.BlockSpec(memory_space=pl.ANY)
+VMEM_SPEC = pl.BlockSpec(memory_space=pltpu.VMEM)
+QKV_ROWS = 576
+OUT_ROWS = 192
 SEQ = 512
+TOKENS = 2 * SEQ
+STEP = 256
+NORM_STEP = 128
 BLOCK = 256
 HEAD = 96
 SCALE = HEAD ** -0.5
@@ -246,73 +232,136 @@
         wait_all(self.whole)
 
 
-def gather_kernel(count, attention, *refs):
-    owns, refs = refs[:count], refs[count:]
-    work = None
-    if attention:
-        work = functools.partial(attention_forward, refs[0], refs[1], refs[2], refs[count + 3])
-        refs = refs[3 : count + 3] + refs[count + 4 :]
-    outs = refs[:count]
-    stage, send_sems, recv_sems, local_sems = refs[count:]
+def norm_stats(x_f32):
+    centered = x_f32 - jnp.mean(x_f32, axis=-1, keepdims=True)
+    inv_std = lax.rsqrt(jnp.mean(centered * centered, axis=-1, keepdims=True) + EPS_NORM)
+    return centered * inv_std, inv_std
+
+
+def token_blocks(body):
+    @pl.loop(0, TOKENS // NORM_STEP)
+    def _(index):
+        body(pl.ds(pl.multiple_of(index * NORM_STEP, NORM_STEP), NORM_STEP))
+
+
+def front_kernel(
+    own_att, own_up, own_down, x_in, gain_a, gain_b, seg, seg_col,
+    w_att, w_up, w_down, qkv_out, attn_out, normed_a_out, x_one_out, normed_b_out,
+    weights, stage, x_one, normed, qkv, attn, part, other, load_sems, send_sems, recv_sems,
+):
     place = Place()
     sender = Sender(place, send_sems, recv_sems)
-    gathers = [WeightGather(place, sender, own, out) for own, out in zip(owns, outs)]
-    loads = [pltpu.make_async_copy(own, stage.at[i], local_sems.at[i]) for i, own in enumerate(owns)]
-    for load in loads:
-        load.start()
-    place.enter()
-    for gather in gathers:
+
+    def copy(source, target, index):
+        started = pltpu.make_async_copy(source, target, load_sems.at[index])
+        started.start()
+        return started
+
+    loads = [copy(x_in, x_one, 0), copy(own_att, weights.at[0], 1), copy(own_up, stage.at[0], 2), copy(own_down, stage.at[1], 3)]
+    place.enter(core=True)
+    att = WeightGather(place, sender, own_att, w_att)
+    mlp = [WeightGather(place, sender, own_up, w_up), WeightGather(place, sender, own_down, w_down)]
+    att.start()
+    att.start_whole()
+    for gather in mlp:
         gather.start()
-    for gather in gathers:
+    for gather in mlp:
         gather.start_whole()
-    stores = []
-    for i in range(count):
-        loads[i].wait()
-        store = pltpu.make_async_copy(stage.at[i], outs[i].at[0], local_sems.at[count + i])
-        store.start()
-        stores.append(store)
-    if work is not None:
-        work(0, 4)
-    for gather in gathers:
+    loads[0].wait()
+
+    def first_norm(rows):
+        x_hat, _ = norm_stats(x_one[rows].astype(F32))
+        normed[rows] = (x_hat * gain_a[...].astype(F32)).astype(BF16)
+
+    token_blocks(first_norm)
+    results = [copy(normed, normed_a_out, 4)]
+    att.second()
+    for load in loads[1:]:
+        load.wait()
+    results += [copy(weights.at[0], w_att.at[0], 5), copy(stage.at[0], w_up.at[0], 6), copy(stage.at[1], w_down.at[0], 7)]
+
+    def project(start, stop):
+        @pl.loop(start, stop)
+        def _(index):
+            block = weights[lax.div(index, 3), lax.rem(index, 3)].reshape(OUT_ROWS, WIDTH)
+            qkv[pl.ds(pl.multiple_of(index * OUT_ROWS, OUT_ROWS), OUT_ROWS)] = dot_rows(block, normed[...]).astype(BF16)
+
+    project(0, 3)
+    att.third()
+    for gather in mlp:
         gather.second()
-    if work is not None:
-        work(4, 10)
-    for gather in gathers:
+    att.finish()
+    others = [copy(w_att.at[shard], weights.at[shard], 7 + shard) for shard in range(1, RING)]
+    for load in others:
+        load.wait()
+    project(3, 12)
+    results.append(copy(qkv, qkv_out, 11))
+    attention_forward(qkv, seg, seg_col, attn, 0, 6)
+    for gather in mlp:
         gather.third()
-    if work is not None:
-        work(10, 16)
-    for gather in gathers:
+    attention_forward(qkv, seg, seg_col, attn, 6, 16)
+    results.append(copy(attn, attn_out, 12))
+    swaps = []
+    for index in range(TOKENS // STEP):
+        rows = pl.ds(index * STEP, STEP)
+        total = None
+        for shard in range(RING):
+            block = weights[shard, 3].reshape(OUT_ROWS, WIDTH)
+            term = dot_cols(attn[shard * OUT_ROWS : (shard + 1) * OUT_ROWS, index * STEP : (index + 1) * STEP], block)
+            total = term if total is None else total + term
+        part[rows] = total.astype(BF16)
+        swaps.append(sender.swap(part.at[rows], other.at[rows]))
+    results[0].wait()
+    wait_all(swaps)
+
+    def second_norm(rows):
+        summed = (part[rows].astype(F32) + other[rows].astype(F32)).astype(BF16)
+        x_new = (x_one[rows].astype(F32) + summed.astype(F32)).astype(BF16)
+        x_one[rows] = x_new
+        x_hat, _ = norm_stats(x_new.astype(F32))
+        normed[rows] = (x_hat * gain_b[...].astype(F32)).astype(BF16)
+
+    token_blocks(second_norm)
+    results += [copy(x_one, x_one_out, 13), copy(normed, normed_b_out, 14)]
+    for gather in mlp:
         gather.finish()
-    for store in stores:
-        store.wait()
+    for result in results[1:]:
+        result.wait()
+    for swap in swaps:
+        swap.wait_send()
     sender.drain()
 
 
-def gather_weights(owns, collective_id, attention=()):
-    count = len(owns)
-    copies = WeightGather.COPIES * count
-    any_spec = pl.BlockSpec(memory_space=pl.ANY)
-    vmem_spec = pl.BlockSpec(memory_space=pltpu.VMEM)
-    out_shape = [jax.ShapeDtypeStruct((RING,) + own.shape, own.dtype) for own in owns]
-    out_specs = [any_spec] * count
-    if attention:
-        rows, tokens = attention[0].shape
-        out_shape.append(jax.ShapeDtypeStruct((rows // 3, tokens), BF16))
-        out_specs.append(vmem_spec)
+def front(own_att, own_up, own_down, x_rows, gain_a, gain_b, seg, seg_col):
+    tokens = (TOKENS, WIDTH)
+    gathered = jax.ShapeDtypeStruct((RING,) + own_att.shape, BF16)
+    rows = jax.ShapeDtypeStruct(tokens, BF16)
+    copies = 3 * WeightGather.COPIES + TOKENS // STEP
     return pl.pallas_call(
-        lambda *refs: gather_kernel(count, bool(attention), *refs),
-        out_shape=out_shape,
-        in_specs=[any_spec] * count + [vmem_spec] * len(attention),
-        out_specs=out_specs,
+        front_kernel,
+        out_shape=[
+            gathered, gathered, gathered,
+            jax.ShapeDtypeStruct((RING * QKV_ROWS, TOKENS), BF16), jax.ShapeDtypeStruct((RING * OUT_ROWS, TOKENS), BF16),
+            rows, rows, rows,
+        ],
+        in_specs=[ANY_SPEC] * 4 + [VMEM_SPEC] * 4,
+        out_specs=[ANY_SPEC] * 8,
         scratch_shapes=[
-            pltpu.VMEM((count,) + owns[0].shape, owns[0].dtype),
+            pltpu.VMEM(gathered.shape, BF16),
+            pltpu.VMEM((2,) + own_att.shape, BF16),
+            pltpu.VMEM(tokens, BF16),
+            pltpu.VMEM(tokens, BF16),
+            pltpu.VMEM((RING * QKV_ROWS, TOKENS), BF16),
+            pltpu.VMEM((RING * OUT_ROWS, TOKENS), BF16),
+            pltpu.VMEM(tokens, BF16),
+            pltpu.VMEM(tokens, BF16),
+            pltpu.SemaphoreType.DMA((15,)),
             pltpu.SemaphoreType.DMA((copies,)),
             pltpu.SemaphoreType.DMA((copies,)),
-            pltpu.SemaphoreType.DMA((2 * count,)),
         ],
-        compiler_params=pltpu.CompilerParams(collective_id=collective_id, has_side_effects=True, vmem_limit_bytes=(40 if attention else 16) << 20),
-        name=f"gather_weights_{collective_id}",
-    )(*owns, *attention)
+        compiler_params=pltpu.CompilerParams(collective_id=1, has_side_effects=True, vmem_limit_bytes=56 << 20),
+        name="front",
+    )(own_att, own_up, own_down, x_rows, gain_a, gain_b, seg, seg_col)
 
 
 ORDERS = (("z", "y", "x", 1), ("y", "x", "z", 0), ("x", "z", "y", 0))
@@ -469,8 +518,6 @@
     return scratch
 
 
-ANY_SPEC = pl.BlockSpec(memory_space=pl.ANY)
-VMEM_SPEC = pl.BlockSpec(memory_space=pltpu.VMEM)
 ATT_WIDTHS = (768, 768)
 MLP_WIDTHS = (640, 512, 384)
 
@@ -510,17 +557,10 @@
     )(grad, gains)
 
 
-QKV_ROWS = 576
-OUT_ROWS = 192
-TOKENS = 2 * SEQ
-STEP = 256
-NORM_STEP = 128
-
-
 def back_kernel(
-    grad_up, grad_down, qkv_in, seg, seg_col, attn, grad_one_in, w_att, normed_in, x_in, gain,
-    out_up, out_down, grad_att, grad_x, gain_grad,
-    qkv, grad_attn, grad_one, normed, w_qkv, w_out, part, other, stage, load_sems, stage_sems,
+    hidden_act, grad_pre, grad_y, normed_b_in, part_b, x_one_in, qkv_in, seg, seg_col, attn, w_att, normed_a_in, x_in, gain_a, gain_b,
+    out_up, out_down, grad_up, grad_down, grad_att, grad_x, gain_grad_a, gain_grad_b,
+    lhs, qkv, grad_attn, grad_one, normed, w_qkv, w_out, part, other, stage, load_sems, lhs_sems, stage_sems, free_sem,
     finals, send_sems, recv_sems, local_sems, *bufs,
 ):
     place = Place()
@@ -536,78 +576,131 @@
         for copy in loads[name]:
             copy.wait()
 
-    load("one", grad_one_in, grad_one, 0)
+    load("one", grad_y, grad_one, 0)
+    load("part", part_b, part, 13)
+    load("normed_b", normed_b_in, normed, 6)
+    load("qkv", qkv_in, qkv, 5)
     for shard in range(RING):
         load("out", w_att.at[shard, pl.ds(QKV_ROWS, OUT_ROWS)], w_out.at[pl.ds(shard * OUT_ROWS, OUT_ROWS)], 1 + shard)
-    load("qkv", qkv_in, qkv, 5)
-    load("normed", normed_in, normed, 6)
     for shard in range(RING):
         load("w", w_att.at[shard, pl.ds(0, QKV_ROWS)], w_qkv.at[pl.ds(shard * QKV_ROWS, QKV_ROWS)], 7 + shard)
     place.enter(core=True)
-    works, planes = grad_works(place, sender, [grad_up, grad_down], MLP_WIDTHS, bufs, finals, [out_up, out_down], local_sems)
-    for work in works:
-        work.start()
-
-    stores = []
-
-    def put(rows, shard, start):
-        slot = len(stores) % 2
-        if len(stores) >= 2:
-            stores[-2].wait()
-        stage[slot] = rows.astype(BF16)
-        copy = pltpu.make_async_copy(stage.at[slot], grad_att.at[shard, pl.ds(start, OUT_ROWS)], stage_sems.at[slot])
-        copy.start()
-        stores.append(copy)
+    works, planes = grad_works(place, sender, [grad_down, grad_up], MLP_WIDTHS, bufs, finals, [out_down, out_up], local_sems)
+    ready("part")
+    early = sender.swap(part, other)
+
+    blocks = RING * RING
+
+    def fetch(source, index, slot):
+        rows = pl.ds(pl.multiple_of(index * OUT_ROWS, OUT_ROWS), OUT_ROWS)
+        return pltpu.make_async_copy(source.at[rows], lhs.at[slot], lhs_sems.at[slot])
+
+    def place_block(target, index, slot):
+        return pltpu.make_async_copy(stage.at[slot], target.at[lax.div(index, RING), lax.rem(index, RING)], stage_sems.at[slot])
+
+    def weight_grad(source, rhs, target):
+        fetch(source, 0, 0).start()
+
+        @pl.loop(0, blocks)
+        def _(index):
+            slot = lax.rem(index, 2)
+            fetch(source, index, slot).wait()
+
+            @pl.when(index + 1 < blocks)
+            def _():
+                fetch(source, index + 1, 1 - slot).start()
+
+            @pl.when(index >= 2)
+            def _():
+                place_block(target, index - 2, slot).wait()
+
+            stage[slot] = dot_plain(lhs[slot], rhs[...]).astype(BF16).reshape(RING, PIECE, WIDTH)
+            place_block(target, index, slot).start()
+
+        for index in (blocks - 2, blocks - 1):
+            place_block(target, index, index % 2).wait()
 
     ready("one")
+    weight_grad(hidden_act, grad_one, grad_down)
+    works[0].start()
+    ready("normed_b")
+    weight_grad(grad_pre, normed, grad_up)
+    works[1].start()
+
+    load("x_one", x_one_in, normed, 14)
+    gain_grad_a[...] = jnp.zeros_like(gain_grad_a)
+    gain_grad_b[...] = jnp.zeros_like(gain_grad_b)
+    early.wait_recv()
+    early.wait_send()
+    ready("x_one")
+
+    def norm_back(rows, gain, gain_grad):
+        x_hat, inv_std = norm_stats(normed[rows].astype(F32))
+        grad = (part[rows].astype(F32) + other[rows].astype(F32)).astype(BF16).astype(F32)
+        gain_grad[...] += jnp.sum(grad * x_hat, axis=0, keepdims=True)
+        grad_hat = grad * gain[...].astype(F32)
+        mean_one = jnp.mean(grad_hat, axis=-1, keepdims=True)
+        mean_two = jnp.mean(grad_hat * x_hat, axis=-1, keepdims=True)
+        back = inv_std * (grad_hat - mean_one - x_hat * mean_two)
+        return (grad_one[rows].astype(F32) + back).astype(BF16)
+
+    def second_norm(rows):
+        grad_one[rows] = norm_back(rows, gain_b, gain_grad_b)
+
+    token_blocks(second_norm)
+    pl.semaphore_signal(free_sem, inc=1, device_id=place.sibling(), device_id_type=MESH_ID)
+    load("normed_a", normed_a_in, normed, 11)
+
     ready("out")
     for shard in range(RING):
         rows = pl.ds(shard * OUT_ROWS, OUT_ROWS)
         grad_attn[rows] = dot_rows(w_out[rows], grad_one[...]).astype(BF16)
     ready("qkv")
-    attention_backward(qkv, seg, seg_col, grad_attn, qkv, 0, 16)
+    attention_backward(qkv, seg, seg_col, grad_attn, qkv, 0, 10)
     works[0].second()
+    attention_backward(qkv, seg, seg_col, grad_attn, qkv, 10, 16)
 
     ready("w")
+    pl.semaphore_wait(free_sem, 1)
     swaps = []
     for index in range(TOKENS // STEP):
         rows = pl.ds(index * STEP, STEP)
         part[rows] = dot_cols(qkv[:, index * STEP : (index + 1) * STEP], w_qkv[...]).astype(BF16)
         swaps.append(sender.swap(part.at[rows], other.at[rows]))
     works[1].second()
+    works[0].third()
+
+    stores = []
+
+    def put(rows, shard, start):
+        slot = len(stores) % 2
+        if len(stores) >= 2:
+            stores[-2].wait()
+        stage[slot] = rows.astype(BF16).reshape(RING, PIECE, WIDTH)
+        copy = pltpu.make_async_copy(stage.at[slot], grad_att.at[shard, start // OUT_ROWS], stage_sems.at[slot])
+        copy.start()
+        stores.append(copy)
+
     for shard in range(RING):
         put(dot_plain(attn[shard * OUT_ROWS : (shard + 1) * OUT_ROWS], grad_one[...]), shard, QKV_ROWS)
-    ready("normed")
+    ready("normed_a")
     for shard in range(RING):
         for block in range(3):
             start = shard * QKV_ROWS + block * OUT_ROWS
             put(dot_plain(qkv[start : start + OUT_ROWS], normed[...]), shard, block * OUT_ROWS)
     for store in stores[-2:]:
         store.wait()
-    load("x", x_in, normed, 11)
-    for work in works:
-        work.third()
+    load("x", x_in, normed, 15)
+    works[1].third()
     ready("x")
-    gain_grad[...] = jnp.zeros_like(gain_grad)
     wait_all(swaps)
     for copy in swaps:
         copy.wait_send()
 
-    @pl.loop(0, TOKENS // NORM_STEP)
-    def _(index):
-        rows = pl.ds(pl.multiple_of(index * NORM_STEP, NORM_STEP), NORM_STEP)
-        x_f32 = normed[rows].astype(F32)
-        centered = x_f32 - jnp.mean(x_f32, axis=-1, keepdims=True)
-        inv_std = lax.rsqrt(jnp.mean(centered * centered, axis=-1, keepdims=True) + EPS_NORM)
-        x_hat = centered * inv_std
-        grad = (part[rows].astype(F32) + other[rows].astype(F32)).astype(BF16).astype(F32)
-        gain_grad[...] += jnp.sum(grad * x_hat, axis=0, keepdims=True)
-        grad_hat = grad * gain[...].astype(F32)
-        mean_one = jnp.mean(grad_hat, axis=-1, keepdims=True)
-        mean_two = jnp.mean(grad_hat * x_hat, axis=-1, keepdims=True)
-        back = inv_std * (grad_hat - mean_one - x_hat * mean_two)
-        part[rows] = (grad_one[rows].astype(F32) + back).astype(BF16)
-
+    def first_norm(rows):
+        part[rows] = norm_back(rows, gain_a, gain_grad_a)
+
+    token_blocks(first_norm)
     result = pltpu.make_async_copy(part, grad_x, load_sems.at[12])
     result.start()
     for work, plane in zip(works, planes):
@@ -621,35 +714,38 @@
     sender.drain()
 
 
-def backward(grad_up, grad_down, qkv_t, seg, seg_col, attn, grad_one, w_att, normed, x_rows, gain):
+def backward(*operands):
     tokens = (TOKENS, WIDTH)
+    piece = jax.ShapeDtypeStruct((RING, RING, PIECE, WIDTH), BF16)
+    grid = jax.ShapeDtypeStruct((RING, RING, RING, PIECE, WIDTH), BF16)
     return pl.pallas_call(
         back_kernel,
         out_shape=[
-            jax.ShapeDtypeStruct(grad_up.shape[1:], BF16),
-            jax.ShapeDtypeStruct(grad_down.shape[1:], BF16),
-            jax.ShapeDtypeStruct(w_att.shape, BF16),
+            piece, piece, grid, grid, grid,
             jax.ShapeDtypeStruct(tokens, BF16),
-            jax.ShapeDtypeStruct((1, WIDTH), F32),
+            jax.ShapeDtypeStruct((1, WIDTH), F32), jax.ShapeDtypeStruct((1, WIDTH), F32),
         ],
-        in_specs=[ANY_SPEC, ANY_SPEC, ANY_SPEC, VMEM_SPEC, VMEM_SPEC, VMEM_SPEC, ANY_SPEC, ANY_SPEC, ANY_SPEC, ANY_SPEC, VMEM_SPEC],
-        out_specs=[ANY_SPEC, ANY_SPEC, ANY_SPEC, ANY_SPEC, VMEM_SPEC],
+        in_specs=[ANY_SPEC] * 7 + [VMEM_SPEC] * 3 + [ANY_SPEC] * 3 + [VMEM_SPEC] * 2,
+        out_specs=[ANY_SPEC] * 6 + [VMEM_SPEC] * 2,
         scratch_shapes=[
-            pltpu.VMEM(qkv_t.shape, BF16),
-            pltpu.VMEM(attn.shape, BF16),
+            pltpu.VMEM((2, OUT_ROWS, TOKENS), BF16),
+            pltpu.VMEM((RING * QKV_ROWS, TOKENS), BF16),
+            pltpu.VMEM((RING * OUT_ROWS, TOKENS), BF16),
             pltpu.VMEM(tokens, BF16),
             pltpu.VMEM(tokens, BF16),
             pltpu.VMEM((RING * QKV_ROWS, WIDTH), BF16),
             pltpu.VMEM((RING * OUT_ROWS, WIDTH), BF16),
             pltpu.VMEM(tokens, BF16),
             pltpu.VMEM(tokens, BF16),
-            pltpu.VMEM((2, OUT_ROWS, WIDTH), BF16),
-            pltpu.SemaphoreType.DMA((13,)),
+            pltpu.VMEM((2, RING, PIECE, WIDTH), BF16),
+            pltpu.SemaphoreType.DMA((16,)),
             pltpu.SemaphoreType.DMA((2,)),
-        ] + comm_scratch(2, MLP_WIDTHS, TOKENS // STEP),
+            pltpu.SemaphoreType.DMA((2,)),
+            pltpu.SemaphoreType.REGULAR,
+        ] + comm_scratch(2, MLP_WIDTHS, TOKENS // STEP + 1),
         compiler_params=pltpu.CompilerParams(collective_id=3, has_side_effects=True, vmem_limit_bytes=67043328),
         name="backward",
-    )(grad_up, grad_down, qkv_t, seg, seg_col, attn, grad_one, w_att, normed, x_rows, gain)
+    )(*operands)
 
 
 def solution(mesh):
@@ -674,29 +770,18 @@
         own_att = grid_of(jnp.concatenate([w_qkv.T, w_out.reshape(heads_loc * head_dim, hidden)], axis=0))
         own_up = grid_of(w_up.T)
         own_down = grid_of(w_down)
-        (w_att,) = gather_weights([own_att], 1)
-        w_att = w_att.reshape(RING, shard_rows, hidden)
-        w_qkv_t = w_att[:, :qkv_cols]
-        w_out_all = w_att[:, qkv_cols:].reshape(RING * heads_loc * head_dim, hidden)
-
         x_rows = own_rows(x_in).reshape(tokens, hidden)
         seg_rows = own_rows(seg_ids)
+        seg_row, seg_col = seg_rows[:, None, :], seg_rows[:, :, None]
         grad_rows = own_rows(grad_y).reshape(tokens, hidden)
-        seg_row, seg_col = seg_rows[:, None, :], seg_rows[:, :, None]
-        normed_a, _, _ = norm_forward(x_rows, gain_one)
-        qkv_t = dot_nt(w_qkv_t, normed_a).astype(BF16)
-        qkv_t = qkv_t.reshape(RING * qkv_cols, tokens)
-        up_t, down, attn_flat = gather_weights([own_up, own_down], 2, (qkv_t, seg_row, seg_col))
+        w_att, up_t, down, qkv_t, attn_flat, normed_a, x_one, normed_b = front(
+            own_att, own_up, own_down, x_rows, gain_one[None], gain_two[None], seg_row, seg_col)
         up_t = up_t.reshape(RING * shard_rows, hidden)
         down = down.reshape(RING * shard_rows, hidden)
 
         def pair_sum(part):
             return part.astype(F32) + core_swap(part).astype(F32)
 
-        part_one = dot_tn(attn_flat, w_out_all).astype(BF16)
-        sum_one = pair_sum(part_one).astype(BF16)
-        x_one = (x_rows.astype(F32) + sum_one.astype(F32)).astype(BF16)
-        normed_b, hat_b, inv_b = norm_forward(x_one, gain_two)
         pre_act = dot_nt(up_t, normed_b)
         act_val, gelu_pull = jax.vjp(gelu_tanh, pre_act)
         hidden_act = act_val.astype(BF16)
@@ -707,17 +792,12 @@
         grad_hidden = dot_nt(down, grad_rows).astype(BF16)
         grad_pre = gelu_pull(grad_hidden.astype(F32))[0].astype(BF16)
 
-        grid_shape = (RING, RING, RING, PIECE, hidden)
-        grad_down_w = dot_nn(hidden_act, grad_rows).astype(BF16).reshape(grid_shape)
-        grad_up_w = dot_nn(grad_pre, normed_b).astype(BF16).reshape(grid_shape)
         part_b = dot_tn(grad_pre, up_t).astype(BF16)
-        grad_norm_b = pair_sum(part_b).astype(BF16)
-        back_b, gain_grad_two = norm_backward(grad_norm_b, hat_b, inv_b, gain_two)
-        grad_x_one = (grad_rows.astype(F32) + back_b).astype(BF16)
-        grad_up_own, grad_down_own, grad_att, grad_x, gain_grad_one = backward(
-            grad_up_w, grad_down_w, qkv_t, seg_row, seg_col, attn_flat, grad_x_one, w_att, normed_a, x_rows, gain_one[None])
-        gains = jnp.concatenate([gain_grad_one, gain_grad_two[None], jnp.zeros((6, hidden), F32)], axis=0)
-        grad_att_own, gains = scatter_last(grad_att.reshape(grid_shape), gains)
+        grad_up_own, grad_down_own, _, _, grad_att, grad_x, gain_grad_one, gain_grad_two = backward(
+            hidden_act, grad_pre, grad_rows, normed_b, part_b, x_one, qkv_t, seg_row, seg_col, attn_flat,
+            w_att.reshape(RING, shard_rows, hidden), normed_a, x_rows, gain_one[None], gain_two[None])
+        gains = jnp.concatenate([gain_grad_one, gain_grad_two, jnp.zeros((6, hidden), F32)], axis=0)
+        grad_att_own, gains = scatter_last(grad_att, gains)
         grad_att_own = grad_att_own.reshape(shard_rows, hidden)
 
         def spread(rows):

time: 586 us -> 578 us (0.986)
  matrix products: 121 us -> 73.5 us
  Pallas kernels: 376 us -> 421 us
  other arithmetic: 21.8 us -> 4.55 us
  waiting for transfers between devices: 3.36 us -> 9.56 us
    dot_general x2 -> x0, matrix products: 32 us -> none  [dot_nn(): lax.dot_general(lhs, rhs, (((lhs.ndim - 1,), (0,)), ((), ())), preferred_...]
    pallas_call x3 -> x2, Pallas kernels: 277 us -> 305 us  [the longest x1 176 us: backward(): pl.pallas_call(back_kernel, out_shape=[piece, piece, grid, grid, grid, ja...]
    pallas_call x1, Pallas kernels: 99 us -> 116 us  [scatter_last(): pl.pallas_call(last_kernel, out_shape=[jax.ShapeDtypeStruct(grad.shape[1:...]
    dot_general x3 -> x2, matrix products: 55.5 us -> 42.8 us  [dot_nt(): lax.dot_general(lhs, rhs, (((lhs.ndim - 1,), (rhs.ndim - 1,)), ((), ())),...]
    reduce_sum x5 -> x0, other arithmetic: 12.3 us -> none  [the longest x1 6.23 us: norm_backward(): grad_gain = jnp.sum(grad_f32 * x_hat, axis=0)]
    convert_element_type x4 -> x1, other arithmetic: 8.6 us -> 1.24 us  [local_step(): y_rows = (x_one.astype(F32) + sum_two.astype(F32)).astype(BF16)]
    unnamed x55 -> x19, local copies, waits for them, and re-layouts: 25.9 us -> 23.1 us
    dot_general x3 -> x2, matrix products: 33.4 us -> 30.6 us  [dot_tn(): lax.dot_general(lhs, rhs, (((0,), (0,)), ((), ())), preferred_element_typ...]
  transfers between devices with their start and end apart: 5 -> 3, of which waited for: 1 -> 2; matrix products, arithmetic and copies ran while one was open for 11% -> 4% of each run, Pallas kernels for 43% -> 20%
where the time goes in v4:
time: 578 us; the launch traced here: 570 us
  Pallas kernels  421 us (73%)
  matrix products  73.5 us (13%)
  local copies, waits for them, and re-layouts  47.2 us (8%)
  between operations  14.4 us (2%)
  waiting for transfers between devices  9.56 us (2%)
    pallas_call x1, Pallas kernels, backward(): pl.pallas_call(back_kernel, out_shape=[piece, piece, grid, grid, grid, ja...  176 us
    pallas_call x1, Pallas kernels, front(): pl.pallas_call(front_kernel, out_shape=[gathered, gathered, gathered, jax...  129 us
    pallas_call x1, Pallas kernels, scatter_last(): pl.pallas_call(last_kernel, out_shape=[jax.ShapeDtypeStruct(grad.shape[1:...  116 us
    dot_general x2, matrix products, dot_nt(): lax.dot_general(lhs, rhs, (((lhs.ndim - 1,), (rhs.ndim - 1,)), ((), ())),...  42.8 us
    dot_general x2, matrix products, dot_tn(): lax.dot_general(lhs, rhs, (((0,), (0,)), ((), ())), preferred_element_typ...  30.6 us
    unnamed x19, local copies, waits for them, and re-layouts  23.1 us
  transfers between devices with their start and end apart: 3, of which 2 were waited for; matrix products, arithmetic and copies ran while one was open for 4% of the time, Pallas kernels for 20%

profile of v4, /device:TPU:0, one launch (start us, length us, event | category | flops | bytes accessed | tf_op | source)
XLA Modules:
  0.0 570.2 jit_solution(954789896029408256)
XLA Ops:
  7.2 0.7 fusion.18
  8.0 0.7 constant_dynamic-slice_fusion.3
  8.7 0.6 broadcast_in_dim.19.seg
  9.3 1.3 broadcast_in_dim.17.gain_a
  10.6 1.3 broadcast_in_dim.18.gain_b
  11.9 1.0 copy.24.seg_col
  12.9 4.3 copy.23
  17.2 3.2 pad_maximum_fusion
  20.4 4.9 constant_dynamic-slice_fusion.1
  25.3 128.9 %front.1 = (bf16[4,4,4,48,1536]{4,3,2,1,0:T(8,128)(2,1)}, bf16[4,4,4,48,1536]{4,3,2,1,0:T(8,128)(2,1)}, bf16[4,4,4,48,1536]{4,3,2,1,0:T(8,128)(2,1)}, bf16[2304,...) custom-call(bf16[4,4,48,1536]{3,2,1,0:T(8,128)(2,1)} %bitcast.35, ...), custom_call_target="tpu_custom_call" | custom-call | tf_op jit(solution)/shard_map/front/pallas_call | solution.py:340
  154.2 19.8 %multiply_convert_fusion = (bf16[3072,1024]{1,0:T(8,128)(2,1)}, f32[3072,1024]{1,0:T(8,128)}) fusion(bf16[3072,1536]{1,0:T(8,128)(2,1)} %bitcast.50, bf16[1024,1536]{1,0:T(8,128)(2,1)} %get-tuple-element.26.normed_b_in), kind=kOutput, calls=%fused_computation.14 | convolution fusion | flops 9691987968 | bytes 31457280 | tf_op jit(solution)/shard_map/dot_general | solution.py:22
  174.0 23.0 %fusion.2.grad_pre = bf16[3072,1024]{1,0:T(8,128)(2,1)} fusion(f32[3072,1024]{1,0:T(8,128)} %get-tuple-element.43, bf16[3072,1536]{1,0:T(8,128)(2,1)} %bitcast.48, bf16[1024,1536]{1,0:T(8,128)(2,1)S(1)} %bitcast.32), kind=kOutput, calls=%fused_computation.6 | convolution fusion | flops 9732882432 | bytes 31457280 | tf_op jit(solution)/shard_map/dot_general | solution.py:22
  197.0 16.1 %convolution_convert_fusion.part_b = bf16[1024,1536]{1,0:T(8,128)(2,1)} fusion(bf16[3072,1024]{1,0:T(8,128)(2,1)} %fusion.2.grad_pre, bf16[3072,1536]{1,0:T(8,128)(2,1)} %bitcast.51), kind=kOutput, calls=%fused_computation.17 | convolution fusion | flops 9665249280 | bytes 18874368 | tf_op jit(solution)/shard_map/dot_general | solution.py:26
  213.2 176.1 %backward.1 = (bf16[4,4,48,1536]{3,2,1,0:T(8,128)(2,1)}, bf16[4,4,48,1536]{3,2,1,0:T(8,128)(2,1)}, bf16[4,4,4,48,1536]{4,3,2,1,0:T(8,128)(2,1)}, bf16[4,4,4,48,1...) custom-call(bf16[3072,1024]{1,0:T(8,128)(2,1)} %get-tuple-element.42, ...), custom_call_target="tpu_custom_call" | custom-call | tf_op jit(solution)/shard_map/backward/pallas_call | solution.py:721
  389.3 2.7 constant_dynamic-slice_fusion
  392.0 14.5 %convolution_convert_fusion.1 = bf16[1024,1536]{1,0:T(8,128)(2,1)S(1)} fusion(bf16[3072,1024]{1,0:T(8,128)(2,1)} %get-tuple-element.42.hidden_act, bf16[3072,1536]{1,0:T(8,128)(2,1)} %bitcast.49), kind=kOutput, calls=%fused_computation.18 | convolution fusion | flops 9665249280 | bytes 18874368 | tf_op jit(solution)/shard_map/dot_general | solution.py:26
  406.5 0.1 collective-permute-start
  406.6 6.7 %collective-permute-done = bf16[1024,1536]{1,0:T(8,128)(2,1)S(1)} collective-permute-done((bf16[1024,1536]{1,0:T(8,128)(2,1)S(1)}, bf16[1024,1536]{1,0:T(8,128)(2,1)S(1)}, u32[]{:S(2)}, u32[]{:S(2)}) %collective-permute-start) | collective-permute-done | bytes 3145760 | tf_op jit(solution)/shard_map/ppermute | solution.py:30
  413.3 1.2 add_convert_fusion
  414.6 1.3 constant_dynamic-slice_fusion.2
  415.9 0.1 pad.2.clone
  416.0 3.7 copy-done
  419.7 115.9 %scatter_last.1 = (bf16[4,4,48,1536]{3,2,1,0:T(8,128)(2,1)S(1)}, f32[8,1536]{1,0:T(8,128)S(1)}) custom-call(bf16[4,4,4,48,1536]{4,3,2,1,0:T(8,128)(2,1)S(1)} %copy-done, f32[8,1536]{1,0:T(8,128)S(1)} %maximum_maximum_fusion.gain_in), custom_call_target="tpu_custom_call" | custom-call | tf_op jit(solution)/shard_map/scatter_last/pallas_call | solution.py:549
  535.6 0.9 slice.22
  536.5 1.4 slice.20
  537.9 2.4 copy.26
  540.3 0.6 slice_reduce_fusion
  540.9 2.8 all-gather.3.cloned.1.call-done
  543.7 11.0 %copy.30 = bf16[8,512,1536]{2,1,0:T(8,128)(2,1)} copy(bf16[8,512,1536]{2,1,0:T(8,128)(2,1)} %all-gather.3.cloned.1.call-done) | data formatting | bytes 25165824
  554.7 2.0 copy-done.1
  556.7 5.0 copy.31
  561.7 1.4 copy.32
  (22 shorter events, 0.2 us)
Async XLA Ops:
  7.2 533.8 %all-gather.5.cloned.1.call-start = ((), (), s32[]{:S(2)}) async-start(), calls=%async_computation.1 | async-start | bytes 14155776 | tf_op jit(solution)/shard_map/all_gather | solution.py:806
  25.3 148.8 %copy-start.3 = (bf16[2,512,1536]{2,1,0:T(8,128)(2,1)}, bf16[2,512,1536]{2,1,0:T(8,128)(2,1)S(1)}, u32[]{:S(2)}) copy-start(bf16[2,512,1536]{2,1,0:T(8,128)(2,1)S(1)} %get-tuple-element.44) | copy-start | bytes 9437188
  391.9 21.4 %copy-start.2 = (bf16[1024,1536]{1,0:T(8,128)(2,1)S(1)}, bf16[1024,1536]{1,0:T(8,128)(2,1)}, u32[]{:S(2)}) copy-start(bf16[1024,1536]{1,0:T(8,128)(2,1)} %get-tuple-element.24.x_one_in) | copy-start | bytes 9437188
  391.9 151.8 %all-gather.3.cloned.1.call-start = ((), (), s32[]{:S(2)}) async-start(), calls=%async_computation | async-start | bytes 14155776 | tf_op jit(solution)/shard_map/all_gather | solution.py:806
  406.5 9.5 %copy-start.6 = (f32[1,1536]{1,0:T(1,128)S(1)}, f32[1,1536]{1,0:T(1,128)}, u32[]{:S(2)}) copy-start(f32[1,1536]{1,0:T(1,128)} %get-tuple-element.34) | copy-start | bytes 18436
  406.5 9.5 %copy-start.7 = (f32[1,1536]{1,0:T(1,128)S(1)}, f32[1,1536]{1,0:T(1,128)}, u32[]{:S(2)}) copy-start(f32[1,1536]{1,0:T(1,128)} %get-tuple-element.35) | copy-start | bytes 18436
  406.5 6.8 %collective-permute-start = (bf16[1024,1536]{1,0:T(8,128)(2,1)S(1)}, bf16[1024,1536]{1,0:T(8,128)(2,1)S(1)}, u32[]{:S(2)}, u32[]{:S(2)}) collective-permute-start(bf16[1024,1536]{1,0:T(8,128)(2,1)S(1)} %convolution_convert_fusion.1), channel_id=1, source_target_pairs={{0,1},{1,0},{2,3},{3,2},{4,5},{5,4},{6,7},{7,6},{8,9},{9,8},{10,11... | collective-permute-start | bytes 9437192 | tf_op jit(solution)/shard_map/ppermute | solution.py:30
  414.6 123.3 %copy-start.5 = (bf16[4,4,48,1536]{3,2,1,0:T(8,128)(2,1)S(1)}, bf16[4,4,48,1536]{3,2,1,0:T(8,128)(2,1)}, u32[]{:S(2)}) copy-start(bf16[4,4,48,1536]{3,2,1,0:T(8,128)(2,1)} %get-tuple-element.38) | copy-start | bytes 7077892
  416.0 3.7 copy-start
  543.7 13.0 %copy-start.1 = (bf16[8,512,1536]{2,1,0:T(8,128)(2,1)S(1)}, bf16[8,512,1536]{2,1,0:T(8,128)(2,1)}, u32[]{:S(2)}) copy-start(bf16[8,512,1536]{2,1,0:T(8,128)(2,1)} %all-gather.5.cloned.1.call-done) | copy-start | bytes 37748740
  556.7 5.0 copy-start.4
Sparse Core Ops, SparseCore 0:
  392.1 63.6 all-gather.4
  458.1 85.6 all-gather.2

commit v5 on v4

--- a/solution.py
+++ b/solution.py
@@ -64,10 +64,13 @@
         barrier = pltpu.get_barrier_semaphore()
         if core:
             pl.semaphore_signal(barrier, inc=1, device_id=self.sibling(), device_id_type=MESH_ID)
+        self.signal_rings(barrier)
+        pl.semaphore_wait(barrier, 9 + core)
+
+    def signal_rings(self, semaphore):
         for axis in "xyz":
             for step in range(1, RING):
-                pl.semaphore_signal(barrier, inc=1, device_id=self.peer(axis, step), device_id_type=MESH_ID)
-        pl.semaphore_wait(barrier, 9 + core)
+                pl.semaphore_signal(semaphore, inc=1, device_id=self.peer(axis, step), device_id_type=MESH_ID)
 
 
 class Sender:
@@ -99,6 +102,12 @@
         copy.start()
         self.used += 1
         return copy
+
+    def settle(self, copies):
+        for copy in copies:
+            copy.wait_send()
+        done = {id(copy) for copy in copies}
+        self.copies = [copy for copy in self.copies if id(copy) not in done]
 
     def drain(self):
         for copy in self.copies:
@@ -505,63 +514,14 @@
     return works, planes
 
 
-def comm_scratch(count, widths, extra):
-    copies = (9 * len(widths) + PlaneGather.COPIES) * count + extra
-    scratch = [
-        pltpu.VMEM((count, PIECE, WIDTH), BF16),
-        pltpu.SemaphoreType.DMA((copies,)),
-        pltpu.SemaphoreType.DMA((copies,)),
-        pltpu.SemaphoreType.DMA((count, 4)),
-    ]
-    for _ in range(count):
-        scratch += GradScatter.scratch(widths)
-    return scratch
-
-
-ATT_WIDTHS = (768, 768)
-MLP_WIDTHS = (640, 512, 384)
-
-
-def last_kernel(grad, gain_in, out, gain_out, gains, gain_bufs, finals, send_sems, recv_sems, local_sems, *bufs):
-    place = Place()
-    sender = Sender(place, send_sems, recv_sems)
-    place.enter()
-    (work,), (plane,) = grad_works(place, sender, [grad], ATT_WIDTHS, bufs, finals, [out], local_sems)
-    gains[0] = gain_in[...]
-    gain_finish = gain_step(place, sender, gains, gain_bufs, 0, "z")
-    work.start()
-    gain_finish()
-    gain_finish = gain_step(place, sender, gains, gain_bufs, 1, "y")
-    work.second()
-    gain_finish()
-    gain_finish = gain_step(place, sender, gains, gain_bufs, 2, "x")
-    work.third()
-    work.finish()
-    plane.start()
-    gain_finish()
-    gain_out[...] = gains[3]
-    plane.second()
-    plane.finish()
-    sender.drain()
-
-
-def scatter_last(grad, gains):
-    return pl.pallas_call(
-        last_kernel,
-        out_shape=[jax.ShapeDtypeStruct(grad.shape[1:], BF16), jax.ShapeDtypeStruct(gains.shape, F32)],
-        in_specs=[ANY_SPEC, VMEM_SPEC],
-        out_specs=[ANY_SPEC, VMEM_SPEC],
-        scratch_shapes=[pltpu.VMEM((4,) + gains.shape, F32), pltpu.VMEM((3, 3) + gains.shape, F32)] + comm_scratch(1, ATT_WIDTHS, 9),
-        compiler_params=pltpu.CompilerParams(collective_id=4, has_side_effects=True, vmem_limit_bytes=32 << 20),
-        name="scatter_last",
-    )(grad, gains)
+WIDTHS = (640, 640, 256)
 
 
 def back_kernel(
     hidden_act, grad_pre, grad_y, normed_b_in, part_b, x_one_in, qkv_in, seg, seg_col, attn, w_att, normed_a_in, x_in, gain_a, gain_b,
-    out_up, out_down, grad_up, grad_down, grad_att, grad_x, gain_grad_a, gain_grad_b,
-    lhs, qkv, grad_attn, grad_one, normed, w_qkv, w_out, part, other, stage, load_sems, lhs_sems, stage_sems, free_sem,
-    finals, send_sems, recv_sems, local_sems, *bufs,
+    out_up, out_down, out_att, grad_up, grad_down, grad_att, grad_x, gain_out,
+    lhs, qkv, grad_attn, grad_one, normed, w_qkv, w_out, part, other, stage, load_sems, lhs_sems, stage_sems, free_sem, ring_sem,
+    gain_grad_a, gain_grad_b, gains, gain_bufs, finals, send_sems, recv_sems, local_sems, *bufs,
 ):
     place = Place()
     sender = Sender(place, send_sems, recv_sems)
@@ -585,7 +545,11 @@
     for shard in range(RING):
         load("w", w_att.at[shard, pl.ds(0, QKV_ROWS)], w_qkv.at[pl.ds(shard * QKV_ROWS, QKV_ROWS)], 7 + shard)
     place.enter(core=True)
-    works, planes = grad_works(place, sender, [grad_down, grad_up], MLP_WIDTHS, bufs, finals, [out_down, out_up], local_sems)
+    works, planes = grad_works(place, sender, [grad_down, grad_up], WIDTHS, bufs, finals, [out_down, out_up], local_sems)
+    tail = bufs[8 * len(WIDTHS) :]
+    reused = [(works[0].bufs[part][0], works[0].bufs[part][1]) + tuple(tail[2 * part : 2 * part + 2]) for part in range(len(WIDTHS))]
+    att_work = GradScatter(place, sender, grad_att, WIDTHS, reused, finals.at[2], local_sems.at[2])
+    att_plane = PlaneGather(place, sender, finals.at[2], out_att, local_sems.at[2, 3])
     ready("part")
     early = sender.swap(part, other)
 
@@ -658,6 +622,7 @@
     ready("qkv")
     attention_backward(qkv, seg, seg_col, grad_attn, qkv, 0, 10)
     works[0].second()
+    place.signal_rings(ring_sem)
     attention_backward(qkv, seg, seg_col, grad_attn, qkv, 10, 16)
 
     ready("w")
@@ -691,6 +656,9 @@
     for store in stores[-2:]:
         store.wait()
     load("x", x_in, normed, 15)
+    sender.settle([copy for copies in works[0].two.values() for copy in copies])
+    pl.semaphore_wait(ring_sem, 9)
+    att_work.start()
     works[1].third()
     ready("x")
     wait_all(swaps)
@@ -701,16 +669,47 @@
         part[rows] = norm_back(rows, gain_a, gain_grad_a)
 
     token_blocks(first_norm)
-    result = pltpu.make_async_copy(part, grad_x, load_sems.at[12])
-    result.start()
+    row_of = lambda step: 2 * place.ahead("x", RING - step) + place.core
+    mine = part.at[pl.ds(pl.multiple_of(place.core * SEQ, SEQ), SEQ)]
+    rows_sent = sender.ring("x", lambda step: mine, lambda step: grad_x.at[row_of(0)])
+    results = []
+    for i in range(2):
+        result = pltpu.make_async_copy(part.at[pl.ds(i * SEQ, SEQ)], grad_x.at[2 * place.pos["x"] + i], load_sems.at[12 + 4 * i])
+        result.start()
+        results.append(result)
+    gains[0] = jnp.zeros_like(gain_out)
+    gains[0, 0:1] = gain_grad_a[...]
+    gains[0, 1:2] = gain_grad_b[...]
+    gain_finish = gain_step(place, sender, gains, gain_bufs, 0, "z")
     for work, plane in zip(works, planes):
         work.finish()
         plane.start()
+    gain_finish()
+    gain_finish = gain_step(place, sender, gains, gain_bufs, 1, "y")
+    att_work.second()
     for plane in planes:
         plane.second()
+    gain_finish()
+    gain_finish = gain_step(place, sender, gains, gain_bufs, 2, "x")
+    att_work.third()
+    passed = []
+    for step, copy in zip(range(1, RING), rows_sent):
+        copy.wait_recv()
+        row = grad_x.at[row_of(step)]
+        passed.append(sender.swap(row, row))
+    att_work.finish()
+    att_plane.start()
+    gain_finish()
+    gain_out[...] = gains[3]
     for plane in planes:
         plane.finish()
-    result.wait()
+    att_plane.second()
+    att_plane.finish()
+    wait_all(passed)
+    for copy in passed:
+        copy.wait_send()
+    for result in results:
+        result.wait()
     sender.drain()
 
 
@@ -718,15 +717,17 @@
     tokens = (TOKENS, WIDTH)
     piece = jax.ShapeDtypeStruct((RING, RING, PIECE, WIDTH), BF16)
     grid = jax.ShapeDtypeStruct((RING, RING, RING, PIECE, WIDTH), BF16)
+    copies = 3 * (9 * len(WIDTHS) + PlaneGather.COPIES) + TOKENS // STEP + 1 + 9 + 6
+    tail = [shape for part in range(len(WIDTHS)) for shape in GradScatter.scratch(WIDTHS)[4 * part + 2 : 4 * part + 4]]
     return pl.pallas_call(
         back_kernel,
         out_shape=[
-            piece, piece, grid, grid, grid,
-            jax.ShapeDtypeStruct(tokens, BF16),
-            jax.ShapeDtypeStruct((1, WIDTH), F32), jax.ShapeDtypeStruct((1, WIDTH), F32),
+            piece, piece, piece, grid, grid, grid,
+            jax.ShapeDtypeStruct((2 * RING, SEQ, WIDTH), BF16),
+            jax.ShapeDtypeStruct((8, WIDTH), F32),
         ],
         in_specs=[ANY_SPEC] * 7 + [VMEM_SPEC] * 3 + [ANY_SPEC] * 3 + [VMEM_SPEC] * 2,
-        out_specs=[ANY_SPEC] * 6 + [VMEM_SPEC] * 2,
+        out_specs=[ANY_SPEC] * 7 + [VMEM_SPEC],
         scratch_shapes=[
             pltpu.VMEM((2, OUT_ROWS, TOKENS), BF16),
             pltpu.VMEM((RING * QKV_ROWS, TOKENS), BF16),
@@ -738,11 +739,20 @@
             pltpu.VMEM(tokens, BF16),
             pltpu.VMEM(tokens, BF16),
             pltpu.VMEM((2, RING, PIECE, WIDTH), BF16),
-            pltpu.SemaphoreType.DMA((16,)),
+            pltpu.SemaphoreType.DMA((17,)),
             pltpu.SemaphoreType.DMA((2,)),
             pltpu.SemaphoreType.DMA((2,)),
             pltpu.SemaphoreType.REGULAR,
-        ] + comm_scratch(2, MLP_WIDTHS, TOKENS // STEP + 1),
+            pltpu.SemaphoreType.REGULAR,
+            pltpu.VMEM((1, WIDTH), F32),
+            pltpu.VMEM((1, WIDTH), F32),
+            pltpu.VMEM((4, 8, WIDTH), F32),
+            pltpu.VMEM((3, 3, 8, WIDTH), F32),
+            pltpu.VMEM((3, PIECE, WIDTH), BF16),
+            pltpu.SemaphoreType.DMA((copies,)),
+            pltpu.SemaphoreType.DMA((copies,)),
+            pltpu.SemaphoreType.DMA((3, 4)),
+        ] + GradScatter.scratch(WIDTHS) + GradScatter.scratch(WIDTHS) + tail,
         compiler_params=pltpu.CompilerParams(collective_id=3, has_side_effects=True, vmem_limit_bytes=67043328),
         name="backward",
     )(*operands)
@@ -793,11 +803,10 @@
         grad_pre = gelu_pull(grad_hidden.astype(F32))[0].astype(BF16)
 
         part_b = dot_tn(grad_pre, up_t).astype(BF16)
-        grad_up_own, grad_down_own, _, _, grad_att, grad_x, gain_grad_one, gain_grad_two = backward(
+        part_b, y_rows = lax.optimization_barrier((part_b, y_rows))
+        grad_up_own, grad_down_own, grad_att_own, _, _, _, grad_x, gains = backward(
             hidden_act, grad_pre, grad_rows, normed_b, part_b, x_one, qkv_t, seg_row, seg_col, attn_flat,
             w_att.reshape(RING, shard_rows, hidden), normed_a, x_rows, gain_one[None], gain_two[None])
-        gains = jnp.concatenate([gain_grad_one, gain_grad_two, jnp.zeros((6, hidden), F32)], axis=0)
-        grad_att_own, gains = scatter_last(grad_att, gains)
         grad_att_own = grad_att_own.reshape(shard_rows, hidden)
 
         def spread(rows):
@@ -807,7 +816,7 @@
 
         return (
             spread(y_rows),
-            spread(grad_x),
+            grad_x,
             gains[0].astype(BF16),
             gains[1].astype(BF16),
             grad_att_own[:qkv_cols].T,

time: 578 us -> 546 us (0.945)
  Pallas kernels: 421 us -> 399 us
  waiting for transfers between devices: 9.56 us -> 0.02 us
    pallas_call x2 -> x1, Pallas kernels: 292 us -> 270 us  [backward(): pl.pallas_call(back_kernel, out_shape=[piece, piece, piece, grid, grid, g...]
    ppermute x1, waiting for transfers between devices: 6.72 us -> 0.01 us  [core_swap(): return lax.ppermute(array, 'tp', [(i, i ^ 1) for i in range(8)])]
    unnamed x19 -> x17, local copies, waits for them, and re-layouts: 23.1 us -> 22.6 us
  transfers between devices with their start and end apart: 3 -> 2, of which waited for: 2 -> 0; matrix products, arithmetic and copies ran while one was open for 4% -> 9% of each run, Pallas kernels for 20% -> 50%
where the time goes in v5:
time: 546 us; the launch traced here: 540 us
  Pallas kernels  399 us (73%)
  matrix products  72.8 us (13%)
  local copies, waits for them, and re-layouts  48.4 us (9%)
  between operations  14.6 us (3%)
    pallas_call x1, Pallas kernels, backward(): pl.pallas_call(back_kernel, out_shape=[piece, piece, piece, grid, grid, g...  270 us
    pallas_call x1, Pallas kernels, front(): pl.pallas_call(front_kernel, out_shape=[gathered, gathered, gathered, jax...  129 us
    dot_general x2, matrix products, dot_nt(): lax.dot_general(lhs, rhs, (((lhs.ndim - 1,), (rhs.ndim - 1,)), ((), ())),...  42.3 us
    dot_general x2, matrix products, dot_tn(): lax.dot_general(lhs, rhs, (((0,), (0,)), ((), ())), preferred_element_typ...  30.5 us
    unnamed x17, local copies, waits for them, and re-layouts  22.6 us
  transfers between devices with their start and end apart: 2, of which 0 were waited for; matrix products, arithmetic and copies ran while one was open for 9% of the time, Pallas kernels for 50%

profile of v5, /device:TPU:0, one launch (start us, length us, event | category | flops | bytes accessed | tf_op | source)
XLA Modules:
  0.0 539.5 jit_solution(8191074054491915505)
XLA Ops:
  7.2 0.0 all-gather.2.cloned.1.call-start
  7.3 0.9 fusion.18
  8.1 0.7 constant_dynamic-slice_fusion.2
  8.8 1.0 copy.24.seg_col
  9.9 0.6 broadcast_in_dim.16.seg
  10.5 1.3 broadcast_in_dim.14.gain_a
  11.8 1.3 broadcast_in_dim.15.gain_b
  13.0 4.3 copy.23
  17.3 4.9 constant_dynamic-slice_fusion.1
  22.2 0.0 copy-done.4
  22.2 1.7 pad_maximum_fusion
  23.9 128.6 %front.1 = (bf16[4,4,4,48,1536]{4,3,2,1,0:T(8,128)(2,1)}, bf16[4,4,4,48,1536]{4,3,2,1,0:T(8,128)(2,1)}, bf16[4,4,4,48,1536]{4,3,2,1,0:T(8,128)(2,1)}, bf16[2304,...) custom-call(bf16[4,4,48,1536]{3,2,1,0:T(8,128)(2,1)} %bitcast.34, ...), custom_call_target="tpu_custom_call" | custom-call | tf_op jit(solution)/shard_map/front/pallas_call | solution.py:349
  152.5 19.1 %multiply_convert_fusion = (bf16[3072,1024]{1,0:T(8,128)(2,1)S(1)}, f32[3072,1024]{1,0:T(8,128)}) fusion(bf16[3072,1536]{1,0:T(8,128)(2,1)} %bitcast.46, bf16[1024,1536]{1,0:T(8,128)(2,1)} %get-tuple-element.25.normed_b_in), kind=kOutput, calls=%fused_computation.14 | convolution fusion | flops 9691987968 | bytes 31457280 | tf_op jit(solution)/shard_map/dot_general | solution.py:22
  171.6 14.6 %convolution_convert_fusion = bf16[1024,1536]{1,0:T(8,128)(2,1)S(1)} fusion(bf16[3072,1024]{1,0:T(8,128)(2,1)S(1)} %get-tuple-element.40.hidden_act, bf16[3072,1536]{1,0:T(8,128)(2,1)} %bitcast.48), kind=kOutput, calls=%fused_computation.17 | convolution fusion | flops 9665249280 | bytes 18874368 | tf_op jit(solution)/shard_map/dot_general | solution.py:26
  186.3 0.1 collective-permute-start
  186.4 0.0 copy-done
  186.4 23.2 %fusion.2.grad_pre = bf16[3072,1024]{1,0:T(8,128)(2,1)} fusion(f32[3072,1024]{1,0:T(8,128)} %get-tuple-element.41, bf16[3072,1536]{1,0:T(8,128)(2,1)} %bitcast.49, bf16[1024,1536]{1,0:T(8,128)(2,1)S(1)} %bitcast.31), kind=kOutput, calls=%fused_computation.6 | convolution fusion | flops 9732882432 | bytes 31457280 | tf_op jit(solution)/shard_map/dot_general | solution.py:22
  209.6 15.9 %convolution_convert_fusion.1.part_b = bf16[1024,1536]{1,0:T(8,128)(2,1)} fusion(bf16[3072,1024]{1,0:T(8,128)(2,1)} %fusion.2.grad_pre, bf16[3072,1536]{1,0:T(8,128)(2,1)} %bitcast.47), kind=kOutput, calls=%fused_computation.18 | convolution fusion | flops 9665249280 | bytes 18874368 | tf_op jit(solution)/shard_map/dot_general | solution.py:26
  225.4 0.0 collective-permute-done
  225.4 0.0 copy-done.1
  225.4 3.1 add_convert_fusion
  228.6 1.3 constant_dynamic-slice_fusion
  229.8 0.0 all-gather.2.cloned.1.call-update
  229.8 270.2 %backward.1 = (bf16[4,4,48,1536]{3,2,1,0:T(8,128)(2,1)}, bf16[4,4,48,1536]{3,2,1,0:T(8,128)(2,1)}, bf16[4,4,48,1536]{3,2,1,0:T(8,128)(2,1)}, bf16[4,4,4,48,1536]...) custom-call(bf16[3072,1024]{1,0:T(8,128)(2,1)} %copy-done.2, ...), custom_call_target="tpu_custom_call" | custom-call | tf_op jit(solution)/shard_map/backward/pallas_call | solution.py:722
  500.1 2.8 slice.20
  502.9 1.9 slice.22
  504.8 4.3 copy.26
  509.1 0.6 slice_reduce_fusion
  509.7 10.5 %copy.30 = bf16[8,512,1536]{2,1,0:T(8,128)(2,1)} copy(bf16[8,512,1536]{2,1,0:T(8,128)(2,1)} %all-gather.2.cloned.1.call-done) | data formatting | bytes 25165824
  520.2 10.7 %copy.31 = bf16[8,512,1536]{2,1,0:T(8,128)(2,1)} copy(bf16[8,512,1536]{2,1,0:T(8,128)(2,1)} %get-tuple-element.53) | data formatting | bytes 25165824
  530.8 0.0 copy-done.3
  530.8 1.4 copy.32
  (12 shorter events, 0.0 us)
Async XLA Ops:
  7.2 15.1 %copy-start.4 = (bf16[1536,576]{0,1:T(8,128)(2,1)S(1)}, bf16[1536,576]{0,1:T(8,128)(2,1)}, u32[]{:S(2)}) copy-start(bf16[1536,576]{0,1:T(8,128)(2,1)} %param.13) | copy-start | bytes 5308420
  7.2 15.1 %copy-start.5 = (bf16[2,96,1536]{2,1,0:T(8,128)(2,1)S(1)}, bf16[2,96,1536]{2,1,0:T(8,128)(2,1)}, u32[]{:S(2)}) copy-start(bf16[2,96,1536]{2,1,0:T(8,128)(2,1)} %param.14) | copy-start | bytes 1769476
  7.2 502.5 %all-gather.2.cloned.1.call-start = ((), (), s32[]{:S(2)}) async-start(), calls=%async_computation | async-start | bytes 14155776 | tf_op jit(solution)/shard_map/all_gather | solution.py:815
  22.2 164.1 %copy-start = (bf16[2,512,1536]{2,1,0:T(8,128)(2,1)}, bf16[2,512,1536]{2,1,0:T(8,128)(2,1)S(1)}, u32[]{:S(2)}) copy-start(bf16[2,512,1536]{2,1,0:T(8,128)(2,1)S(1)} %get-tuple-element.42) | copy-start | bytes 9437188
  171.6 14.6 %copy-start.2 = (bf16[3072,1024]{1,0:T(8,128)(2,1)}, bf16[3072,1024]{1,0:T(8,128)(2,1)S(1)}, u32[]{:S(2)}) copy-start(bf16[3072,1024]{1,0:T(8,128)(2,1)S(1)} %get-tuple-element.40.hidden_act) | copy-start | bytes 18874372
  186.3 39.2 %collective-permute-start = (bf16[1024,1536]{1,0:T(8,128)(2,1)S(1)}, bf16[1024,1536]{1,0:T(8,128)(2,1)}, u32[]{:S(2)}, u32[]{:S(2)}) collective-permute-start(bf16[1024,1536]{1,0:T(8,128)(2,1)S(1)} %convolution_convert_fusion), channel_id=1, source_target_pairs={{0,1},{1,0},{2,3},{3,2},{4,5},{5,4},{6,7},{7,6},{8,9},{9,8},{10,11... | collective-permute-start | bytes 9437192 | tf_op jit(solution)/shard_map/ppermute | solution.py:30
  209.5 15.9 %copy-start.1 = (bf16[1024,1536]{1,0:T(8,128)(2,1)S(1)}, bf16[1024,1536]{1,0:T(8,128)(2,1)}, u32[]{:S(2)}) copy-start(bf16[1024,1536]{1,0:T(8,128)(2,1)} %get-tuple-element.26.x_one_in) | copy-start | bytes 9437188
  500.0 9.0 %copy-start.6 = (f32[8,1536]{1,0:T(8,128)S(1)}, f32[8,1536]{1,0:T(8,128)}, u32[]{:S(2)}) copy-start(f32[8,1536]{1,0:T(8,128)} %get-tuple-element.34) | copy-start | bytes 147460
  520.2 10.7 %copy-start.3 = (bf16[4,4,48,1536]{3,2,1,0:T(8,128)(2,1)S(1)}, bf16[4,4,48,1536]{3,2,1,0:T(8,128)(2,1)}, u32[]{:S(2)}) copy-start(bf16[4,4,48,1536]{3,2,1,0:T(8,128)(2,1)} %get-tuple-element.37) | copy-start | bytes 7077892
Sparse Core Ops, SparseCore 0:
  230.0 107.1 all-gather.1

commit v6 on v5

--- a/solution.py
+++ b/solution.py
@@ -92,6 +92,17 @@
             started.append(copy)
         self.copies += started
         return started
+
+    def send(self, axis, step, source, target):
+        copy = pltpu.make_async_remote_copy(
+            src_ref=source, dst_ref=target,
+            send_sem=self.send_sems.at[self.used], recv_sem=self.recv_sems.at[self.used],
+            device_id=self.place.peer(axis, step), device_id_type=MESH_ID,
+        )
+        copy.start()
+        self.used += 1
+        self.copies.append(copy)
+        return copy
 
     def swap(self, source, target):
         copy = pltpu.make_async_remote_copy(
@@ -197,8 +208,34 @@
             head_slice(out, index, 1 + i, BLOCK, SEQ)[...] = whole[:, BLOCK:].astype(BF16)
 
 
+class Relay:
+    COPIES = 6
+
+    def __init__(self, sender, axis, own, up, down, on_up, on_down):
+        self.sender, self.axis = sender, axis
+        self.on_up, self.on_down = on_up, on_down
+        self.ups = [sender.send(axis, 1, own(half), up(half)) for half in range(2)]
+        self.downs = [sender.send(axis, 3, own(half), down(half)) for half in range(2)]
+
+    @classmethod
+    def at_place(cls, sender, axis, region, own=None):
+        place = sender.place
+        here = lambda half: region(place.pos[axis], half)
+        behind, ahead = region(place.ahead(axis, 3), 0), region(place.ahead(axis, 1), 1)
+        return cls(sender, axis, own or here, here, here, (behind, behind), (ahead, ahead))
+
+    def pass_on(self):
+        self.ups[0].wait_recv()
+        self.passed = [self.sender.send(self.axis, 1, *self.on_up)]
+        self.downs[1].wait_recv()
+        self.passed.append(self.sender.send(self.axis, 3, *self.on_down))
+
+    def finish(self):
+        wait_all([self.ups[1], self.downs[0]] + self.passed)
+
+
 class WeightGather:
-    COPIES = 21
+    COPIES = 12 + 3 * Relay.COPIES
 
     def __init__(self, place, sender, own, out):
         self.place, self.sender, self.own, self.out = place, sender, own, out
@@ -217,8 +254,10 @@
 
     def start_whole(self):
         cols = pl.ds(2 * THIRD, THIRD)
-        self.whole = self.sender.ring(
-            "x", lambda step: self.own.at[:, :, :, cols], lambda step: self.out.at[RING - step, :, :, :, cols])
+        spot = lambda shard, half: self.out.at[shard, pl.ds(2 * half, 2), :, :, cols]
+        self.whole = Relay(
+            self.sender, "x", lambda half: self.own.at[pl.ds(2 * half, 2), :, :, cols],
+            lambda half: spot(3, half), lambda half: spot(1, half), (spot(3, 0), spot(2, 0)), (spot(1, 1), spot(2, 1)))
 
     def second(self):
         self.mid = []
@@ -228,17 +267,22 @@
             self.mid.append(self.sender.ring(axis, spot, spot))
 
     def third(self):
-        z, y = self.place.pos["z"], self.place.pos["y"]
+        shards = pl.ds(1, 3)
         wait_all(self.mid[0])
-        line = lambda step: self.out.at[pl.ds(1, 3), z, :, :, pl.ds(0, THIRD)]
-        self.far = self.sender.ring("z", line, line)
+        line = lambda pos, half: self.out.at[shards, pos, pl.ds(2 * half, 2), :, pl.ds(0, THIRD)]
+        self.far = [Relay.at_place(self.sender, "z", line)]
         wait_all(self.mid[1])
-        row = lambda step: self.out.at[pl.ds(1, 3), :, y, :, pl.ds(THIRD, THIRD)]
-        self.far += self.sender.ring("y", row, row)
+        row = lambda pos, half: self.out.at[shards, pl.ds(2 * half, 2), pos, :, pl.ds(THIRD, THIRD)]
+        self.far.append(Relay.at_place(self.sender, "y", row))
+
+    def pass_on(self):
+        for far in self.far:
+            far.pass_on()
 
     def finish(self):
-        wait_all(self.far)
-        wait_all(self.whole)
+        for far in self.far:
+            far.finish()
+        self.whole.finish()
 
 
 def norm_stats(x_f32):
@@ -274,8 +318,6 @@
     att.start_whole()
     for gather in mlp:
         gather.start()
-    for gather in mlp:
-        gather.start_whole()
     loads[0].wait()
 
     def first_norm(rows):
@@ -299,16 +341,24 @@
     att.third()
     for gather in mlp:
         gather.second()
+    att.whole.pass_on()
+    for gather in mlp:
+        gather.start_whole()
+    att.pass_on()
     att.finish()
     others = [copy(w_att.at[shard], weights.at[shard], 7 + shard) for shard in range(1, RING)]
     for load in others:
         load.wait()
     project(3, 12)
     results.append(copy(qkv, qkv_out, 11))
-    attention_forward(qkv, seg, seg_col, attn, 0, 6)
     for gather in mlp:
         gather.third()
-    attention_forward(qkv, seg, seg_col, attn, 6, 16)
+    attention_forward(qkv, seg, seg_col, attn, 0, 10)
+    mlp[0].whole.pass_on()
+    mlp[0].pass_on()
+    attention_forward(qkv, seg, seg_col, attn, 10, 16)
+    mlp[1].whole.pass_on()
+    mlp[1].pass_on()
     results.append(copy(attn, attn_out, 12))
     swaps = []
     for index in range(TOKENS // STEP):
@@ -464,7 +514,7 @@
 
 
 class PlaneGather:
-    COPIES = 12
+    COPIES = 6 + 2 * Relay.COPIES
 
     def __init__(self, place, sender, final, out, local_sem):
         self.place, self.sender, self.final, self.out, self.local_sem = place, sender, final, out, local_sem
@@ -480,17 +530,21 @@
                 axis, lambda step: self.final.at[:, cols], lambda step: self.out.at[z, y, :, cols]))
 
     def second(self):
-        z, y = self.place.pos["z"], self.place.pos["y"]
         self.store.wait()
         wait_all(self.near[0])
-        line = lambda step: self.out.at[z, :, :, pl.ds(0, HALF)]
-        self.far = self.sender.ring("z", line, line)
+        line = lambda pos, half: self.out.at[pos, pl.ds(2 * half, 2), :, pl.ds(0, HALF)]
+        self.far = [Relay.at_place(self.sender, "z", line)]
         wait_all(self.near[1])
-        row = lambda step: self.out.at[:, y, :, pl.ds(HALF, HALF)]
-        self.far += self.sender.ring("y", row, row)
+        row = lambda pos, half: self.out.at[pl.ds(2 * half, 2), pos, :, pl.ds(HALF, HALF)]
+        self.far.append(Relay.at_place(self.sender, "y", row))
+
+    def pass_on(self):
+        for far in self.far:
+            far.pass_on()
 
     def finish(self):
-        wait_all(self.far)
+        for far in self.far:
+            far.finish()
 
 
 def gain_step(place, sender, gains, bufs, index, axis):
@@ -669,9 +723,10 @@
         part[rows] = norm_back(rows, gain_a, gain_grad_a)
 
     token_blocks(first_norm)
-    row_of = lambda step: 2 * place.ahead("x", RING - step) + place.core
-    mine = part.at[pl.ds(pl.multiple_of(place.core * SEQ, SEQ), SEQ)]
-    rows_sent = sender.ring("x", lambda step: mine, lambda step: grad_x.at[row_of(0)])
+    row_of = lambda pos: 2 * pos + place.core
+    part_rows = SEQ // 2
+    mine = lambda half: part.at[pl.ds(pl.multiple_of(place.core * SEQ + half * part_rows, part_rows), part_rows)]
+    rows_sent = Relay.at_place(sender, "x", lambda pos, half: grad_x.at[row_of(pos), pl.ds(half * part_rows, part_rows)], mine)
     results = []
     for i in range(2):
         result = pltpu.make_async_copy(part.at[pl.ds(i * SEQ, SEQ)], grad_x.at[2 * place.pos["x"] + i], load_sems.at[12 + 4 * i])
@@ -691,19 +746,23 @@
         plane.second()
     gain_finish()
     gain_finish = gain_step(place, sender, gains, gain_bufs, 2, "x")
+    rows_sent.pass_on()
     att_work.third()
-    passed = []
-    for step, copy in zip(range(1, RING), rows_sent):
-        copy.wait_recv()
-        row = grad_x.at[row_of(step)]
-        passed.append(sender.swap(row, row))
+    for plane in planes:
+        plane.pass_on()
     att_work.finish()
     att_plane.start()
+    rows_sent.finish()
+    passed = []
+    for step in range(1, RING):
+        row = grad_x.at[row_of(place.ahead("x", step))]
+        passed.append(sender.swap(row, row))
     gain_finish()
     gain_out[...] = gains[3]
     for plane in planes:
         plane.finish()
     att_plane.second()
+    att_plane.pass_on()
     att_plane.finish()
     wait_all(passed)
     for copy in passed:
@@ -717,7 +776,7 @@
     tokens = (TOKENS, WIDTH)
     piece = jax.ShapeDtypeStruct((RING, RING, PIECE, WIDTH), BF16)
     grid = jax.ShapeDtypeStruct((RING, RING, RING, PIECE, WIDTH), BF16)
-    copies = 3 * (9 * len(WIDTHS) + PlaneGather.COPIES) + TOKENS // STEP + 1 + 9 + 6
+    copies = 3 * (9 * len(WIDTHS) + PlaneGather.COPIES) + TOKENS // STEP + 1 + 9 + Relay.COPIES + 3
     tail = [shape for part in range(len(WIDTHS)) for shape in GradScatter.scratch(WIDTHS)[4 * part + 2 : 4 * part + 4]]
     return pl.pallas_call(
         back_kernel,

time: 546 us -> 506 us (0.927)
  Pallas kernels: 399 us -> 357 us
    pallas_call x1, Pallas kernels: 270 us -> 245 us  [backward(): pl.pallas_call(back_kernel, out_shape=[piece, piece, piece, grid, grid, g...]
    pallas_call x1, Pallas kernels: 129 us -> 111 us  [front(): pl.pallas_call(front_kernel, out_shape=[gathered, gathered, gathered, jax...]
  transfers between devices with their start and end apart: 2 -> 2, of which waited for: 0 -> 0; matrix products, arithmetic and copies ran while one was open for 9% -> 10% of each run, Pallas kernels for 50% -> 49%
where the time goes in v6:
time: 506 us; the launch traced here: 498 us
  Pallas kernels  357 us (71%)
  matrix products  72.8 us (14%)
  local copies, waits for them, and re-layouts  48.4 us (10%)
  between operations  14.6 us (3%)
    pallas_call x1, Pallas kernels, backward(): pl.pallas_call(back_kernel, out_shape=[piece, piece, piece, grid, grid, g...  245 us
    pallas_call x1, Pallas kernels, front(): pl.pallas_call(front_kernel, out_shape=[gathered, gathered, gathered, jax...  111 us
    dot_general x2, matrix products, dot_nt(): lax.dot_general(lhs, rhs, (((lhs.ndim - 1,), (rhs.ndim - 1,)), ((), ())),...  42.3 us
    dot_general x2, matrix products, dot_tn(): lax.dot_general(lhs, rhs, (((0,), (0,)), ((), ())), preferred_element_typ...  30.5 us
    unnamed x17, local copies, waits for them, and re-layouts  22.6 us
  transfers between devices with their start and end apart: 2, of which 0 were waited for; matrix products, arithmetic and copies ran while one was open for 10% of the time, Pallas kernels for 49%

profile of v6, /device:TPU:0, one launch (start us, length us, event | category | flops | bytes accessed | tf_op | source)
XLA Modules:
  0.0 498.5 jit_solution(17314676636992682147)
XLA Ops:
  7.2 0.0 copy-start.4
  7.2 0.0 copy-start.5
  7.2 0.0 all-gather.2.cloned.1.call-start
  7.3 0.9 fusion.18
  8.1 0.7 constant_dynamic-slice_fusion.2
  8.8 1.0 copy.24.seg_col
  9.9 0.6 broadcast_in_dim.16.seg
  10.5 1.3 broadcast_in_dim.14.gain_a
  11.8 1.3 broadcast_in_dim.15.gain_b
  13.0 4.3 copy.23
  17.3 4.9 constant_dynamic-slice_fusion.1
  22.2 1.7 pad_maximum_fusion
  23.9 111.4 %front.1 = (bf16[4,4,4,48,1536]{4,3,2,1,0:T(8,128)(2,1)}, bf16[4,4,4,48,1536]{4,3,2,1,0:T(8,128)(2,1)}, bf16[4,4,4,48,1536]{4,3,2,1,0:T(8,128)(2,1)}, bf16[2304,...) custom-call(bf16[4,4,48,1536]{3,2,1,0:T(8,128)(2,1)} %bitcast.34, ...), custom_call_target="tpu_custom_call" | custom-call | tf_op jit(solution)/shard_map/front/pallas_call | solution.py:399
  135.3 19.1 %multiply_convert_fusion = (bf16[3072,1024]{1,0:T(8,128)(2,1)S(1)}, f32[3072,1024]{1,0:T(8,128)}) fusion(bf16[3072,1536]{1,0:T(8,128)(2,1)} %bitcast.46, bf16[1024,1536]{1,0:T(8,128)(2,1)} %get-tuple-element.25.normed_b_in), kind=kOutput, calls=%fused_computation.14 | convolution fusion | flops 9691987968 | bytes 31457280 | tf_op jit(solution)/shard_map/dot_general | solution.py:22
  154.5 14.6 %convolution_convert_fusion = bf16[1024,1536]{1,0:T(8,128)(2,1)S(1)} fusion(bf16[3072,1024]{1,0:T(8,128)(2,1)S(1)} %get-tuple-element.40.hidden_act, bf16[3072,1536]{1,0:T(8,128)(2,1)} %bitcast.48), kind=kOutput, calls=%fused_computation.17 | convolution fusion | flops 9665249280 | bytes 18874368 | tf_op jit(solution)/shard_map/dot_general | solution.py:26
  169.1 0.0 copy-done.2
  169.1 0.9 collective-permute-start
  170.0 23.2 %fusion.2.grad_pre = bf16[3072,1024]{1,0:T(8,128)(2,1)} fusion(f32[3072,1024]{1,0:T(8,128)} %get-tuple-element.41, bf16[3072,1536]{1,0:T(8,128)(2,1)} %bitcast.49, bf16[1024,1536]{1,0:T(8,128)(2,1)S(1)} %bitcast.31), kind=kOutput, calls=%fused_computation.6 | convolution fusion | flops 9732882432 | bytes 31457280 | tf_op jit(solution)/shard_map/dot_general | solution.py:22
  193.2 15.9 %convolution_convert_fusion.1.part_b = bf16[1024,1536]{1,0:T(8,128)(2,1)} fusion(bf16[3072,1024]{1,0:T(8,128)(2,1)} %fusion.2.grad_pre, bf16[3072,1536]{1,0:T(8,128)(2,1)} %bitcast.47), kind=kOutput, calls=%fused_computation.18 | convolution fusion | flops 9665249280 | bytes 18874368 | tf_op jit(solution)/shard_map/dot_general | solution.py:26
  209.0 0.0 collective-permute-done
  209.0 3.1 add_convert_fusion
  212.2 1.3 constant_dynamic-slice_fusion
  213.4 0.0 all-gather.2.cloned.1.call-update
  213.5 245.5 %backward.1 = (bf16[4,4,48,1536]{3,2,1,0:T(8,128)(2,1)}, bf16[4,4,48,1536]{3,2,1,0:T(8,128)(2,1)}, bf16[4,4,48,1536]{3,2,1,0:T(8,128)(2,1)}, bf16[4,4,4,48,1536]...) custom-call(bf16[3072,1024]{1,0:T(8,128)(2,1)} %copy-done.2, ...), custom_call_target="tpu_custom_call" | custom-call | tf_op jit(solution)/shard_map/backward/pallas_call | solution.py:781
  458.9 2.8 slice.20
  461.7 1.9 slice.22
  463.7 4.3 copy.26
  467.9 0.6 slice_reduce_fusion
  468.6 10.5 %copy.30 = bf16[8,512,1536]{2,1,0:T(8,128)(2,1)} copy(bf16[8,512,1536]{2,1,0:T(8,128)(2,1)} %all-gather.2.cloned.1.call-done) | data formatting | bytes 25165824
  479.0 10.7 %copy.31 = bf16[8,512,1536]{2,1,0:T(8,128)(2,1)} copy(bf16[8,512,1536]{2,1,0:T(8,128)(2,1)} %get-tuple-element.53) | data formatting | bytes 25165824
  489.7 0.0 copy-done.3
  489.7 1.4 copy.32
  (12 shorter events, 0.0 us)
Async XLA Ops:
  7.2 15.1 %copy-start.4 = (bf16[1536,576]{0,1:T(8,128)(2,1)S(1)}, bf16[1536,576]{0,1:T(8,128)(2,1)}, u32[]{:S(2)}) copy-start(bf16[1536,576]{0,1:T(8,128)(2,1)} %param.13) | copy-start | bytes 5308420
  7.2 15.1 %copy-start.5 = (bf16[2,96,1536]{2,1,0:T(8,128)(2,1)S(1)}, bf16[2,96,1536]{2,1,0:T(8,128)(2,1)}, u32[]{:S(2)}) copy-start(bf16[2,96,1536]{2,1,0:T(8,128)(2,1)} %param.14) | copy-start | bytes 1769476
  7.2 461.4 %all-gather.2.cloned.1.call-start = ((), (), s32[]{:S(2)}) async-start(), calls=%async_computation | async-start | bytes 14155776 | tf_op jit(solution)/shard_map/all_gather | solution.py:874
  22.2 147.8 %copy-start = (bf16[2,512,1536]{2,1,0:T(8,128)(2,1)}, bf16[2,512,1536]{2,1,0:T(8,128)(2,1)S(1)}, u32[]{:S(2)}) copy-start(bf16[2,512,1536]{2,1,0:T(8,128)(2,1)S(1)} %get-tuple-element.42) | copy-start | bytes 9437188
  154.5 14.6 %copy-start.2 = (bf16[3072,1024]{1,0:T(8,128)(2,1)}, bf16[3072,1024]{1,0:T(8,128)(2,1)S(1)}, u32[]{:S(2)}) copy-start(bf16[3072,1024]{1,0:T(8,128)(2,1)S(1)} %get-tuple-element.40.hidden_act) | copy-start | bytes 18874372
  169.1 39.9 %collective-permute-start = (bf16[1024,1536]{1,0:T(8,128)(2,1)S(1)}, bf16[1024,1536]{1,0:T(8,128)(2,1)}, u32[]{:S(2)}, u32[]{:S(2)}) collective-permute-start(bf16[1024,1536]{1,0:T(8,128)(2,1)S(1)} %convolution_convert_fusion), channel_id=1, source_target_pairs={{0,1},{1,0},{2,3},{3,2},{4,5},{5,4},{6,7},{7,6},{8,9},{9,8},{10,11... | collective-permute-start | bytes 9437192 | tf_op jit(solution)/shard_map/ppermute | solution.py:30
  193.2 15.9 %copy-start.1 = (bf16[1024,1536]{1,0:T(8,128)(2,1)S(1)}, bf16[1024,1536]{1,0:T(8,128)(2,1)}, u32[]{:S(2)}) copy-start(bf16[1024,1536]{1,0:T(8,128)(2,1)} %get-tuple-element.26.x_one_in) | copy-start | bytes 9437188
  458.9 9.0 %copy-start.6 = (f32[8,1536]{1,0:T(8,128)S(1)}, f32[8,1536]{1,0:T(8,128)}, u32[]{:S(2)}) copy-start(f32[8,1536]{1,0:T(8,128)} %get-tuple-element.34) | copy-start | bytes 147460
  479.0 10.7 %copy-start.3 = (bf16[4,4,48,1536]{3,2,1,0:T(8,128)(2,1)S(1)}, bf16[4,4,48,1536]{3,2,1,0:T(8,128)(2,1)}, u32[]{:S(2)}) copy-start(bf16[4,4,48,1536]{3,2,1,0:T(8,128)(2,1)} %get-tuple-element.37) | copy-start | bytes 7077892
Sparse Core Ops, SparseCore 0:
  213.6 105.4 all-gather.1

commit v7 on v6

--- a/solution.py
+++ b/solution.py
@@ -445,37 +445,72 @@
             ]
         return shapes
 
-    def cut(self, part, step):
+    def cut(self, part, step, half=None):
         axis = ORDERS[part][0]
         index = self.place.block(axis, step)
         cols = pl.ds(*self.cols[part])
+        lead = pl.ds(0, RING) if half is None else pl.ds(2 * half, 2)
         if axis == "x":
-            return self.grads.at[index, :, :, :, cols]
+            return self.grads.at[index, lead, :, :, cols]
         if axis == "z":
-            return self.grads.at[:, index, :, :, cols]
-        return self.grads.at[:, :, index, :, cols]
+            return self.grads.at[lead, index, :, :, cols]
+        return self.grads.at[lead, :, index, :, cols]
+
+    def load(self, source, target, index):
+        copy = pltpu.make_async_copy(source, target, self.local_sems.at[index])
+        copy.start()
+        return copy
 
     def start(self):
-        self.loads, self.one, self.two, self.three = [], [], {}, {}
+        self.loads, self.far, self.raw, self.sums, self.two, self.three = [], [], [], [], {}, {}
+        low, high = pl.ds(0, 2), pl.ds(2, 2)
         for part in self.parts:
-            self.one.append(self.sender.ring(
-                ORDERS[part][0], lambda step: self.cut(part, step), lambda step: self.bufs[part][1].at[step - 1]))
+            axis, first = ORDERS[part][0], self.bufs[part][1]
+            self.far.append([
+                self.sender.send(axis, 1, self.cut(part, 2, 0), first.at[1, low]),
+                self.sender.send(axis, 3, self.cut(part, 2, 1), first.at[1, high])])
         for part in self.parts:
-            load = pltpu.make_async_copy(self.cut(part, 0), self.bufs[part][0], self.local_sems.at[part])
-            load.start()
-            self.loads.append(load)
+            axis, first = ORDERS[part][0], self.bufs[part][1]
+            self.raw.append([
+                self.sender.send(axis, 1, self.cut(part, 1, 1), first.at[0, high]),
+                self.sender.send(axis, 3, self.cut(part, 3, 0), first.at[2, low])])
+        for part in self.parts:
+            mine = self.bufs[part][0]
+            self.loads.append([
+                self.load(self.cut(part, 1, 0), mine.at[low], part), self.load(self.cut(part, 3, 1), mine.at[high], 4 + part)])
+
+    def relay(self):
+        low, high = pl.ds(0, 2), pl.ds(2, 2)
+        for part in self.parts:
+            for load in self.loads[part]:
+                load.wait()
+            wait_all(self.far[part])
+            axis, mine, first = ORDERS[part][0], self.bufs[part][0], self.bufs[part][1]
+
+            @pl.loop(0, RING)
+            def _(a):
+                for b in range(RING):
+                    mine[a, b] = (mine[a, b].astype(F32) + first[1, a, b].astype(F32)).astype(BF16)
+
+            self.sums.append([
+                self.sender.send(axis, 1, mine.at[low], first.at[0, low]),
+                self.sender.send(axis, 3, mine.at[high], first.at[2, high])])
 
     def second(self):
+        own = []
         for part in self.parts:
-            self.loads[part].wait()
-            wait_all(self.one[part])
+            self.sender.settle(self.sums[part])
+            own.append(self.load(self.cut(part, 0), self.bufs[part][0], part))
+        for part in self.parts:
+            own[part].wait()
+            wait_all(self.raw[part] + self.sums[part])
             mine, first, second, _ = self.bufs[part]
 
             @pl.loop(0, RING)
             def _(a):
                 for b in range(RING):
                     total = mine[a, b].astype(F32)
-                    for k in range(3):
+                    for k in (0, 2):
                         total = total + first[k, a, b].astype(F32)
                     mine[a, b] = total.astype(BF16)
 
@@ -643,6 +678,7 @@
     works[0].start()
     ready("normed_b")
     weight_grad(grad_pre, normed, grad_up)
+    works[0].relay()
     works[1].start()
 
     load("x_one", x_one_in, normed, 14)
@@ -674,7 +710,9 @@
         rows = pl.ds(shard * OUT_ROWS, OUT_ROWS)
         grad_attn[rows] = dot_rows(w_out[rows], grad_one[...]).astype(BF16)
     ready("qkv")
-    attention_backward(qkv, seg, seg_col, grad_attn, qkv, 0, 10)
+    attention_backward(qkv, seg, seg_col, grad_attn, qkv, 0, 6)
+    works[1].relay()
+    attention_backward(qkv, seg, seg_col, grad_attn, qkv, 6, 10)
     works[0].second()
     place.signal_rings(ring_sem)
     attention_backward(qkv, seg, seg_col, grad_attn, qkv, 10, 16)
@@ -736,6 +774,7 @@
     gains[0, 0:1] = gain_grad_a[...]
     gains[0, 1:2] = gain_grad_b[...]
     gain_finish = gain_step(place, sender, gains, gain_bufs, 0, "z")
+    att_work.relay()
     for work, plane in zip(works, planes):
         work.finish()
         plane.start()
@@ -776,7 +815,7 @@
     tokens = (TOKENS, WIDTH)
     piece = jax.ShapeDtypeStruct((RING, RING, PIECE, WIDTH), BF16)
     grid = jax.ShapeDtypeStruct((RING, RING, RING, PIECE, WIDTH), BF16)
-    copies = 3 * (9 * len(WIDTHS) + PlaneGather.COPIES) + TOKENS // STEP + 1 + 9 + Relay.COPIES + 3
+    copies = 3 * (12 * len(WIDTHS) + PlaneGather.COPIES) + TOKENS // STEP + 1 + 9 + Relay.COPIES + 3
     tail = [shape for part in range(len(WIDTHS)) for shape in GradScatter.scratch(WIDTHS)[4 * part + 2 : 4 * part + 4]]
     return pl.pallas_call(
         back_kernel,
@@ -810,7 +849,7 @@
             pltpu.VMEM((3, PIECE, WIDTH), BF16),
             pltpu.SemaphoreType.DMA((copies,)),
             pltpu.SemaphoreType.DMA((copies,)),
-            pltpu.SemaphoreType.DMA((3, 4)),
+            pltpu.SemaphoreType.DMA((3, 8)),
         ] + GradScatter.scratch(WIDTHS) + GradScatter.scratch(WIDTHS) + tail,
         compiler_params=pltpu.CompilerParams(collective_id=3, has_side_effects=True, vmem_limit_bytes=67043328),
         name="backward",

time: 506 us -> 482 us (0.953)
  Pallas kernels: 357 us -> 333 us
    pallas_call x1, Pallas kernels: 245 us -> 222 us  [backward(): pl.pallas_call(back_kernel, out_shape=[piece, piece, piece, grid, grid, g...]
  transfers between devices with their start and end apart: 2 -> 2, of which waited for: 0 -> 0; matrix products, arithmetic and copies ran while one was open for 10% -> 10% of each run, Pallas kernels for 49% -> 47%
where the time goes in v7:
time: 482 us; the launch traced here: 475 us
  Pallas kernels  333 us (69%)
  matrix products  72.8 us (15%)
  local copies, waits for them, and re-layouts  48.4 us (10%)
  between operations  14.3 us (3%)
    pallas_call x1, Pallas kernels, backward(): pl.pallas_call(back_kernel, out_shape=[piece, piece, piece, grid, grid, g...  222 us
    pallas_call x1, Pallas kernels, front(): pl.pallas_call(front_kernel, out_shape=[gathered, gathered, gathered, jax...  111 us
    dot_general x2, matrix products, dot_nt(): lax.dot_general(lhs, rhs, (((lhs.ndim - 1,), (rhs.ndim - 1,)), ((), ())),...  42.3 us
    dot_general x2, matrix products, dot_tn(): lax.dot_general(lhs, rhs, (((0,), (0,)), ((), ())), preferred_element_typ...  30.5 us
    unnamed x17, local copies, waits for them, and re-layouts  22.6 us
  transfers between devices with their start and end apart: 2, of which 0 were waited for; matrix products, arithmetic and copies ran while one was open for 10% of the time, Pallas kernels for 47%

profile of v7, /device:TPU:0, one launch (start us, length us, event | category | flops | bytes accessed | tf_op | source)
XLA Modules:
  0.0 474.6 jit_solution(5567706142690666438)
XLA Ops:
  7.2 0.0 copy-start.4
  7.2 0.0 copy-start.5
  7.2 0.0 all-gather.2.cloned.1.call-start
  7.3 0.9 fusion.18
  8.1 0.7 constant_dynamic-slice_fusion.2
  8.8 1.0 copy.24.seg_col
  9.9 0.6 broadcast_in_dim.16.seg
  10.5 1.3 broadcast_in_dim.14.gain_a
  11.8 1.3 broadcast_in_dim.15.gain_b
  13.0 4.3 copy.23
  17.3 4.9 %constant_dynamic-slice_fusion.1 = (bf16[2,512,1536]{2,1,0:T(8,128)(2,1)S(1)}, bf16[2,512,1536]{2,1,0:T(8,128)(2,1)}) fusion(bf16[8,512,1536]{2,1,0:T(8,128)(2,1)} %param.17, s32[]{:T(128)S(6)} %select_n.20, bf16[8,512,1536]{2,1,0:T(8,128)(2,1)} %param.9), kind=kLoop, calls=%fused_computation.23 | loop fusion | bytes 12582916 | tf_op jit(solution)/shard_map/dynamic_slice | solution.py:873
  22.2 1.7 pad_maximum_fusion
  23.9 111.4 %front.1 = (bf16[4,4,4,48,1536]{4,3,2,1,0:T(8,128)(2,1)}, bf16[4,4,4,48,1536]{4,3,2,1,0:T(8,128)(2,1)}, bf16[4,4,4,48,1536]{4,3,2,1,0:T(8,128)(2,1)}, bf16[2304,...) custom-call(bf16[4,4,48,1536]{3,2,1,0:T(8,128)(2,1)} %bitcast.34, ...), custom_call_target="tpu_custom_call" | custom-call | tf_op jit(solution)/shard_map/front/pallas_call | solution.py:399
  135.3 19.1 %multiply_convert_fusion = (bf16[3072,1024]{1,0:T(8,128)(2,1)S(1)}, f32[3072,1024]{1,0:T(8,128)}) fusion(bf16[3072,1536]{1,0:T(8,128)(2,1)} %bitcast.46, bf16[1024,1536]{1,0:T(8,128)(2,1)} %get-tuple-element.25.normed_b_in), kind=kOutput, calls=%fused_computation.14 | convolution fusion | flops 9691987968 | bytes 31457280 | tf_op jit(solution)/shard_map/dot_general | solution.py:22
  154.5 14.6 %convolution_convert_fusion = bf16[1024,1536]{1,0:T(8,128)(2,1)S(1)} fusion(bf16[3072,1024]{1,0:T(8,128)(2,1)S(1)} %get-tuple-element.40.hidden_act, bf16[3072,1536]{1,0:T(8,128)(2,1)} %bitcast.48), kind=kOutput, calls=%fused_computation.17 | convolution fusion | flops 9665249280 | bytes 18874368 | tf_op jit(solution)/shard_map/dot_general | solution.py:26
  169.1 0.0 copy-done.2
  169.1 0.9 collective-permute-start
  170.0 23.2 %fusion.2.grad_pre = bf16[3072,1024]{1,0:T(8,128)(2,1)} fusion(f32[3072,1024]{1,0:T(8,128)} %get-tuple-element.41, bf16[3072,1536]{1,0:T(8,128)(2,1)} %bitcast.49, bf16[1024,1536]{1,0:T(8,128)(2,1)S(1)} %bitcast.31), kind=kOutput, calls=%fused_computation.6 | convolution fusion | flops 9732882432 | bytes 31457280 | tf_op jit(solution)/shard_map/dot_general | solution.py:22
  193.2 15.9 %convolution_convert_fusion.1.part_b = bf16[1024,1536]{1,0:T(8,128)(2,1)} fusion(bf16[3072,1024]{1,0:T(8,128)(2,1)} %fusion.2.grad_pre, bf16[3072,1536]{1,0:T(8,128)(2,1)} %bitcast.47), kind=kOutput, calls=%fused_computation.18 | convolution fusion | flops 9665249280 | bytes 18874368 | tf_op jit(solution)/shard_map/dot_general | solution.py:26
  209.0 0.0 collective-permute-done
  209.0 3.1 add_convert_fusion
  212.2 1.3 constant_dynamic-slice_fusion
  213.4 0.0 all-gather.2.cloned.1.call-update
  213.5 221.9 %backward.1 = (bf16[4,4,48,1536]{3,2,1,0:T(8,128)(2,1)}, bf16[4,4,48,1536]{3,2,1,0:T(8,128)(2,1)}, bf16[4,4,48,1536]{3,2,1,0:T(8,128)(2,1)}, bf16[4,4,4,48,1536]...) custom-call(bf16[3072,1024]{1,0:T(8,128)(2,1)} %copy-done.2, ...), custom_call_target="tpu_custom_call" | custom-call | tf_op jit(solution)/shard_map/backward/pallas_call | solution.py:820
  435.4 2.8 slice.20
  438.2 1.9 slice.22
  440.1 4.3 copy.26
  444.4 0.0 copy-done.6
  444.4 0.6 slice_reduce_fusion
  445.0 10.5 %copy.30 = bf16[8,512,1536]{2,1,0:T(8,128)(2,1)} copy(bf16[8,512,1536]{2,1,0:T(8,128)(2,1)} %all-gather.2.cloned.1.call-done) | data formatting | bytes 25165824
  455.5 10.7 %copy.31 = bf16[8,512,1536]{2,1,0:T(8,128)(2,1)} copy(bf16[8,512,1536]{2,1,0:T(8,128)(2,1)} %get-tuple-element.53) | data formatting | bytes 25165824
  466.2 1.4 copy.32
  (12 shorter events, 0.0 us)
Async XLA Ops:
  7.2 15.1 %copy-start.4 = (bf16[1536,576]{0,1:T(8,128)(2,1)S(1)}, bf16[1536,576]{0,1:T(8,128)(2,1)}, u32[]{:S(2)}) copy-start(bf16[1536,576]{0,1:T(8,128)(2,1)} %param.13) | copy-start | bytes 5308420
  7.2 15.1 %copy-start.5 = (bf16[2,96,1536]{2,1,0:T(8,128)(2,1)S(1)}, bf16[2,96,1536]{2,1,0:T(8,128)(2,1)}, u32[]{:S(2)}) copy-start(bf16[2,96,1536]{2,1,0:T(8,128)(2,1)} %param.14) | copy-start | bytes 1769476
  7.2 437.8 %all-gather.2.cloned.1.call-start = ((), (), s32[]{:S(2)}) async-start(), calls=%async_computation | async-start | bytes 14155776 | tf_op jit(solution)/shard_map/all_gather | solution.py:913
  22.2 147.8 %copy-start = (bf16[2,512,1536]{2,1,0:T(8,128)(2,1)}, bf16[2,512,1536]{2,1,0:T(8,128)(2,1)S(1)}, u32[]{:S(2)}) copy-start(bf16[2,512,1536]{2,1,0:T(8,128)(2,1)S(1)} %get-tuple-element.42) | copy-start | bytes 9437188
  154.5 14.6 %copy-start.2 = (bf16[3072,1024]{1,0:T(8,128)(2,1)}, bf16[3072,1024]{1,0:T(8,128)(2,1)S(1)}, u32[]{:S(2)}) copy-start(bf16[3072,1024]{1,0:T(8,128)(2,1)S(1)} %get-tuple-element.40.hidden_act) | copy-start | bytes 18874372
  169.1 39.9 %collective-permute-start = (bf16[1024,1536]{1,0:T(8,128)(2,1)S(1)}, bf16[1024,1536]{1,0:T(8,128)(2,1)}, u32[]{:S(2)}, u32[]{:S(2)}) collective-permute-start(bf16[1024,1536]{1,0:T(8,128)(2,1)S(1)} %convolution_convert_fusion), channel_id=1, source_target_pairs={{0,1},{1,0},{2,3},{3,2},{4,5},{5,4},{6,7},{7,6},{8,9},{9,8},{10,11... | collective-permute-start | bytes 9437192 | tf_op jit(solution)/shard_map/ppermute | solution.py:30
  193.2 15.9 %copy-start.1 = (bf16[1024,1536]{1,0:T(8,128)(2,1)S(1)}, bf16[1024,1536]{1,0:T(8,128)(2,1)}, u32[]{:S(2)}) copy-start(bf16[1024,1536]{1,0:T(8,128)(2,1)} %get-tuple-element.26.x_one_in) | copy-start | bytes 9437188
  435.4 9.0 %copy-start.6 = (f32[8,1536]{1,0:T(8,128)S(1)}, f32[8,1536]{1,0:T(8,128)}, u32[]{:S(2)}) copy-start(f32[8,1536]{1,0:T(8,128)} %get-tuple-element.34) | copy-start | bytes 147460
  455.5 10.7 %copy-start.3 = (bf16[4,4,48,1536]{3,2,1,0:T(8,128)(2,1)S(1)}, bf16[4,4,48,1536]{3,2,1,0:T(8,128)(2,1)}, u32[]{:S(2)}) copy-start(bf16[4,4,48,1536]{3,2,1,0:T(8,128)(2,1)} %get-tuple-element.37) | copy-start | bytes 7077892
Sparse Core Ops, SparseCore 0:
  213.6 97.6 all-gather.1
